TPU v7x, 32 devices: a whole 2x2x4 slice. The times are simulated.
32 devices in a mesh: groups: 2 (over x), seq: 8 (over z, y), head: 2 (over core).
Axes of the slice: x: 2, y: 2, z: 4, core: 2. Of those that a mesh axis runs over, the one named last changes fastest.
Arguments:
- queries: bfloat16 [2048, 6144], P(('groups', 'seq', 'head')), parts along dimension 0, may hold values from -600 to 600
- latents: bfloat16 [2048, 576], P(('groups', 'seq')), parts along dimension 0, may hold values from -600 to 600
- latent_gain: float32 [512], replicated, may hold values from 0.1 to 1.9
- key_up: bfloat16 [32, 128, 512], P('head'), may hold values from -0.5 to 0.5
- value_up: bfloat16 [32, 512, 128], P('head'), may hold values from -1 to 1
- out_weight: bfloat16 [4096, 7168], P('head', 'seq'), may hold values from -0.09375 to 0.09375
Outputs:
- mixed: bfloat16 [16, 2, 64, 7168], P('groups', 'head', None, 'seq'), parts along dimension 0
There are 2 independent parts, one for each index of `groups`. A program takes and returns all parts, laid end to end along the dimension named above; an argument that names none is the same for every part. Nothing has to cross between parts.
All inputs are finite; a program needn't handle non-finite values.
Results may differ from a plain program's by a relative error of at most 0.013.
Values may be sent and summed in bfloat16 or wider, within the bound.
No kernel may reach another device: no remote copies, remote signals or barrier semaphores. Data moves between devices by JAX's collectives and lax.ppermute only.
A program may use at most 128 MiB of HBM per device.

v0:
```python
import functools

import jax
import jax.numpy as jnp
import numpy as np
from jax import lax
from jax.experimental import pallas as pl
from jax.experimental.pallas import tpu as pltpu
from jax.sharding import PartitionSpec as P


KV = 512
ROPE = 64
NOPE = 128
VD = 128
QK = NOPE + ROPE
WIDE = KV + 2 * ROPE
EPS = 1e-06
HIDDEN = -1e30


def rope_table(total):
    middle = ROPE // 2
    frequency = (10000.0 ** (-np.arange(middle, dtype=np.float32) / middle)).astype(np.float32)
    angles = (np.arange(total, dtype=np.float32)[:, None] * frequency).astype(np.float64)
    cosine, sine = np.cos(angles), np.sin(angles)
    return np.concatenate([cosine, cosine, -sine, sine], -1).astype(np.float32)


def rotate(values, table):
    middle = ROPE // 2
    swapped = jnp.concatenate([values[:, middle:], values[:, :middle]], -1)
    return values * table[:, :ROPE] + swapped * table[:, ROPE:]


def tag_lanes(rows, value):
    lane = lax.broadcasted_iota(jnp.int32, (rows, ROPE), 1)
    return value(lane).astype(jnp.bfloat16)


def prepare_kernel(half, latents, gain, table, full_out, half_out):
    block = lax.axis_index("seq")
    latent_f = latents[...].astype(jnp.float32)
    tokens = latent_f.shape[1]
    compressed = latent_f[:KV]
    spread = jnp.mean(compressed * compressed, axis=0, keepdims=True)
    normed = (compressed * lax.rsqrt(spread + EPS)).T * gain[...]
    full_out[:, :KV] = normed.astype(jnp.bfloat16)
    here = table[pl.ds(pl.multiple_of(block * tokens, tokens), tokens), :]
    rope = rotate(latent_f[KV:].T, here).astype(jnp.bfloat16)
    tags = tag_lanes(tokens, lambda lane: jnp.where(lane == block, 1.0, 0.0))
    full_out[:, KV:] = jnp.concatenate([rope, tags], -1)
    start = lax.axis_index("head") * half
    half_out[...] = full_out[pl.ds(pl.multiple_of(start, half), half), :]


def prepare(latents, gain, table):
    rows = latents.shape[1]
    half = rows // 2
    return pl.pallas_call(
        functools.partial(prepare_kernel, half),
        out_shape=[
            jax.ShapeDtypeStruct((rows, WIDE), jnp.bfloat16),
            jax.ShapeDtypeStruct((half, WIDE), jnp.bfloat16),
        ],
        cost_estimate=pl.CostEstimate(
            flops=10**8, bytes_accessed=4 * rows * WIDE, transcendentals=rows
        ),
        compiler_params=pltpu.CompilerParams(vmem_limit_bytes=12 << 20),
        name="prepare",
    )(latents, gain, table)


def lift_kernel(queries, key_up, table, out):
    rows = queries.shape[0]
    heads = key_up.shape[0]
    block = lax.axis_index("seq")
    first = pl.multiple_of((2 * block + lax.axis_index("head")) * rows, rows)
    for head in range(heads):
        plain = queries[:, head * QK : head * QK + NOPE]
        lifted = jnp.dot(plain, key_up[head], preferred_element_type=jnp.float32)
        out[pl.ds(head * rows, rows), :KV] = lifted.astype(jnp.bfloat16)
    turning = jnp.concatenate(
        [
            queries[:, head * QK + NOPE : (head + 1) * QK].astype(jnp.float32)
            for head in range(heads)
        ],
        0,
    )
    here = jnp.concatenate([table[pl.ds(first, rows), :]] * heads, 0)
    turned = rotate(turning, here).astype(jnp.bfloat16)
    tags = tag_lanes(heads * rows, lambda lane: jnp.where(lane > block, HIDDEN, 0.0))
    out[:, KV:] = jnp.concatenate([turned, tags], -1)


def lift(queries, key_up, table, other):
    rows = queries.shape[0]
    heads = key_up.shape[0]
    step = 8
    steps = heads // step

    def query_block(i):
        half = lax.axis_index("head")
        return (0, (1 - half if other else half) * steps + i)

    return pl.pallas_call(
        lift_kernel,
        grid=(steps,),
        in_specs=[
            pl.BlockSpec((rows, step * QK), query_block),
            pl.BlockSpec((step, NOPE, KV), lambda i: (i, 0, 0)),
            pl.BlockSpec(table.shape, lambda i: (0, 0)),
        ],
        out_specs=pl.BlockSpec((step * rows, WIDE), lambda i: (i, 0)),
        out_shape=jax.ShapeDtypeStruct((heads * rows, WIDE), jnp.bfloat16),
        cost_estimate=pl.CostEstimate(
            flops=2 * heads * rows * NOPE * KV,
            bytes_accessed=2 * heads * (NOPE * KV + rows * (QK + WIDE)),
            transcendentals=0,
        ),
        compiler_params=pltpu.CompilerParams(vmem_limit_bytes=12 << 20),
        name="lift",
    )(queries, key_up, table)


def attend_kernel(part, groups, query_rows, value_up, *rest):
    groups, (out, keys) = rest[:groups], rest[groups:]
    total = query_rows.shape[0]
    heads = value_up.shape[0]
    rows = total // heads
    own = groups[0].shape[0]

    @pl.when(pl.program_id(0) == 0)
    def _():
        start = 0
        for group in groups:
            keys[start : start + group.shape[0], :] = group[...]
            start += group.shape[0]

    factor = QK ** (-0.5) * float(np.log2(np.e))
    offset = lax.axis_index("head") * rows

    def score_rows(i):
        return lax.dot_general(
            query_rows[i * part : (i + 1) * part, :],
            keys[...],
            (((1,), (1,)), ((), ())),
            preferred_element_type=jnp.float32,
        )

    def finish(i, score):
        query_pos = offset + lax.rem(lax.broadcasted_iota(jnp.int32, (part, own), 0), rows)
        key_pos = lax.broadcasted_iota(jnp.int32, (part, own), 1)
        diagonal = jnp.where(key_pos <= query_pos, score[:, :own], HIDDEN)
        score = jnp.concatenate([diagonal, score[:, own:]], 1)
        peak = jnp.max(score, axis=-1, keepdims=True)
        probs = jnp.exp2((score - peak) * factor)
        totals = jnp.sum(probs, axis=-1, keepdims=True)
        sums = jnp.dot(
            probs.astype(jnp.bfloat16), keys[:, :KV], preferred_element_type=jnp.float32
        )
        latent_out = (sums / totals).astype(jnp.bfloat16)
        for j in range(part // rows):
            head = i * (part // rows) + j
            piece = jnp.dot(
                latent_out[j * rows : (j + 1) * rows],
                value_up[head],
                preferred_element_type=jnp.float32,
            )
            out[:, head * VD : (head + 1) * VD] = piece.astype(jnp.bfloat16)

    count = total // part
    score = score_rows(0)
    for i in range(count):
        later = score_rows(i + 1) if i + 1 < count else None
        finish(i, score)
        score = later


def attend(query_rows, value_up, keys, rows):
    heads = value_up.shape[0]
    step = 8
    steps = heads // step
    key_total = sum(key.shape[0] for key in keys)
    return pl.pallas_call(
        functools.partial(attend_kernel, 4 * rows, len(keys)),
        grid=(steps,),
        in_specs=[
            pl.BlockSpec((step * rows, WIDE), lambda i: (i, 0)),
            pl.BlockSpec((step, KV, VD), lambda i: (i, 0, 0)),
        ]
        + [pl.BlockSpec(key.shape, lambda i: (0, 0)) for key in keys],
        out_specs=pl.BlockSpec((rows, step * VD), lambda i: (0, i)),
        out_shape=jax.ShapeDtypeStruct((rows, heads * VD), jnp.bfloat16),
        scratch_shapes=[pltpu.VMEM((key_total, WIDE), jnp.bfloat16)],
        cost_estimate=pl.CostEstimate(
            flops=2 * heads * rows * (key_total * (WIDE + KV) + KV * VD),
            bytes_accessed=2 * heads * (KV * VD + rows * (WIDE + VD)) + 2 * key_total * WIDE,
            transcendentals=heads * rows * key_total,
        ),
        compiler_params=pltpu.CompilerParams(
            vmem_limit_bytes=(12 << 20) + 16 * key_total * WIDE
        ),
        name="attend",
    )(query_rows, value_up, *keys)


def gather_plan(count):
    moves = []
    bit = count // 2
    slots = [0]
    while bit:
        moves += [(slot, bit) for slot in slots]
        slots += [slot | bit for slot in slots]
        bit //= 2
    return moves


def layer(queries, latents, latent_gain, key_up, value_up, out_weight):
    seq_count = lax.axis_size("seq")
    head_count = lax.axis_size("head")
    seq_index = lax.axis_index("seq")
    rows = queries.shape[0]
    tok_block = latents.shape[0]
    table = jnp.asarray(rope_table(seq_count * tok_block))
    swap_pairs = [(i, (i + 1) % head_count) for i in range(head_count)]
    everyone = range(seq_count)

    own_keys, half_keys = prepare(latents.T, latent_gain.reshape(1, KV), table)
    slots = {0: half_keys}
    for slot, bit in gather_plan(seq_count):
        slots[slot | bit] = lax.ppermute(slots[slot], "seq", [(d ^ bit, d) for d in everyone])
    near = [m for m in range(1, seq_count) if m % 2 == 0] + [1]
    far = [m for m in range(2, seq_count) if m % 2 == 1]
    near_keys = jnp.concatenate([slots[m] for m in near], 0)
    far_keys = jnp.concatenate([slots[m] for m in far], 0)
    near_swap = lax.ppermute(near_keys, "head", swap_pairs)
    far_swap = lax.ppermute(far_keys, "head", swap_pairs)
    keys = [own_keys, near_keys, far_keys, near_swap, far_swap]

    key_other = lax.ppermute(key_up, "head", swap_pairs)
    value_other = lax.ppermute(value_up, "head", swap_pairs)
    weight_other = lax.ppermute(out_weight, "head", swap_pairs)
    rows_a = lift(queries, key_up, table, False)
    heads_a = attend(rows_a, value_up, keys, rows)
    rows_b = lift(queries, key_other, table, True)
    heads_b = attend(rows_b, value_other, keys, rows)

    order = list(range(0, seq_count, 2)) + list(range(seq_count - 1, 0, -2))
    place = {device: i for i, device in enumerate(order)}
    right = [(order[i], order[(i + 1) % seq_count]) for i in everyone]
    left = [(b, a) for a, b in right]
    steps = seq_count // 2
    source = np.array(
        [[order[(place[d] + k) % seq_count] for k in everyone] for d in everyone], np.int32
    )
    sources = jnp.asarray(source)[seq_index]

    def project(first, second):
        return (
            jnp.dot(first, out_weight, preferred_element_type=jnp.float32)
            + jnp.dot(second, weight_other, preferred_element_type=jnp.float32)
        ).astype(jnp.bfloat16)

    mixed = jnp.zeros((seq_count, 1, rows, out_weight.shape[1]), jnp.bfloat16)

    def put(mixed, first, second, offset):
        return lax.dynamic_update_slice(
            mixed,
            project(first, second)[None, None],
            (sources[offset % seq_count], 0, 0, 0),
        )

    right_a, right_b, left_a, left_b = heads_a, heads_b, heads_a, heads_b
    mixed = put(mixed, heads_a, heads_b, 0)
    for step in range(1, steps + 1):
        last = step == steps
        right_a = lax.ppermute(right_a, "seq", right)
        if not last:
            left_a = lax.ppermute(left_a, "seq", left)
            right_b = lax.ppermute(right_b, "seq", right)
        left_b = lax.ppermute(left_b, "seq", left)
        if last:
            mixed = put(mixed, right_a, left_b, step)
        else:
            mixed = put(mixed, right_a, right_b, -step)
            mixed = put(mixed, left_a, left_b, step)
    return mixed


def solution(mesh):
    placed = (
        P(("groups", "seq", "head"), None),
        P(("groups", "seq"), None),
        P(),
        P("head", None, None),
        P("head", None, None),
        P("head", "seq"),
    )
    return jax.shard_map(
        layer,
        mesh=mesh,
        in_specs=placed,
        out_specs=P("groups", "head", None, "seq"),
        check_vma=False,
    )
```

profile of v0, /device:TPU:0, one launch (start us, length us, event | category | flops | bytes accessed | tf_op | source)
XLA Modules:
  0.0 115.0 jit_solution(4146063829910319535)
XLA Ops:
  0.0 0.5 collective-permute-start.11
  0.5 0.0 collective-permute-start.9
  0.5 0.5 collective-permute-start.10
  1.0 1.0 copy-done
  2.0 0.9 copy-done.6
  3.0 0.7 copy-done.7
  3.6 0.3 prepare.1
  4.0 3.6 %collective-permute-start.1 = (bf16[64,640]{1,0:T(8,128)(2,1)S(1)}, bf16[64,640]{1,0:T(8,128)(2,1)S(1)}, u32[]{:S(2)}, u32[]{:S(2)}) collective-permute-start(bf16[64,640]{1,0:T(8,128)(2,1)S(1)} %get-tuple-element.8), channel_id=1, source_target_pairs={{8,0},{10,2},{12,4},{14,6},{0,8},{2,10},{4,12},{6,14},{9,1},{11,3}... | collective-permute-start | bytes 245768 | tf_op jit(solution)/shard_map/ppermute | solution.py:232
  7.6 1.6 %collective-permute-start = (bf16[64,640]{1,0:T(8,128)(2,1)S(1)}, bf16[64,640]{1,0:T(8,128)(2,1)S(1)}, u32[]{:S(2)}, u32[]{:S(2)}) collective-permute-start(bf16[64,640]{1,0:T(8,128)(2,1)S(1)} %get-tuple-element.8), channel_id=1, source_target_pairs={{4,0},{6,2},{0,4},{2,6},{12,8},{14,10},{8,12},{10,14},{5,1},{7,3},... | collective-permute-start | bytes 245768 | tf_op jit(solution)/shard_map/ppermute | solution.py:232
  9.2 3.4 %collective-permute-done.1 = bf16[64,640]{1,0:T(8,128)(2,1)S(1)} collective-permute-done((bf16[64,640]{1,0:T(8,128)(2,1)S(1)}, bf16[64,640]{1,0:T(8,128)(2,1)S(1)}, u32[]{:S(2)}, u32[]{:S(2)}) %collective-permute-start.1) | collective-permute-done | bytes 81952 | tf_op jit(solution)/shard_map/ppermute | solution.py:232
  12.6 1.6 %collective-permute-start.3 = (bf16[64,640]{1,0:T(8,128)(2,1)S(1)}, bf16[64,640]{1,0:T(8,128)(2,1)S(1)}, u32[]{:S(2)}, u32[]{:S(2)}) collective-permute-start(bf16[64,640]{1,0:T(8,128)(2,1)S(1)} %get-tuple-element.8), channel_id=1, source_target_pairs={{2,0},{0,2},{6,4},{4,6},{10,8},{8,10},{14,12},{12,14},{3,1},{1,3},... | collective-permute-start | bytes 245768 | tf_op jit(solution)/shard_map/ppermute | solution.py:232
  14.1 0.6 collective-permute-start.2
  14.8 3.8 %collective-permute-done.2 = bf16[64,640]{1,0:T(8,128)(2,1)S(1)} collective-permute-done((bf16[64,640]{1,0:T(8,128)(2,1)S(1)}, bf16[64,640]{1,0:T(8,128)(2,1)S(1)}, u32[]{:S(2)}, u32[]{:S(2)}) %collective-permute-start.2) | collective-permute-done | bytes 81952 | tf_op jit(solution)/shard_map/ppermute | solution.py:232
  18.6 0.5 collective-permute-start.5
  19.1 1.6 %collective-permute-start.4 = (bf16[64,640]{1,0:T(8,128)(2,1)S(1)}, bf16[64,640]{1,0:T(8,128)(2,1)S(1)}, u32[]{:S(2)}, u32[]{:S(2)}) collective-permute-start(bf16[64,640]{1,0:T(8,128)(2,1)S(1)} %collective-permute-done), channel_id=1, source_target_pairs={{2,0},{0,2},{6,4},{4,6},{10,8},{8,10},{14,12},{12,14},{3,1},{1,3},... | collective-permute-start | bytes 245768 | tf_op jit(solution)/shard_map/ppermute | solution.py:232
  20.7 3.2 %collective-permute-done.4 = bf16[64,640]{1,0:T(8,128)(2,1)S(1)} collective-permute-done((bf16[64,640]{1,0:T(8,128)(2,1)S(1)}, bf16[64,640]{1,0:T(8,128)(2,1)S(1)}, u32[]{:S(2)}, u32[]{:S(2)}) %collective-permute-start.4) | collective-permute-done | bytes 81952 | tf_op jit(solution)/shard_map/ppermute | solution.py:232
  23.9 1.3 %collective-permute-start.6 = (bf16[64,640]{1,0:T(8,128)(2,1)S(1)}, bf16[64,640]{1,0:T(8,128)(2,1)S(1)}, u32[]{:S(2)}, u32[]{:S(2)}) collective-permute-start(bf16[64,640]{1,0:T(8,128)(2,1)S(1)} %collective-permute-done.2), channel_id=1, source_target_pairs={{2,0},{0,2},{6,4},{4,6},{10,8},{8,10},{14,12},{12,14},{3,1},{1,3},... | collective-permute-start | bytes 245768 | tf_op jit(solution)/shard_map/ppermute | solution.py:232
  25.3 3.6 %collective-permute-done.6 = bf16[64,640]{1,0:T(8,128)(2,1)S(1)} collective-permute-done((bf16[64,640]{1,0:T(8,128)(2,1)S(1)}, bf16[64,640]{1,0:T(8,128)(2,1)S(1)}, u32[]{:S(2)}, u32[]{:S(2)}) %collective-permute-start.6) | collective-permute-done | bytes 81952 | tf_op jit(solution)/shard_map/ppermute | solution.py:232
  28.9 0.1 collective-permute-start.8
  29.0 1.0 copy-done.1
  30.0 1.1 copy-done.3
  31.1 1.6 %copy-done.5 = bf16[16,128,512]{2,1,0:T(8,128)(2,1)S(1)} copy-done((bf16[16,128,512]{2,1,0:T(8,128)(2,1)S(1)}, bf16[16,128,512]{2,1,0:T(8,128)(2,1)}, u32[]{:S(2)}) %copy-start.5) | copy-done | bytes 2097176
  32.7 0.8 lift.2.query_rows
  33.5 0.8 copy-done.8
  34.3 3.9 %attend.2 = bf16[64,2048]{1,0:T(8,128)(2,1)S(1)} custom-call(bf16[1024,640]{1,0:T(8,128)(2,1)S(1)} %lift.2.query_rows, bf16[16,512,128]{2,1,0:T(8,128)(2,1)S(1)} %copy-done.8, bf16[128,640]{1,0:T(8,128)(2,1)S(1)} %get-tuple-element.7.rest_0_, bf16[256,640]{1,0:T(8,128)(2,1)S(1)} %constant_dynamic-update-slice_fusion.rest_1_, ...), custom_call_target="tpu_custom_call" | custom-call | flops 2550136832 | bytes 4980736 | tf_op jit(solution)/shard_map/attend/pallas_call | solution.py:185
  38.3 0.8 collective-permute-start.12
  39.1 0.8 lift.3.query_rows
  40.0 4.0 %attend.3 = bf16[64,2048]{1,0:T(8,128)(2,1)S(1)} custom-call(bf16[1024,640]{1,0:T(8,128)(2,1)S(1)} %lift.3.query_rows, bf16[16,512,128]{2,1,0:T(8,128)(2,1)S(1)} %collective-permute-done.10.value_up, bf16[128,640]{1,0:T(8,128)(2,1)S(1)} %get-tuple-element.7.rest_0_, bf16[256,640]{1,0:T(8,128)(2,1)S(1)} %constant_dynamic-update-slice_fusion.rest_1_, ...), custom_call_target="tpu_custom_call" | custom-call | flops 2550136832 | bytes 4980736 | tf_op jit(solution)/shard_map/attend/pallas_call | solution.py:185
  43.9 1.3 %collective-permute-start.15 = (bf16[64,2048]{1,0:T(8,128)(2,1)S(1)}, bf16[64,2048]{1,0:T(8,128)(2,1)S(1)}, u32[]{:S(2)}, u32[]{:S(2)}) collective-permute-start(bf16[64,2048]{1,0:T(8,128)(2,1)S(1)} %attend.3), channel_id=1, source_target_pairs={{4,0},{8,4},{12,8},{14,12},{10,14},{6,10},{2,6},{0,2},{5,1},{9,5},... | collective-permute-start | bytes 786440 | tf_op jit(solution)/shard_map/ppermute | solution.py:282
  45.2 1.2 %collective-permute-start.14 = (bf16[64,2048]{1,0:T(8,128)(2,1)S(1)}, bf16[64,2048]{1,0:T(8,128)(2,1)S(1)}, u32[]{:S(2)}, u32[]{:S(2)}) collective-permute-start(bf16[64,2048]{1,0:T(8,128)(2,1)S(1)} %attend.2), channel_id=1, source_target_pairs={{4,0},{8,4},{12,8},{14,12},{10,14},{6,10},{2,6},{0,2},{5,1},{9,5},... | collective-permute-start | bytes 786440 | tf_op jit(solution)/shard_map/ppermute | solution.py:280
  46.5 0.6 collective-permute-done.12
  47.0 0.8 collective-permute-start.16
  47.8 1.7 %collective-permute-start.13 = (bf16[64,2048]{1,0:T(8,128)(2,1)S(1)}, bf16[64,2048]{1,0:T(8,128)(2,1)S(1)}, u32[]{:S(2)}, u32[]{:S(2)}) collective-permute-start(bf16[64,2048]{1,0:T(8,128)(2,1)S(1)} %attend.3), channel_id=1, source_target_pairs={{0,4},{4,8},{8,12},{12,14},{14,10},{10,6},{6,2},{2,0},{1,5},{5,9},... | collective-permute-start | bytes 786440 | tf_op jit(solution)/shard_map/ppermute | solution.py:281
  49.5 3.7 %collective-permute-done.15 = bf16[64,2048]{1,0:T(8,128)(2,1)S(1)} collective-permute-done((bf16[64,2048]{1,0:T(8,128)(2,1)S(1)}, bf16[64,2048]{1,0:T(8,128)(2,1)S(1)}, u32[]{:S(2)}, u32[]{:S(2)}) %collective-permute-start.15) | collective-permute-done | bytes 262176 | tf_op jit(solution)/shard_map/ppermute | solution.py:282
  53.2 1.2 %collective-permute-start.19 = (bf16[64,2048]{1,0:T(8,128)(2,1)S(1)}, bf16[64,2048]{1,0:T(8,128)(2,1)S(1)}, u32[]{:S(2)}, u32[]{:S(2)}) collective-permute-start(bf16[64,2048]{1,0:T(8,128)(2,1)S(1)} %collective-permute-done.15), channel_id=1, source_target_pairs={{4,0},{8,4},{12,8},{14,12},{10,14},{6,10},{2,6},{0,2},{5,1},{9,5},... | collective-permute-start | bytes 786440 | tf_op jit(solution)/shard_map/ppermute | solution.py:282
  54.4 4.4 %collective-permute-done.14 = bf16[64,2048]{1,0:T(8,128)(2,1)S(1)} collective-permute-done((bf16[64,2048]{1,0:T(8,128)(2,1)S(1)}, bf16[64,2048]{1,0:T(8,128)(2,1)S(1)}, u32[]{:S(2)}, u32[]{:S(2)}) %collective-permute-start.14) | collective-permute-done | bytes 262176 | tf_op jit(solution)/shard_map/ppermute | solution.py:280
  58.8 1.2 %collective-permute-start.18 = (bf16[64,2048]{1,0:T(8,128)(2,1)S(1)}, bf16[64,2048]{1,0:T(8,128)(2,1)S(1)}, u32[]{:S(2)}, u32[]{:S(2)}) collective-permute-start(bf16[64,2048]{1,0:T(8,128)(2,1)S(1)} %collective-permute-done.14), channel_id=1, source_target_pairs={{4,0},{8,4},{12,8},{14,12},{10,14},{6,10},{2,6},{0,2},{5,1},{9,5},... | collective-permute-start | bytes 786440 | tf_op jit(solution)/shard_map/ppermute | solution.py:280
  60.0 0.8 collective-permute-start.20
  60.8 1.7 %collective-permute-start.17 = (bf16[64,2048]{1,0:T(8,128)(2,1)S(1)}, bf16[64,2048]{1,0:T(8,128)(2,1)S(1)}, u32[]{:S(2)}, u32[]{:S(2)}) collective-permute-start(bf16[64,2048]{1,0:T(8,128)(2,1)S(1)} %collective-permute-done.13), channel_id=1, source_target_pairs={{0,4},{4,8},{8,12},{12,14},{14,10},{10,6},{6,2},{2,0},{1,5},{5,9},... | collective-permute-start | bytes 786440 | tf_op jit(solution)/shard_map/ppermute | solution.py:281
  62.5 1.9 %collective-permute-done.19 = bf16[64,2048]{1,0:T(8,128)(2,1)S(1)} collective-permute-done((bf16[64,2048]{1,0:T(8,128)(2,1)S(1)}, bf16[64,2048]{1,0:T(8,128)(2,1)S(1)}, u32[]{:S(2)}, u32[]{:S(2)}) %collective-permute-start.19) | collective-permute-done | bytes 262176 | tf_op jit(solution)/shard_map/ppermute | solution.py:282
  64.4 1.2 %collective-permute-start.23 = (bf16[64,2048]{1,0:T(8,128)(2,1)S(1)}, bf16[64,2048]{1,0:T(8,128)(2,1)S(1)}, u32[]{:S(2)}, u32[]{:S(2)}) collective-permute-start(bf16[64,2048]{1,0:T(8,128)(2,1)S(1)} %collective-permute-done.19), channel_id=1, source_target_pairs={{4,0},{8,4},{12,8},{14,12},{10,14},{6,10},{2,6},{0,2},{5,1},{9,5},... | collective-permute-start | bytes 786440 | tf_op jit(solution)/shard_map/ppermute | solution.py:282
  65.6 0.7 constant_dynamic-slice_fusion
  66.3 0.7 fusion.24
  82.0 1.3 %collective-permute-start.22 = (bf16[64,2048]{1,0:T(8,128)(2,1)S(1)}, bf16[64,2048]{1,0:T(8,128)(2,1)S(1)}, u32[]{:S(2)}, u32[]{:S(2)}) collective-permute-start(bf16[64,2048]{1,0:T(8,128)(2,1)S(1)} %collective-permute-done.18), channel_id=1, source_target_pairs={{4,0},{8,4},{12,8},{14,12},{10,14},{6,10},{2,6},{0,2},{5,1},{9,5},... | collective-permute-start | bytes 786440 | tf_op jit(solution)/shard_map/ppermute | solution.py:280
  83.3 0.8 collective-permute-start.24
  84.1 0.8 collective-permute-start.21
  84.9 1.2 %collective-permute-start.25 = (bf16[64,2048]{1,0:T(8,128)(2,1)S(1)}, bf16[64,2048]{1,0:T(8,128)(2,1)S(1)}, u32[]{:S(2)}, u32[]{:S(2)}) collective-permute-start(bf16[64,2048]{1,0:T(8,128)(2,1)S(1)} %collective-permute-done.23), channel_id=1, source_target_pairs={{4,0},{8,4},{12,8},{14,12},{10,14},{6,10},{2,6},{0,2},{5,1},{9,5},... | collective-permute-start | bytes 786440 | tf_op jit(solution)/shard_map/ppermute | solution.py:282
  86.1 2.7 %fusion.25 = f32[64,896]{1,0:T(8,128)S(1)} fusion(bf16[64,2048]{1,0:T(8,128)(2,1)S(1)} %attend.3, bf16[2048,896]{1,0:T(8,128)(2,1)} %collective-permute-done.11), kind=kOutput, calls=%fused_computation.41 | convolution fusion | flops 234881024 | bytes 4161536 | tf_op jit(solution)/shard_map/dot_general | solution.py:262
  88.8 0.1 broadcast_in_dim.27
  89.0 0.7 fusion.23
  89.7 2.7 %fusion.26 = f32[64,896]{1,0:T(8,128)S(1)} fusion(bf16[64,2048]{1,0:T(8,128)(2,1)S(1)} %collective-permute-done.13, bf16[2048,896]{1,0:T(8,128)(2,1)} %collective-permute-done.11), kind=kOutput, calls=%fused_computation.42 | convolution fusion | flops 234881024 | bytes 4161536 | tf_op jit(solution)/shard_map/dot_general | solution.py:262
  92.4 2.7 %fusion.27 = f32[64,896]{1,0:T(8,128)S(1)} fusion(bf16[64,2048]{1,0:T(8,128)(2,1)S(1)} %collective-permute-done.15, bf16[2048,896]{1,0:T(8,128)(2,1)} %collective-permute-done.11), kind=kOutput, calls=%fused_computation.43 | convolution fusion | flops 234881024 | bytes 4161536 | tf_op jit(solution)/shard_map/dot_general | solution.py:262
  95.2 2.7 %fusion.28 = f32[64,896]{1,0:T(8,128)S(1)} fusion(bf16[64,2048]{1,0:T(8,128)(2,1)S(1)} %collective-permute-done.17, bf16[2048,896]{1,0:T(8,128)(2,1)} %collective-permute-done.11), kind=kOutput, calls=%fused_computation.44 | convolution fusion | flops 234881024 | bytes 4161536 | tf_op jit(solution)/shard_map/dot_general | solution.py:262
  97.9 2.7 %fusion.29 = f32[64,896]{1,0:T(8,128)S(1)} fusion(bf16[64,2048]{1,0:T(8,128)(2,1)S(1)} %collective-permute-done.19, bf16[2048,896]{1,0:T(8,128)(2,1)} %collective-permute-done.11), kind=kOutput, calls=%fused_computation.45 | convolution fusion | flops 234881024 | bytes 4161536 | tf_op jit(solution)/shard_map/dot_general | solution.py:262
  100.7 2.7 %fusion.30 = f32[64,896]{1,0:T(8,128)S(1)} fusion(bf16[64,2048]{1,0:T(8,128)(2,1)S(1)} %collective-permute-done.21, bf16[2048,896]{1,0:T(8,128)(2,1)} %collective-permute-done.11), kind=kOutput, calls=%fused_computation.46 | convolution fusion | flops 234881024 | bytes 4161536 | tf_op jit(solution)/shard_map/dot_general | solution.py:262
  103.4 0.7 fusion.21
  104.1 0.7 fusion.19
  104.8 0.7 fusion.17
  105.6 0.7 fusion.15
  106.3 0.7 fusion.13
  107.0 2.8 %fusion.31 = f32[64,896]{1,0:T(8,128)S(1)} fusion(bf16[64,2048]{1,0:T(8,128)(2,1)S(1)} %collective-permute-done.23, bf16[2048,896]{1,0:T(8,128)(2,1)} %collective-permute-done.11), kind=kOutput, calls=%fused_computation.47 | convolution fusion | flops 234881024 | bytes 4161536 | tf_op jit(solution)/shard_map/dot_general | solution.py:262
  109.8 0.7 fusion.11
  110.5 3.1 %fusion.32 = f32[64,896]{1,0:T(8,128)S(1)} fusion(bf16[64,2048]{1,0:T(8,128)(2,1)S(1)} %collective-permute-done.25, bf16[2048,896]{1,0:T(8,128)(2,1)} %collective-permute-done.11), kind=kOutput, calls=%fused_computation.48 | convolution fusion | flops 234881024 | bytes 4161536 | tf_op jit(solution)/shard_map/dot_general | solution.py:262
  113.6 1.4 %fusion.9 = bf16[8,1,64,896]{3,2,1,0:T(8,128)(2,1)} fusion(bf16[8,1,64,896]{3,2,1,0:T(8,128)(2,1)} %copy-done.10, s32[]{:T(128)S(6)} %select_n.35, f32[64,896]{1,0:T(8,128)S(1)} %fusion.32, bf16[64,2048]{1,0:T(8,128)(2,1)S(1)} %collective-permute-done.24, bf16[2048,896]{1,0:T(8,128)(2,1)S(1)} %copy-done.9), kind=kOutput, calls=%fused_computation.17 | convolution fusion | flops 234995712 | bytes 4276228 | tf_op jit(solution)/shard_map/dot_general | solution.py:261
  (41 shorter events, 0.2 us)
Async XLA Ops:
  0.0 86.1 %collective-permute-start.11 = (bf16[2048,896]{1,0:T(8,128)(2,1)}, bf16[2048,896]{1,0:T(8,128)(2,1)}, u32[]{:S(2)}, u32[]{:S(2)}) collective-permute-start(bf16[2048,896]{1,0:T(8,128)(2,1)} %param.13), channel_id=1, source_target_pairs={{0,1},{1,0},{2,3},{3,2},{4,5},{5,4},{6,7},{7,6},{8,9},{9,8},{10,11... | collective-permute-start | bytes 11010056 | tf_op jit(solution)/shard_map/ppermute | solution.py:243
  0.5 38.6 %collective-permute-start.9 = (bf16[16,128,512]{2,1,0:T(8,128)(2,1)}, bf16[16,128,512]{2,1,0:T(8,128)(2,1)S(1)}, u32[]{:S(2)}, u32[]{:S(2)}) collective-permute-start(bf16[16,128,512]{2,1,0:T(8,128)(2,1)} %key_up.1), channel_id=1, source_target_pairs={{0,1},{1,0},{2,3},{3,2},{4,5},{5,4},{6,7},{7,6},{8,9},{9,8},{10,11... | collective-permute-start | bytes 6291464 | tf_op jit(solution)/shard_map/ppermute | solution.py:241
  0.5 39.5 %collective-permute-start.10 = (bf16[16,512,128]{2,1,0:T(8,128)(2,1)}, bf16[16,512,128]{2,1,0:T(8,128)(2,1)S(1)}, u32[]{:S(2)}, u32[]{:S(2)}) collective-permute-start(bf16[16,512,128]{2,1,0:T(8,128)(2,1)} %value_up.1), channel_id=1, source_target_pairs={{0,1},{1,0},{2,3},{3,2},{4,5},{5,4},{6,7},{7,6},{8,9},{9,8},{10,11... | collective-permute-start | bytes 6291464 | tf_op jit(solution)/shard_map/ppermute | solution.py:242
  1.0 1.0 copy-start
  2.0 0.9 copy-start.6
  3.0 0.7 copy-start.7
  4.0 8.6 %collective-permute-start.1 = (bf16[64,640]{1,0:T(8,128)(2,1)S(1)}, bf16[64,640]{1,0:T(8,128)(2,1)S(1)}, u32[]{:S(2)}, u32[]{:S(2)}) collective-permute-start(bf16[64,640]{1,0:T(8,128)(2,1)S(1)} %get-tuple-element.8), channel_id=1, source_target_pairs={{8,0},{10,2},{12,4},{14,6},{0,8},{2,10},{4,12},{6,14},{9,1},{11,3}... | collective-permute-start | bytes 245768 | tf_op jit(solution)/shard_map/ppermute | solution.py:232
  7.6 6.5 %collective-permute-start = (bf16[64,640]{1,0:T(8,128)(2,1)S(1)}, bf16[64,640]{1,0:T(8,128)(2,1)S(1)}, u32[]{:S(2)}, u32[]{:S(2)}) collective-permute-start(bf16[64,640]{1,0:T(8,128)(2,1)S(1)} %get-tuple-element.8), channel_id=1, source_target_pairs={{4,0},{6,2},{0,4},{2,6},{12,8},{14,10},{8,12},{10,14},{5,1},{7,3},... | collective-permute-start | bytes 245768 | tf_op jit(solution)/shard_map/ppermute | solution.py:232
  12.6 6.5 %collective-permute-start.3 = (bf16[64,640]{1,0:T(8,128)(2,1)S(1)}, bf16[64,640]{1,0:T(8,128)(2,1)S(1)}, u32[]{:S(2)}, u32[]{:S(2)}) collective-permute-start(bf16[64,640]{1,0:T(8,128)(2,1)S(1)} %get-tuple-element.8), channel_id=1, source_target_pairs={{2,0},{0,2},{6,4},{4,6},{10,8},{8,10},{14,12},{12,14},{3,1},{1,3},... | collective-permute-start | bytes 245768 | tf_op jit(solution)/shard_map/ppermute | solution.py:232
  14.1 4.4 %collective-permute-start.2 = (bf16[64,640]{1,0:T(8,128)(2,1)S(1)}, bf16[64,640]{1,0:T(8,128)(2,1)S(1)}, u32[]{:S(2)}, u32[]{:S(2)}) collective-permute-start(bf16[64,640]{1,0:T(8,128)(2,1)S(1)} %collective-permute-done.1), channel_id=1, source_target_pairs={{4,0},{6,2},{0,4},{2,6},{12,8},{14,10},{8,12},{10,14},{5,1},{7,3},... | collective-permute-start | bytes 245768 | tf_op jit(solution)/shard_map/ppermute | solution.py:232
  18.6 5.3 %collective-permute-start.5 = (bf16[64,640]{1,0:T(8,128)(2,1)S(1)}, bf16[64,640]{1,0:T(8,128)(2,1)S(1)}, u32[]{:S(2)}, u32[]{:S(2)}) collective-permute-start(bf16[64,640]{1,0:T(8,128)(2,1)S(1)} %collective-permute-done.1), channel_id=1, source_target_pairs={{2,0},{0,2},{6,4},{4,6},{10,8},{8,10},{14,12},{12,14},{3,1},{1,3},... | collective-permute-start | bytes 245768 | tf_op jit(solution)/shard_map/ppermute | solution.py:232
  19.1 4.8 %collective-permute-start.4 = (bf16[64,640]{1,0:T(8,128)(2,1)S(1)}, bf16[64,640]{1,0:T(8,128)(2,1)S(1)}, u32[]{:S(2)}, u32[]{:S(2)}) collective-permute-start(bf16[64,640]{1,0:T(8,128)(2,1)S(1)} %collective-permute-done), channel_id=1, source_target_pairs={{2,0},{0,2},{6,4},{4,6},{10,8},{8,10},{14,12},{12,14},{3,1},{1,3},... | collective-permute-start | bytes 245768 | tf_op jit(solution)/shard_map/ppermute | solution.py:232
  23.9 9.6 %collective-permute-start.7 = (bf16[256,640]{1,0:T(8,128)(2,1)S(1)}, bf16[256,640]{1,0:T(8,128)(2,1)S(1)}, u32[]{:S(2)}, u32[]{:S(2)}) collective-permute-start(bf16[256,640]{1,0:T(8,128)(2,1)S(1)} %constant_dynamic-update-slice_fusion.rest_1_), channel_id=1, source_target_pairs={{0,1},{1,0},{2,3},{3,2},{4,5},{5,4},{6,7},{7,6},{8,9},{9,8},{10,11... | collective-permute-start | bytes 983048 | tf_op jit(solution)/shard_map/ppermute | solution.py:237
  23.9 4.9 %collective-permute-start.6 = (bf16[64,640]{1,0:T(8,128)(2,1)S(1)}, bf16[64,640]{1,0:T(8,128)(2,1)S(1)}, u32[]{:S(2)}, u32[]{:S(2)}) collective-permute-start(bf16[64,640]{1,0:T(8,128)(2,1)S(1)} %collective-permute-done.2), channel_id=1, source_target_pairs={{2,0},{0,2},{6,4},{4,6},{10,8},{8,10},{14,12},{12,14},{3,1},{1,3},... | collective-permute-start | bytes 245768 | tf_op jit(solution)/shard_map/ppermute | solution.py:232
  28.9 4.7 %collective-permute-start.8 = (bf16[192,640]{1,0:T(8,128)(2,1)S(1)}, bf16[192,640]{1,0:T(8,128)(2,1)S(1)}, u32[]{:S(2)}, u32[]{:S(2)}) collective-permute-start(bf16[192,640]{1,0:T(8,128)(2,1)S(1)} %constant_dynamic-update-slice_fusion.4.rest_2_), channel_id=1, source_target_pairs={{0,1},{1,0},{2,3},{3,2},{4,5},{5,4},{6,7},{7,6},{8,9},{9,8},{10,11... | collective-permute-start | bytes 737288 | tf_op jit(solution)/shard_map/ppermute | solution.py:238
  29.0 1.0 copy-start.1
  30.0 1.1 copy-start.3
  31.1 1.6 %copy-start.5 = (bf16[16,128,512]{2,1,0:T(8,128)(2,1)S(1)}, bf16[16,128,512]{2,1,0:T(8,128)(2,1)}, u32[]{:S(2)}) copy-start(bf16[16,128,512]{2,1,0:T(8,128)(2,1)} %key_up.1) | copy-start | bytes 6291460
  32.7 1.6 %copy-start.8 = (bf16[16,512,128]{2,1,0:T(8,128)(2,1)S(1)}, bf16[16,512,128]{2,1,0:T(8,128)(2,1)}, u32[]{:S(2)}) copy-start(bf16[16,512,128]{2,1,0:T(8,128)(2,1)} %value_up.1) | copy-start | bytes 6291460
  34.3 4.8 %copy-start.2 = (f32[1024,128]{1,0:T(8,128)S(1)}, f32[1024,128]{1,0:T(8,128)}, u32[]{:S(2)}) copy-start(f32[1024,128]{1,0:T(8,128)} %constant.16.clone.table) | copy-start | bytes 1572868
  34.3 4.8 %copy-start.4 = (bf16[64,6144]{1,0:T(8,128)(2,1)S(1)}, bf16[64,6144]{1,0:T(8,128)(2,1)}, u32[]{:S(2)}) copy-start(bf16[64,6144]{1,0:T(8,128)(2,1)} %queries.3) | copy-start | bytes 2359300
  38.3 8.8 %collective-permute-start.12 = (bf16[64,2048]{1,0:T(8,128)(2,1)S(1)}, bf16[64,2048]{1,0:T(8,128)(2,1)S(1)}, u32[]{:S(2)}, u32[]{:S(2)}) collective-permute-start(bf16[64,2048]{1,0:T(8,128)(2,1)S(1)} %attend.2), channel_id=1, source_target_pairs={{0,4},{4,8},{8,12},{12,14},{14,10},{10,6},{6,2},{2,0},{1,5},{5,9},... | collective-permute-start | bytes 786440 | tf_op jit(solution)/shard_map/ppermute | solution.py:278
  43.9 9.2 %collective-permute-start.15 = (bf16[64,2048]{1,0:T(8,128)(2,1)S(1)}, bf16[64,2048]{1,0:T(8,128)(2,1)S(1)}, u32[]{:S(2)}, u32[]{:S(2)}) collective-permute-start(bf16[64,2048]{1,0:T(8,128)(2,1)S(1)} %attend.3), channel_id=1, source_target_pairs={{4,0},{8,4},{12,8},{14,12},{10,14},{6,10},{2,6},{0,2},{5,1},{9,5},... | collective-permute-start | bytes 786440 | tf_op jit(solution)/shard_map/ppermute | solution.py:282
  45.2 13.6 %collective-permute-start.14 = (bf16[64,2048]{1,0:T(8,128)(2,1)S(1)}, bf16[64,2048]{1,0:T(8,128)(2,1)S(1)}, u32[]{:S(2)}, u32[]{:S(2)}) collective-permute-start(bf16[64,2048]{1,0:T(8,128)(2,1)S(1)} %attend.2), channel_id=1, source_target_pairs={{4,0},{8,4},{12,8},{14,12},{10,14},{6,10},{2,6},{0,2},{5,1},{9,5},... | collective-permute-start | bytes 786440 | tf_op jit(solution)/shard_map/ppermute | solution.py:280
  47.0 13.0 %collective-permute-start.16 = (bf16[64,2048]{1,0:T(8,128)(2,1)S(1)}, bf16[64,2048]{1,0:T(8,128)(2,1)S(1)}, u32[]{:S(2)}, u32[]{:S(2)}) collective-permute-start(bf16[64,2048]{1,0:T(8,128)(2,1)S(1)} %collective-permute-done.12), channel_id=1, source_target_pairs={{0,4},{4,8},{8,12},{12,14},{14,10},{10,6},{6,2},{2,0},{1,5},{5,9},... | collective-permute-start | bytes 786440 | tf_op jit(solution)/shard_map/ppermute | solution.py:278
  47.8 13.0 %collective-permute-start.13 = (bf16[64,2048]{1,0:T(8,128)(2,1)S(1)}, bf16[64,2048]{1,0:T(8,128)(2,1)S(1)}, u32[]{:S(2)}, u32[]{:S(2)}) collective-permute-start(bf16[64,2048]{1,0:T(8,128)(2,1)S(1)} %attend.3), channel_id=1, source_target_pairs={{0,4},{4,8},{8,12},{12,14},{14,10},{10,6},{6,2},{2,0},{1,5},{5,9},... | collective-permute-start | bytes 786440 | tf_op jit(solution)/shard_map/ppermute | solution.py:281
  53.2 11.2 %collective-permute-start.19 = (bf16[64,2048]{1,0:T(8,128)(2,1)S(1)}, bf16[64,2048]{1,0:T(8,128)(2,1)S(1)}, u32[]{:S(2)}, u32[]{:S(2)}) collective-permute-start(bf16[64,2048]{1,0:T(8,128)(2,1)S(1)} %collective-permute-done.15), channel_id=1, source_target_pairs={{4,0},{8,4},{12,8},{14,12},{10,14},{6,10},{2,6},{0,2},{5,1},{9,5},... | collective-permute-start | bytes 786440 | tf_op jit(solution)/shard_map/ppermute | solution.py:282
  58.8 23.2 %collective-permute-start.18 = (bf16[64,2048]{1,0:T(8,128)(2,1)S(1)}, bf16[64,2048]{1,0:T(8,128)(2,1)S(1)}, u32[]{:S(2)}, u32[]{:S(2)}) collective-permute-start(bf16[64,2048]{1,0:T(8,128)(2,1)S(1)} %collective-permute-done.14), channel_id=1, source_target_pairs={{4,0},{8,4},{12,8},{14,12},{10,14},{6,10},{2,6},{0,2},{5,1},{9,5},... | collective-permute-start | bytes 786440 | tf_op jit(solution)/shard_map/ppermute | solution.py:280
  60.0 23.2 %collective-permute-start.20 = (bf16[64,2048]{1,0:T(8,128)(2,1)S(1)}, bf16[64,2048]{1,0:T(8,128)(2,1)S(1)}, u32[]{:S(2)}, u32[]{:S(2)}) collective-permute-start(bf16[64,2048]{1,0:T(8,128)(2,1)S(1)} %collective-permute-done.16), channel_id=1, source_target_pairs={{0,4},{4,8},{8,12},{12,14},{14,10},{10,6},{6,2},{2,0},{1,5},{5,9},... | collective-permute-start | bytes 786440 | tf_op jit(solution)/shard_map/ppermute | solution.py:278
  60.8 23.2 %collective-permute-start.17 = (bf16[64,2048]{1,0:T(8,128)(2,1)S(1)}, bf16[64,2048]{1,0:T(8,128)(2,1)S(1)}, u32[]{:S(2)}, u32[]{:S(2)}) collective-permute-start(bf16[64,2048]{1,0:T(8,128)(2,1)S(1)} %collective-permute-done.13), channel_id=1, source_target_pairs={{0,4},{4,8},{8,12},{12,14},{14,10},{10,6},{6,2},{2,0},{1,5},{5,9},... | collective-permute-start | bytes 786440 | tf_op jit(solution)/shard_map/ppermute | solution.py:281
  64.4 20.4 %collective-permute-start.23 = (bf16[64,2048]{1,0:T(8,128)(2,1)S(1)}, bf16[64,2048]{1,0:T(8,128)(2,1)S(1)}, u32[]{:S(2)}, u32[]{:S(2)}) collective-permute-start(bf16[64,2048]{1,0:T(8,128)(2,1)S(1)} %collective-permute-done.19), channel_id=1, source_target_pairs={{4,0},{8,4},{12,8},{14,12},{10,14},{6,10},{2,6},{0,2},{5,1},{9,5},... | collective-permute-start | bytes 786440 | tf_op jit(solution)/shard_map/ppermute | solution.py:282
  81.9 7.0 %copy-start.9 = (bf16[2048,896]{1,0:T(8,128)(2,1)S(1)}, bf16[2048,896]{1,0:T(8,128)(2,1)}, u32[]{:S(2)}) copy-start(bf16[2048,896]{1,0:T(8,128)(2,1)} %param.13) | copy-start | bytes 11010052
  82.0 27.8 %collective-permute-start.22 = (bf16[64,2048]{1,0:T(8,128)(2,1)S(1)}, bf16[64,2048]{1,0:T(8,128)(2,1)S(1)}, u32[]{:S(2)}, u32[]{:S(2)}) collective-permute-start(bf16[64,2048]{1,0:T(8,128)(2,1)S(1)} %collective-permute-done.18), channel_id=1, source_target_pairs={{4,0},{8,4},{12,8},{14,12},{10,14},{6,10},{2,6},{0,2},{5,1},{9,5},... | collective-permute-start | bytes 786440 | tf_op jit(solution)/shard_map/ppermute | solution.py:280
  83.3 30.3 %collective-permute-start.24 = (bf16[64,2048]{1,0:T(8,128)(2,1)S(1)}, bf16[64,2048]{1,0:T(8,128)(2,1)S(1)}, u32[]{:S(2)}, u32[]{:S(2)}) collective-permute-start(bf16[64,2048]{1,0:T(8,128)(2,1)S(1)} %collective-permute-done.20), channel_id=1, source_target_pairs={{0,4},{4,8},{8,12},{12,14},{14,10},{10,6},{6,2},{2,0},{1,5},{5,9},... | collective-permute-start | bytes 786440 | tf_op jit(solution)/shard_map/ppermute | solution.py:278
  84.1 16.6 %collective-permute-start.21 = (bf16[64,2048]{1,0:T(8,128)(2,1)S(1)}, bf16[64,2048]{1,0:T(8,128)(2,1)S(1)}, u32[]{:S(2)}, u32[]{:S(2)}) collective-permute-start(bf16[64,2048]{1,0:T(8,128)(2,1)S(1)} %collective-permute-done.17), channel_id=1, source_target_pairs={{0,4},{4,8},{8,12},{12,14},{14,10},{10,6},{6,2},{2,0},{1,5},{5,9},... | collective-permute-start | bytes 786440 | tf_op jit(solution)/shard_map/ppermute | solution.py:281
  84.9 25.7 %collective-permute-start.25 = (bf16[64,2048]{1,0:T(8,128)(2,1)S(1)}, bf16[64,2048]{1,0:T(8,128)(2,1)S(1)}, u32[]{:S(2)}, u32[]{:S(2)}) collective-permute-start(bf16[64,2048]{1,0:T(8,128)(2,1)S(1)} %collective-permute-done.23), channel_id=1, source_target_pairs={{4,0},{8,4},{12,8},{14,12},{10,14},{6,10},{2,6},{0,2},{5,1},{9,5},... | collective-permute-start | bytes 786440 | tf_op jit(solution)/shard_map/ppermute | solution.py:282
  110.5 3.1 %copy-start.10 = (bf16[8,1,64,896]{3,2,1,0:T(8,128)(2,1)}, bf16[8,1,64,896]{3,2,1,0:T(8,128)(2,1)S(1)}, u32[]{:S(2)}) copy-start(bf16[8,1,64,896]{3,2,1,0:T(8,128)(2,1)S(1)} %fusion.11) | copy-start | bytes 2752516
where the time goes:
time: 116 us; the launch traced here: 115 us
  matrix products  28.6 us (25%)
  starting transfers between devices  28 us (24%)
  waiting for transfers between devices  24.5 us (21%)
  between operations  15.2 us (13%)
  Pallas kernels  9.84 us (8%)
  local copies, waits for them, and re-layouts  8.73 us (8%)
    dot_general x8, matrix products, project(): jnp.dot(second, weight_other, preferred_element_type=jnp.float32)  22.2 us
    ppermute x7, waiting for transfers between devices, layer(): lax.ppermute(slots[slot], 'seq', [(d ^ bit, d) for d in everyone])  14 us
    ppermute x7, starting transfers between devices, layer(): lax.ppermute(slots[slot], 'seq', [(d ^ bit, d) for d in everyone])  10.8 us
    pallas_call x2, Pallas kernels, attend(): pl.pallas_call(functools.partial(attend_kernel, 4 * rows, len(keys)), gri...  7.9 us
    unnamed x27, local copies, waits for them, and re-layouts  7.24 us
    dot_general x8, matrix products, project(): jnp.dot(first, out_weight, preferred_element_type=jnp.float32)  6.43 us
    ppermute x4, waiting for transfers between devices, layer(): left_b = lax.ppermute(left_b, 'seq', left)  5.55 us
    ppermute x4, starting transfers between devices, layer(): left_b = lax.ppermute(left_b, 'seq', left)  4.97 us
  transfers between devices with their start and end apart: 26, of which 8 were waited for; matrix products, arithmetic and copies ran while one was open for 25% of the time, Pallas kernels for 9%

commit v1 on v0

--- a/solution.py
+++ b/solution.py
@@ -19,18 +19,13 @@
 HIDDEN = -1e30
 
 
-def rope_table(total):
+def rope_angles(position, index):
     middle = ROPE // 2
-    frequency = (10000.0 ** (-np.arange(middle, dtype=np.float32) / middle)).astype(np.float32)
-    angles = (np.arange(total, dtype=np.float32)[:, None] * frequency).astype(np.float64)
-    cosine, sine = np.cos(angles), np.sin(angles)
-    return np.concatenate([cosine, cosine, -sine, sine], -1).astype(np.float32)
-
-
-def rotate(values, table):
-    middle = ROPE // 2
-    swapped = jnp.concatenate([values[:, middle:], values[:, :middle]], -1)
-    return values * table[:, :ROPE] + swapped * table[:, ROPE:]
+    frequency = jnp.ones(index.shape, jnp.float32)
+    for bit in range(middle.bit_length() - 1):
+        factor = float(10000.0 ** (-(1 << bit) / middle))
+        frequency *= jnp.where((index >> bit) % 2 == 1, factor, 1.0)
+    return position.astype(jnp.float32) * frequency
 
 
 def tag_lanes(rows, value):
@@ -38,7 +33,7 @@
     return value(lane).astype(jnp.bfloat16)
 
 
-def prepare_kernel(half, latents, gain, table, full_out, half_out):
+def prepare_kernel(half, latents, gain, full_out, half_out):
     block = lax.axis_index("seq")
     latent_f = latents[...].astype(jnp.float32)
     tokens = latent_f.shape[1]
@@ -46,15 +41,20 @@
     spread = jnp.mean(compressed * compressed, axis=0, keepdims=True)
     normed = (compressed * lax.rsqrt(spread + EPS)).T * gain[...]
     full_out[:, :KV] = normed.astype(jnp.bfloat16)
-    here = table[pl.ds(pl.multiple_of(block * tokens, tokens), tokens), :]
-    rope = rotate(latent_f[KV:].T, here).astype(jnp.bfloat16)
+    shape = (ROPE // 2, tokens)
+    position = block * tokens + lax.broadcasted_iota(jnp.int32, shape, 1)
+    angles = rope_angles(position, lax.broadcasted_iota(jnp.int32, shape, 0))
+    cosine, sine = jnp.cos(angles), jnp.sin(angles)
+    former, latter = latent_f[KV : KV + ROPE // 2], latent_f[KV + ROPE // 2 :]
+    halves = [former * cosine - latter * sine, former * sine + latter * cosine]
+    rope = jnp.concatenate(halves, 0).T.astype(jnp.bfloat16)
     tags = tag_lanes(tokens, lambda lane: jnp.where(lane == block, 1.0, 0.0))
     full_out[:, KV:] = jnp.concatenate([rope, tags], -1)
     start = lax.axis_index("head") * half
     half_out[...] = full_out[pl.ds(pl.multiple_of(start, half), half), :]
 
 
-def prepare(latents, gain, table):
+def prepare(latents, gain):
     rows = latents.shape[1]
     half = rows // 2
     return pl.pallas_call(
@@ -63,23 +63,31 @@
             jax.ShapeDtypeStruct((rows, WIDE), jnp.bfloat16),
             jax.ShapeDtypeStruct((half, WIDE), jnp.bfloat16),
         ],
+        compiler_params=pltpu.CompilerParams(vmem_limit_bytes=12 << 20),
         cost_estimate=pl.CostEstimate(
             flops=10**8, bytes_accessed=4 * rows * WIDE, transcendentals=rows
         ),
-        compiler_params=pltpu.CompilerParams(vmem_limit_bytes=12 << 20),
         name="prepare",
-    )(latents, gain, table)
-
-
-def lift_kernel(queries, key_up, table, out):
+    )(latents, gain)
+
+
+def lift_kernel(queries, key_up, out):
     rows = queries.shape[0]
     heads = key_up.shape[0]
     block = lax.axis_index("seq")
-    first = pl.multiple_of((2 * block + lax.axis_index("head")) * rows, rows)
     for head in range(heads):
         plain = queries[:, head * QK : head * QK + NOPE]
         lifted = jnp.dot(plain, key_up[head], preferred_element_type=jnp.float32)
         out[pl.ds(head * rows, rows), :KV] = lifted.astype(jnp.bfloat16)
+    shape = (rows, ROPE)
+    first = (2 * block + lax.axis_index("head")) * rows
+    position = first + lax.broadcasted_iota(jnp.int32, shape, 0)
+    lane = lax.broadcasted_iota(jnp.int32, shape, 1)
+    upper = lane >= ROPE // 2
+    angles = rope_angles(position, jnp.where(upper, lane - ROPE // 2, lane))
+    cosine = jnp.concatenate([jnp.cos(angles)] * heads, 0)
+    sine = jnp.sin(angles)
+    sine = jnp.concatenate([jnp.where(upper, sine, -sine)] * heads, 0)
     turning = jnp.concatenate(
         [
             queries[:, head * QK + NOPE : (head + 1) * QK].astype(jnp.float32)
@@ -87,13 +95,13 @@
         ],
         0,
     )
-    here = jnp.concatenate([table[pl.ds(first, rows), :]] * heads, 0)
-    turned = rotate(turning, here).astype(jnp.bfloat16)
+    swapped = jnp.concatenate([turning[:, ROPE // 2 :], turning[:, : ROPE // 2]], -1)
+    turned = (turning * cosine + swapped * sine).astype(jnp.bfloat16)
     tags = tag_lanes(heads * rows, lambda lane: jnp.where(lane > block, HIDDEN, 0.0))
     out[:, KV:] = jnp.concatenate([turned, tags], -1)
 
 
-def lift(queries, key_up, table, other):
+def lift(queries, key_up, other):
     rows = queries.shape[0]
     heads = key_up.shape[0]
     step = 8
@@ -109,7 +117,6 @@
         in_specs=[
             pl.BlockSpec((rows, step * QK), query_block),
             pl.BlockSpec((step, NOPE, KV), lambda i: (i, 0, 0)),
-            pl.BlockSpec(table.shape, lambda i: (0, 0)),
         ],
         out_specs=pl.BlockSpec((step * rows, WIDE), lambda i: (i, 0)),
         out_shape=jax.ShapeDtypeStruct((heads * rows, WIDE), jnp.bfloat16),
@@ -120,7 +127,7 @@
         ),
         compiler_params=pltpu.CompilerParams(vmem_limit_bytes=12 << 20),
         name="lift",
-    )(queries, key_up, table)
+    )(queries, key_up)
 
 
 def attend_kernel(part, groups, query_rows, value_up, *rest):
@@ -205,6 +212,65 @@
     )(query_rows, value_up, *keys)
 
 
+def project_kernel(count, offsets, *refs):
+    pieces = len(offsets)
+    firsts, seconds = refs[:pieces], refs[pieces : 2 * pieces]
+    own_weight, other_weight = refs[2 * pieces : 2 * pieces + 2]
+    out, held, sems = refs[-3:]
+    rows = firsts[0].shape[0]
+
+    def stack(parts):
+        return jnp.concatenate([part[...] for part in parts], 0) if pieces > 1 else parts[0][...]
+
+    product = jnp.dot(stack(firsts), own_weight[...], preferred_element_type=jnp.float32)
+    product += jnp.dot(stack(seconds), other_weight[...], preferred_element_type=jnp.float32)
+    held[...] = product.astype(jnp.bfloat16)
+    block = lax.axis_index("seq")
+    half = block // 2
+    place = jnp.where(block - 2 * half == 0, half, count - 1 - half)
+    copies = []
+    for i, offset in enumerate(offsets):
+        at = lax.rem(place + offset % count, count)
+        source = jnp.where(at < count // 2, 2 * at, 2 * (count - 1 - at) + 1)
+        copies.append(
+            pltpu.make_async_copy(held.at[pl.ds(i * rows, rows), :], out.at[source, 0], sems.at[i])
+        )
+        copies[-1].start()
+    for copy in copies:
+        copy.wait()
+
+
+def project(count, offsets, firsts, seconds, own_weight, other_weight, mixed):
+    rows, depth = firsts[0].shape
+    columns = own_weight.shape[1]
+    pieces = len(offsets)
+    operands = [*firsts, *seconds, own_weight, other_weight]
+    aliases = {}
+    if mixed is not None:
+        aliases = {len(operands): 0}
+        operands.append(mixed)
+    vmem = pl.BlockSpec(memory_space=pltpu.VMEM)
+    anywhere = pl.BlockSpec(memory_space=pl.ANY)
+    return pl.pallas_call(
+        functools.partial(project_kernel, count, offsets),
+        in_specs=[vmem] * (2 * pieces + 2) + [anywhere] * len(aliases),
+        out_specs=anywhere,
+        out_shape=jax.ShapeDtypeStruct((count, 1, rows, columns), jnp.bfloat16),
+        scratch_shapes=[
+            pltpu.VMEM((pieces * rows, columns), jnp.bfloat16),
+            pltpu.SemaphoreType.DMA((pieces,)),
+        ],
+        input_output_aliases=aliases,
+        compiler_params=pltpu.CompilerParams(vmem_limit_bytes=8 << 20),
+        cost_estimate=pl.CostEstimate(
+            flops=4 * pieces * rows * depth * columns,
+            bytes_accessed=4 * depth * columns,
+            transcendentals=0,
+        ),
+        name="project",
+    )(*operands)
+
+
 def gather_plan(count):
     moves = []
     bit = count // 2
@@ -219,14 +285,11 @@
 def layer(queries, latents, latent_gain, key_up, value_up, out_weight):
     seq_count = lax.axis_size("seq")
     head_count = lax.axis_size("head")
-    seq_index = lax.axis_index("seq")
     rows = queries.shape[0]
-    tok_block = latents.shape[0]
-    table = jnp.asarray(rope_table(seq_count * tok_block))
     swap_pairs = [(i, (i + 1) % head_count) for i in range(head_count)]
     everyone = range(seq_count)
 
-    own_keys, half_keys = prepare(latents.T, latent_gain.reshape(1, KV), table)
+    own_keys, half_keys = prepare(latents.T, latent_gain.reshape(1, KV))
     slots = {0: half_keys}
     for slot, bit in gather_plan(seq_count):
         slots[slot | bit] = lax.ppermute(slots[slot], "seq", [(d ^ bit, d) for d in everyone])
@@ -241,38 +304,24 @@
     key_other = lax.ppermute(key_up, "head", swap_pairs)
     value_other = lax.ppermute(value_up, "head", swap_pairs)
     weight_other = lax.ppermute(out_weight, "head", swap_pairs)
-    rows_a = lift(queries, key_up, table, False)
+    rows_a = lift(queries, key_up, False)
     heads_a = attend(rows_a, value_up, keys, rows)
-    rows_b = lift(queries, key_other, table, True)
+    rows_b = lift(queries, key_other, True)
     heads_b = attend(rows_b, value_other, keys, rows)
 
     order = list(range(0, seq_count, 2)) + list(range(seq_count - 1, 0, -2))
-    place = {device: i for i, device in enumerate(order)}
     right = [(order[i], order[(i + 1) % seq_count]) for i in everyone]
     left = [(b, a) for a, b in right]
     steps = seq_count // 2
-    source = np.array(
-        [[order[(place[d] + k) % seq_count] for k in everyone] for d in everyone], np.int32
-    )
-    sources = jnp.asarray(source)[seq_index]
-
-    def project(first, second):
-        return (
-            jnp.dot(first, out_weight, preferred_element_type=jnp.float32)
-            + jnp.dot(second, weight_other, preferred_element_type=jnp.float32)
-        ).astype(jnp.bfloat16)
-
-    mixed = jnp.zeros((seq_count, 1, rows, out_weight.shape[1]), jnp.bfloat16)
-
-    def put(mixed, first, second, offset):
-        return lax.dynamic_update_slice(
-            mixed,
-            project(first, second)[None, None],
-            (sources[offset % seq_count], 0, 0, 0),
+
+    def put(mixed, *pieces):
+        firsts, seconds, offsets = zip(*pieces)
+        return project(
+            seq_count, offsets, firsts, seconds, out_weight, weight_other, mixed
         )
 
     right_a, right_b, left_a, left_b = heads_a, heads_b, heads_a, heads_b
-    mixed = put(mixed, heads_a, heads_b, 0)
+    mixed = put(None, (heads_a, heads_b, 0))
     for step in range(1, steps + 1):
         last = step == steps
         right_a = lax.ppermute(right_a, "seq", right)
@@ -281,10 +330,9 @@
             right_b = lax.ppermute(right_b, "seq", right)
         left_b = lax.ppermute(left_b, "seq", left)
         if last:
-            mixed = put(mixed, right_a, left_b, step)
+            mixed = put(mixed, (right_a, left_b, step))
         else:
-            mixed = put(mixed, right_a, right_b, -step)
-            mixed = put(mixed, left_a, left_b, step)
+            mixed = put(mixed, (right_a, right_b, -step), (left_a, left_b, step))
     return mixed
 
 

time: 116 us -> 86.5 us (0.75)
  matrix products: 28.6 us -> 0 us
  between operations: 15.2 us -> 0.36 us
  Pallas kernels: 9.84 us -> 20 us
  waiting for transfers between devices: 24.5 us -> 33.1 us
  local copies, waits for them, and re-layouts: 8.73 us -> 5.03 us
    dot_general x16 -> x0, matrix products: 28.6 us -> none  [the longest x8 22.2 us: project(): jnp.dot(second, weight_other, preferred_element_type=jnp.float32)]
    pallas_call x0 -> x5, Pallas kernels: none -> 9.92 us  [project(): pl.pallas_call(functools.partial(project_kernel, count, offsets), in_spec...]
    ppermute x4, waiting for transfers between devices: 5.55 us -> 10.2 us  [layer(): left_b = lax.ppermute(left_b, 'seq', left)]
    ppermute x3, waiting for transfers between devices: 4.39 us -> 8.79 us  [layer(): left_a = lax.ppermute(left_a, 'seq', left)]
    unnamed x27 -> x19, local copies, waits for them, and re-layouts: 7.24 us -> 5 us
    ppermute x3, starting transfers between devices: 4.19 us -> 2.4 us  [layer(): right_b = lax.ppermute(right_b, 'seq', right)]
    ppermute x4, starting transfers between devices: 3.22 us -> 4.93 us  [layer(): right_a = lax.ppermute(right_a, 'seq', right)]
  transfers between devices with their start and end apart: 26 -> 26, of which waited for: 8 -> 11; matrix products, arithmetic and copies ran while one was open for 25% -> 0% of each run, Pallas kernels for 9% -> 21%
where the time goes in v1:
time: 86.5 us; the launch traced here: 86.3 us
  waiting for transfers between devices  33.1 us (38%)
  starting transfers between devices  27.8 us (32%)
  Pallas kernels  20 us (23%)
  local copies, waits for them, and re-layouts  5.03 us (6%)
    ppermute x7, waiting for transfers between devices, layer(): lax.ppermute(slots[slot], 'seq', [(d ^ bit, d) for d in everyone])  14 us
    ppermute x7, starting transfers between devices, layer(): lax.ppermute(slots[slot], 'seq', [(d ^ bit, d) for d in everyone])  10.8 us
    ppermute x4, waiting for transfers between devices, layer(): left_b = lax.ppermute(left_b, 'seq', left)  10.2 us
    pallas_call x5, Pallas kernels, project(): pl.pallas_call(functools.partial(project_kernel, count, offsets), in_spec...  9.92 us
    ppermute x3, waiting for transfers between devices, layer(): left_a = lax.ppermute(left_a, 'seq', left)  8.79 us
    pallas_call x2, Pallas kernels, attend(): pl.pallas_call(functools.partial(attend_kernel, 4 * rows, len(keys)), gri...  7.9 us
    unnamed x19, local copies, waits for them, and re-layouts  5 us
    ppermute x4, starting transfers between devices, layer(): left_b = lax.ppermute(left_b, 'seq', left)  4.94 us
  transfers between devices with their start and end apart: 26, of which 11 were waited for; matrix products, arithmetic and copies ran while one was open for 0% of the time, Pallas kernels for 21%

profile of v1, /device:TPU:0, one launch (start us, length us, event | category | flops | bytes accessed | tf_op | source)
XLA Modules:
  0.0 86.3 jit_solution(1630781196044693269)
XLA Ops:
  0.0 0.5 collective-permute-start.19
  0.5 0.0 collective-permute-start.13
  0.5 0.5 collective-permute-start.14
  1.0 0.9 %copy-done.5 = bf16[128,576]{0,1:T(8,128)(2,1)S(1)} copy-done((bf16[128,576]{0,1:T(8,128)(2,1)S(1)}, bf16[128,576]{0,1:T(8,128)(2,1)}, u32[]{:S(2)}) %copy-start.5) | copy-done | bytes 147480
  1.9 0.7 copy-done.6
  2.6 0.3 prepare.1
  2.9 3.6 %collective-permute-start.1 = (bf16[64,640]{1,0:T(8,128)(2,1)S(1)}, bf16[64,640]{1,0:T(8,128)(2,1)S(1)}, u32[]{:S(2)}, u32[]{:S(2)}) collective-permute-start(bf16[64,640]{1,0:T(8,128)(2,1)S(1)} %get-tuple-element.8), channel_id=1, source_target_pairs={{8,0},{10,2},{12,4},{14,6},{0,8},{2,10},{4,12},{6,14},{9,1},{11,3}... | collective-permute-start | bytes 245768 | tf_op jit(solution)/shard_map/ppermute | solution.py:295
  6.5 1.6 %collective-permute-start = (bf16[64,640]{1,0:T(8,128)(2,1)S(1)}, bf16[64,640]{1,0:T(8,128)(2,1)S(1)}, u32[]{:S(2)}, u32[]{:S(2)}) collective-permute-start(bf16[64,640]{1,0:T(8,128)(2,1)S(1)} %get-tuple-element.8), channel_id=1, source_target_pairs={{4,0},{6,2},{0,4},{2,6},{12,8},{14,10},{8,12},{10,14},{5,1},{7,3},... | collective-permute-start | bytes 245768 | tf_op jit(solution)/shard_map/ppermute | solution.py:295
  8.1 3.4 %collective-permute-done.1 = bf16[64,640]{1,0:T(8,128)(2,1)S(1)} collective-permute-done((bf16[64,640]{1,0:T(8,128)(2,1)S(1)}, bf16[64,640]{1,0:T(8,128)(2,1)S(1)}, u32[]{:S(2)}, u32[]{:S(2)}) %collective-permute-start.1) | collective-permute-done | bytes 81952 | tf_op jit(solution)/shard_map/ppermute | solution.py:295
  11.5 1.6 %collective-permute-start.3 = (bf16[64,640]{1,0:T(8,128)(2,1)S(1)}, bf16[64,640]{1,0:T(8,128)(2,1)S(1)}, u32[]{:S(2)}, u32[]{:S(2)}) collective-permute-start(bf16[64,640]{1,0:T(8,128)(2,1)S(1)} %get-tuple-element.8), channel_id=1, source_target_pairs={{2,0},{0,2},{6,4},{4,6},{10,8},{8,10},{14,12},{12,14},{3,1},{1,3},... | collective-permute-start | bytes 245768 | tf_op jit(solution)/shard_map/ppermute | solution.py:295
  13.1 0.0 collective-permute-done
  13.1 0.6 collective-permute-start.2
  13.7 3.8 %collective-permute-done.2 = bf16[64,640]{1,0:T(8,128)(2,1)S(1)} collective-permute-done((bf16[64,640]{1,0:T(8,128)(2,1)S(1)}, bf16[64,640]{1,0:T(8,128)(2,1)S(1)}, u32[]{:S(2)}, u32[]{:S(2)}) %collective-permute-start.2) | collective-permute-done | bytes 81952 | tf_op jit(solution)/shard_map/ppermute | solution.py:295
  17.5 0.5 collective-permute-start.5
  18.0 0.0 collective-permute-done.3
  18.0 1.6 %collective-permute-start.4 = (bf16[64,640]{1,0:T(8,128)(2,1)S(1)}, bf16[64,640]{1,0:T(8,128)(2,1)S(1)}, u32[]{:S(2)}, u32[]{:S(2)}) collective-permute-start(bf16[64,640]{1,0:T(8,128)(2,1)S(1)} %collective-permute-done), channel_id=1, source_target_pairs={{2,0},{0,2},{6,4},{4,6},{10,8},{8,10},{14,12},{12,14},{3,1},{1,3},... | collective-permute-start | bytes 245768 | tf_op jit(solution)/shard_map/ppermute | solution.py:295
  19.6 3.2 %collective-permute-done.4 = bf16[64,640]{1,0:T(8,128)(2,1)S(1)} collective-permute-done((bf16[64,640]{1,0:T(8,128)(2,1)S(1)}, bf16[64,640]{1,0:T(8,128)(2,1)S(1)}, u32[]{:S(2)}, u32[]{:S(2)}) %collective-permute-start.4) | collective-permute-done | bytes 81952 | tf_op jit(solution)/shard_map/ppermute | solution.py:295
  22.8 0.0 collective-permute-start.7
  22.8 0.0 collective-permute-done.5
  22.8 1.3 %collective-permute-start.6 = (bf16[64,640]{1,0:T(8,128)(2,1)S(1)}, bf16[64,640]{1,0:T(8,128)(2,1)S(1)}, u32[]{:S(2)}, u32[]{:S(2)}) collective-permute-start(bf16[64,640]{1,0:T(8,128)(2,1)S(1)} %collective-permute-done.2), channel_id=1, source_target_pairs={{2,0},{0,2},{6,4},{4,6},{10,8},{8,10},{14,12},{12,14},{3,1},{1,3},... | collective-permute-start | bytes 245768 | tf_op jit(solution)/shard_map/ppermute | solution.py:295
  24.2 3.6 %collective-permute-done.6 = bf16[64,640]{1,0:T(8,128)(2,1)S(1)} collective-permute-done((bf16[64,640]{1,0:T(8,128)(2,1)S(1)}, bf16[64,640]{1,0:T(8,128)(2,1)S(1)}, u32[]{:S(2)}, u32[]{:S(2)}) %collective-permute-start.6) | collective-permute-done | bytes 81952 | tf_op jit(solution)/shard_map/ppermute | solution.py:295
  27.8 0.1 collective-permute-start.8
  27.9 0.0 copy-start.1
  27.9 1.1 %copy-done.1 = bf16[64,6144]{1,0:T(8,128)(2,1)S(1)} copy-done((bf16[64,6144]{1,0:T(8,128)(2,1)S(1)}, bf16[64,6144]{1,0:T(8,128)(2,1)}, u32[]{:S(2)}) %copy-start.1) | copy-done | bytes 786456
  29.0 1.6 %copy-done.3 = bf16[16,128,512]{2,1,0:T(8,128)(2,1)S(1)} copy-done((bf16[16,128,512]{2,1,0:T(8,128)(2,1)S(1)}, bf16[16,128,512]{2,1,0:T(8,128)(2,1)}, u32[]{:S(2)}) %copy-start.3) | copy-done | bytes 2097176
  30.6 0.9 %lift.2.query_rows = bf16[1024,640]{1,0:T(8,128)(2,1)S(1)} custom-call(bf16[64,6144]{1,0:T(8,128)(2,1)S(1)} %copy-done.1, bf16[16,128,512]{2,1,0:T(8,128)(2,1)S(1)} %copy-done.3), custom_call_target="tpu_custom_call" | custom-call | flops 134217728 | bytes 3801088 | tf_op jit(solution)/shard_map/lift/pallas_call | solution.py:114
  31.5 0.0 collective-permute-done.7.rest_3_
  31.5 0.0 collective-permute-done.8.rest_4_
  31.6 0.6 copy-done.4
  32.2 3.9 %attend.2.refs_0_ = bf16[64,2048]{1,0:T(8,128)(2,1)S(1)} custom-call(bf16[1024,640]{1,0:T(8,128)(2,1)S(1)} %lift.2.query_rows, bf16[16,512,128]{2,1,0:T(8,128)(2,1)S(1)} %copy-done.4, bf16[128,640]{1,0:T(8,128)(2,1)S(1)} %get-tuple-element.7.rest_0_, bf16[256,640]{1,0:T(8,128)(2,1)S(1)} %constant_dynamic-update-slice_fusion.rest_1_, ...), custom_call_target="tpu_custom_call" | custom-call | flops 2550136832 | bytes 4980736 | tf_op jit(solution)/shard_map/attend/pallas_call | solution.py:192
  36.1 0.9 collective-permute-start.9
  37.0 0.0 collective-permute-done.13.key_up
  37.0 0.9 %lift.3.query_rows = bf16[1024,640]{1,0:T(8,128)(2,1)S(1)} custom-call(bf16[64,6144]{1,0:T(8,128)(2,1)S(1)} %copy-done.2, bf16[16,128,512]{2,1,0:T(8,128)(2,1)S(1)} %collective-permute-done.13.key_up), custom_call_target="tpu_custom_call" | custom-call | flops 134217728 | bytes 3801088 | tf_op jit(solution)/shard_map/lift/pallas_call | solution.py:114
  37.9 0.0 collective-permute-done.14.value_up
  37.9 0.0 copy-start
  38.0 4.0 %attend.3.refs_1_ = bf16[64,2048]{1,0:T(8,128)(2,1)S(1)} custom-call(bf16[1024,640]{1,0:T(8,128)(2,1)S(1)} %lift.3.query_rows, bf16[16,512,128]{2,1,0:T(8,128)(2,1)S(1)} %collective-permute-done.14.value_up, bf16[128,640]{1,0:T(8,128)(2,1)S(1)} %get-tuple-element.7.rest_0_, bf16[256,640]{1,0:T(8,128)(2,1)S(1)} %constant_dynamic-update-slice_fusion.rest_1_, ...), custom_call_target="tpu_custom_call" | custom-call | flops 2550136832 | bytes 4980736 | tf_op jit(solution)/shard_map/attend/pallas_call | solution.py:192
  41.9 1.3 %collective-permute-start.15 = (bf16[64,2048]{1,0:T(8,128)(2,1)S(1)}, bf16[64,2048]{1,0:T(8,128)(2,1)S(1)}, u32[]{:S(2)}, u32[]{:S(2)}) collective-permute-start(bf16[64,2048]{1,0:T(8,128)(2,1)S(1)} %attend.3.refs_1_), channel_id=1, source_target_pairs={{4,0},{8,4},{12,8},{14,12},{10,14},{6,10},{2,6},{0,2},{5,1},{9,5},... | collective-permute-start | bytes 786440 | tf_op jit(solution)/shard_map/ppermute | solution.py:331
  43.2 1.2 %collective-permute-start.20 = (bf16[64,2048]{1,0:T(8,128)(2,1)S(1)}, bf16[64,2048]{1,0:T(8,128)(2,1)S(1)}, u32[]{:S(2)}, u32[]{:S(2)}) collective-permute-start(bf16[64,2048]{1,0:T(8,128)(2,1)S(1)} %attend.2.refs_0_), channel_id=1, source_target_pairs={{4,0},{8,4},{12,8},{14,12},{10,14},{6,10},{2,6},{0,2},{5,1},{9,5},... | collective-permute-start | bytes 786440 | tf_op jit(solution)/shard_map/ppermute | solution.py:329
  44.4 0.8 collective-permute-start.23
  45.2 0.0 collective-permute-done.9.refs_0_
  45.2 0.8 collective-permute-start.10
  46.0 5.1 %collective-permute-done.15.refs_3_ = bf16[64,2048]{1,0:T(8,128)(2,1)S(1)} collective-permute-done((bf16[64,2048]{1,0:T(8,128)(2,1)S(1)}, bf16[64,2048]{1,0:T(8,128)(2,1)S(1)}, u32[]{:S(2)}, u32[]{:S(2)}) %collective-permute-start.15) | collective-permute-done | bytes 262176 | tf_op jit(solution)/shard_map/ppermute | solution.py:331
  51.2 1.2 %collective-permute-start.16 = (bf16[64,2048]{1,0:T(8,128)(2,1)S(1)}, bf16[64,2048]{1,0:T(8,128)(2,1)S(1)}, u32[]{:S(2)}, u32[]{:S(2)}) collective-permute-start(bf16[64,2048]{1,0:T(8,128)(2,1)S(1)} %collective-permute-done.15.refs_3_), channel_id=1, source_target_pairs={{4,0},{8,4},{12,8},{14,12},{10,14},{6,10},{2,6},{0,2},{5,1},{9,5},... | collective-permute-start | bytes 786440 | tf_op jit(solution)/shard_map/ppermute | solution.py:331
  52.4 4.4 %collective-permute-done.20.refs_1_ = bf16[64,2048]{1,0:T(8,128)(2,1)S(1)} collective-permute-done((bf16[64,2048]{1,0:T(8,128)(2,1)S(1)}, bf16[64,2048]{1,0:T(8,128)(2,1)S(1)}, u32[]{:S(2)}, u32[]{:S(2)}) %collective-permute-start.20) | collective-permute-done | bytes 262176 | tf_op jit(solution)/shard_map/ppermute | solution.py:329
  56.8 1.2 %collective-permute-start.21 = (bf16[64,2048]{1,0:T(8,128)(2,1)S(1)}, bf16[64,2048]{1,0:T(8,128)(2,1)S(1)}, u32[]{:S(2)}, u32[]{:S(2)}) collective-permute-start(bf16[64,2048]{1,0:T(8,128)(2,1)S(1)} %collective-permute-done.20.refs_1_), channel_id=1, source_target_pairs={{4,0},{8,4},{12,8},{14,12},{10,14},{6,10},{2,6},{0,2},{5,1},{9,5},... | collective-permute-start | bytes 786440 | tf_op jit(solution)/shard_map/ppermute | solution.py:329
  58.0 0.8 collective-permute-start.24
  58.8 0.0 collective-permute-done.10.refs_0_
  58.8 1.7 %collective-permute-start.11 = (bf16[64,2048]{1,0:T(8,128)(2,1)S(1)}, bf16[64,2048]{1,0:T(8,128)(2,1)S(1)}, u32[]{:S(2)}, u32[]{:S(2)}) collective-permute-start(bf16[64,2048]{1,0:T(8,128)(2,1)S(1)} %collective-permute-done.10.refs_0_), channel_id=1, source_target_pairs={{0,4},{4,8},{8,12},{12,14},{14,10},{10,6},{6,2},{2,0},{1,5},{5,9},... | collective-permute-start | bytes 786440 | tf_op jit(solution)/shard_map/ppermute | solution.py:327
  60.5 1.9 %collective-permute-done.16.refs_3_ = bf16[64,2048]{1,0:T(8,128)(2,1)S(1)} collective-permute-done((bf16[64,2048]{1,0:T(8,128)(2,1)S(1)}, bf16[64,2048]{1,0:T(8,128)(2,1)S(1)}, u32[]{:S(2)}, u32[]{:S(2)}) %collective-permute-start.16) | collective-permute-done | bytes 262176 | tf_op jit(solution)/shard_map/ppermute | solution.py:331
  62.4 1.2 %collective-permute-start.17 = (bf16[64,2048]{1,0:T(8,128)(2,1)S(1)}, bf16[64,2048]{1,0:T(8,128)(2,1)S(1)}, u32[]{:S(2)}, u32[]{:S(2)}) collective-permute-start(bf16[64,2048]{1,0:T(8,128)(2,1)S(1)} %collective-permute-done.16.refs_3_), channel_id=1, source_target_pairs={{4,0},{8,4},{12,8},{14,12},{10,14},{6,10},{2,6},{0,2},{5,1},{9,5},... | collective-permute-start | bytes 786440 | tf_op jit(solution)/shard_map/ppermute | solution.py:331
  63.6 4.4 %collective-permute-done.21.refs_1_ = bf16[64,2048]{1,0:T(8,128)(2,1)S(1)} collective-permute-done((bf16[64,2048]{1,0:T(8,128)(2,1)S(1)}, bf16[64,2048]{1,0:T(8,128)(2,1)S(1)}, u32[]{:S(2)}, u32[]{:S(2)}) %collective-permute-start.21) | collective-permute-done | bytes 262176 | tf_op jit(solution)/shard_map/ppermute | solution.py:329
  68.0 1.2 %collective-permute-start.22 = (bf16[64,2048]{1,0:T(8,128)(2,1)S(1)}, bf16[64,2048]{1,0:T(8,128)(2,1)S(1)}, u32[]{:S(2)}, u32[]{:S(2)}) collective-permute-start(bf16[64,2048]{1,0:T(8,128)(2,1)S(1)} %collective-permute-done.21.refs_1_), channel_id=1, source_target_pairs={{4,0},{8,4},{12,8},{14,12},{10,14},{6,10},{2,6},{0,2},{5,1},{9,5},... | collective-permute-start | bytes 786440 | tf_op jit(solution)/shard_map/ppermute | solution.py:329
  69.2 0.8 collective-permute-start.25
  70.0 0.1 collective-permute-done.11.refs_0_
  70.2 1.6 %collective-permute-start.12 = (bf16[64,2048]{1,0:T(8,128)(2,1)S(1)}, bf16[64,2048]{1,0:T(8,128)(2,1)S(1)}, u32[]{:S(2)}, u32[]{:S(2)}) collective-permute-start(bf16[64,2048]{1,0:T(8,128)(2,1)S(1)} %collective-permute-done.11.refs_0_), channel_id=1, source_target_pairs={{0,4},{4,8},{8,12},{12,14},{14,10},{10,6},{6,2},{2,0},{1,5},{5,9},... | collective-permute-start | bytes 786440 | tf_op jit(solution)/shard_map/ppermute | solution.py:327
  71.7 1.9 %collective-permute-done.17.refs_3_ = bf16[64,2048]{1,0:T(8,128)(2,1)S(1)} collective-permute-done((bf16[64,2048]{1,0:T(8,128)(2,1)S(1)}, bf16[64,2048]{1,0:T(8,128)(2,1)S(1)}, u32[]{:S(2)}, u32[]{:S(2)}) %collective-permute-start.17) | collective-permute-done | bytes 262176 | tf_op jit(solution)/shard_map/ppermute | solution.py:331
  73.6 1.2 %collective-permute-start.18 = (bf16[64,2048]{1,0:T(8,128)(2,1)S(1)}, bf16[64,2048]{1,0:T(8,128)(2,1)S(1)}, u32[]{:S(2)}, u32[]{:S(2)}) collective-permute-start(bf16[64,2048]{1,0:T(8,128)(2,1)S(1)} %collective-permute-done.17.refs_3_), channel_id=1, source_target_pairs={{4,0},{8,4},{12,8},{14,12},{10,14},{6,10},{2,6},{0,2},{5,1},{9,5},... | collective-permute-start | bytes 786440 | tf_op jit(solution)/shard_map/ppermute | solution.py:331
  74.9 2.0 %project.5.refs_6_ = bf16[8,1,64,896]{3,2,1,0:T(8,128)(2,1)} custom-call(bf16[64,2048]{1,0:T(8,128)(2,1)S(1)} %attend.2.refs_0_, bf16[64,2048]{1,0:T(8,128)(2,1)S(1)} %attend.3.refs_1_, bf16[2048,896]{1,0:T(8,128)(2,1)S(1)} %copy-done, bf16[2048,896]{1,0:T(8,128)(2,1)S(1)} %collective-permute-done.19.refs_3_.refs_5_), custom_call_target="tpu_custom_call" | custom-call | flops 469762048 | bytes 7340032 | tf_op jit(solution)/shard_map/project/pallas_call | solution.py:254
  76.9 2.0 %project.6.refs_6_ = bf16[8,1,64,896]{3,2,1,0:T(8,128)(2,1)} custom-call(bf16[64,2048]{1,0:T(8,128)(2,1)S(1)} %collective-permute-done.9.refs_0_, bf16[64,2048]{1,0:T(8,128)(2,1)S(1)} %collective-permute-done.20.refs_1_, bf16[64,2048]{1,0:T(8,128)(2,1)S(1)} %collective-permute-done.23.refs_2_, ...), custom_call_target="tpu_custom_call", output_to_operand_aliasing={{}: (6, {})} | custom-call | flops 939524096 | bytes 7340032 | tf_op jit(solution)/shard_map/project/pallas_call | solution.py:254
  78.9 2.0 %project.7.refs_6_ = bf16[8,1,64,896]{3,2,1,0:T(8,128)(2,1)} custom-call(bf16[64,2048]{1,0:T(8,128)(2,1)S(1)} %collective-permute-done.10.refs_0_, bf16[64,2048]{1,0:T(8,128)(2,1)S(1)} %collective-permute-done.21.refs_1_, bf16[64,2048]{1,0:T(8,128)(2,1)S(1)} %collective-permute-done.24.refs_2_, ...), custom_call_target="tpu_custom_call", output_to_operand_aliasing={{}: (6, {})} | custom-call | flops 939524096 | bytes 7340032 | tf_op jit(solution)/shard_map/project/pallas_call | solution.py:254
  80.8 0.0 collective-permute-done.22.refs_1_
  80.9 2.0 %project.8.refs_4_ = bf16[8,1,64,896]{3,2,1,0:T(8,128)(2,1)} custom-call(bf16[64,2048]{1,0:T(8,128)(2,1)S(1)} %collective-permute-done.11.refs_0_, bf16[64,2048]{1,0:T(8,128)(2,1)S(1)} %collective-permute-done.22.refs_1_, bf16[64,2048]{1,0:T(8,128)(2,1)S(1)} %collective-permute-done.25.refs_2_, ...), custom_call_target="tpu_custom_call", output_to_operand_aliasing={{}: (6, {})} | custom-call | flops 939524096 | bytes 7340032 | tf_op jit(solution)/shard_map/project/pallas_call | solution.py:254
  82.8 1.3 %collective-permute-done.18.refs_1_ = bf16[64,2048]{1,0:T(8,128)(2,1)S(1)} collective-permute-done((bf16[64,2048]{1,0:T(8,128)(2,1)S(1)}, bf16[64,2048]{1,0:T(8,128)(2,1)S(1)}, u32[]{:S(2)}, u32[]{:S(2)}) %collective-permute-start.18) | collective-permute-done | bytes 262176 | tf_op jit(solution)/shard_map/ppermute | solution.py:331
  84.1 2.0 %project.9 = bf16[8,1,64,896]{3,2,1,0:T(8,128)(2,1)} custom-call(bf16[64,2048]{1,0:T(8,128)(2,1)S(1)} %collective-permute-done.12.refs_0_, bf16[64,2048]{1,0:T(8,128)(2,1)S(1)} %collective-permute-done.18.refs_1_, bf16[2048,896]{1,0:T(8,128)(2,1)S(1)} %copy-done, ...), custom_call_target="tpu_custom_call", output_to_operand_aliasing={{}: (4, {})} | custom-call | flops 469762048 | bytes 7340032 | tf_op jit(solution)/shard_map/project/pallas_call | solution.py:254
  (19 shorter events, 0.1 us)
Async XLA Ops:
  0.0 74.9 %collective-permute-start.19 = (bf16[2048,896]{1,0:T(8,128)(2,1)}, bf16[2048,896]{1,0:T(8,128)(2,1)S(1)}, u32[]{:S(2)}, u32[]{:S(2)}) collective-permute-start(bf16[2048,896]{1,0:T(8,128)(2,1)} %refs_2_.3), channel_id=1, source_target_pairs={{0,1},{1,0},{2,3},{3,2},{4,5},{5,4},{6,7},{7,6},{8,9},{9,8},{10,11... | collective-permute-start | bytes 11010056 | tf_op jit(solution)/shard_map/ppermute | solution.py:306
  0.5 36.5 %collective-permute-start.13 = (bf16[16,128,512]{2,1,0:T(8,128)(2,1)}, bf16[16,128,512]{2,1,0:T(8,128)(2,1)S(1)}, u32[]{:S(2)}, u32[]{:S(2)}) collective-permute-start(bf16[16,128,512]{2,1,0:T(8,128)(2,1)} %key_up.1), channel_id=1, source_target_pairs={{0,1},{1,0},{2,3},{3,2},{4,5},{5,4},{6,7},{7,6},{8,9},{9,8},{10,11... | collective-permute-start | bytes 6291464 | tf_op jit(solution)/shard_map/ppermute | solution.py:304
  0.5 37.4 %collective-permute-start.14 = (bf16[16,512,128]{2,1,0:T(8,128)(2,1)}, bf16[16,512,128]{2,1,0:T(8,128)(2,1)S(1)}, u32[]{:S(2)}, u32[]{:S(2)}) collective-permute-start(bf16[16,512,128]{2,1,0:T(8,128)(2,1)} %value_up.1), channel_id=1, source_target_pairs={{0,1},{1,0},{2,3},{3,2},{4,5},{5,4},{6,7},{7,6},{8,9},{9,8},{10,11... | collective-permute-start | bytes 6291464 | tf_op jit(solution)/shard_map/ppermute | solution.py:305
  1.0 0.9 %copy-start.5 = (bf16[128,576]{0,1:T(8,128)(2,1)S(1)}, bf16[128,576]{0,1:T(8,128)(2,1)}, u32[]{:S(2)}) copy-start(bf16[128,576]{0,1:T(8,128)(2,1)} %param.7) | copy-start | bytes 442372
  1.9 0.7 copy-start.6
  2.9 8.6 %collective-permute-start.1 = (bf16[64,640]{1,0:T(8,128)(2,1)S(1)}, bf16[64,640]{1,0:T(8,128)(2,1)S(1)}, u32[]{:S(2)}, u32[]{:S(2)}) collective-permute-start(bf16[64,640]{1,0:T(8,128)(2,1)S(1)} %get-tuple-element.8), channel_id=1, source_target_pairs={{8,0},{10,2},{12,4},{14,6},{0,8},{2,10},{4,12},{6,14},{9,1},{11,3}... | collective-permute-start | bytes 245768 | tf_op jit(solution)/shard_map/ppermute | solution.py:295
  6.5 6.5 %collective-permute-start = (bf16[64,640]{1,0:T(8,128)(2,1)S(1)}, bf16[64,640]{1,0:T(8,128)(2,1)S(1)}, u32[]{:S(2)}, u32[]{:S(2)}) collective-permute-start(bf16[64,640]{1,0:T(8,128)(2,1)S(1)} %get-tuple-element.8), channel_id=1, source_target_pairs={{4,0},{6,2},{0,4},{2,6},{12,8},{14,10},{8,12},{10,14},{5,1},{7,3},... | collective-permute-start | bytes 245768 | tf_op jit(solution)/shard_map/ppermute | solution.py:295
  11.5 6.5 %collective-permute-start.3 = (bf16[64,640]{1,0:T(8,128)(2,1)S(1)}, bf16[64,640]{1,0:T(8,128)(2,1)S(1)}, u32[]{:S(2)}, u32[]{:S(2)}) collective-permute-start(bf16[64,640]{1,0:T(8,128)(2,1)S(1)} %get-tuple-element.8), channel_id=1, source_target_pairs={{2,0},{0,2},{6,4},{4,6},{10,8},{8,10},{14,12},{12,14},{3,1},{1,3},... | collective-permute-start | bytes 245768 | tf_op jit(solution)/shard_map/ppermute | solution.py:295
  13.1 4.4 %collective-permute-start.2 = (bf16[64,640]{1,0:T(8,128)(2,1)S(1)}, bf16[64,640]{1,0:T(8,128)(2,1)S(1)}, u32[]{:S(2)}, u32[]{:S(2)}) collective-permute-start(bf16[64,640]{1,0:T(8,128)(2,1)S(1)} %collective-permute-done.1), channel_id=1, source_target_pairs={{4,0},{6,2},{0,4},{2,6},{12,8},{14,10},{8,12},{10,14},{5,1},{7,3},... | collective-permute-start | bytes 245768 | tf_op jit(solution)/shard_map/ppermute | solution.py:295
  17.5 5.3 %collective-permute-start.5 = (bf16[64,640]{1,0:T(8,128)(2,1)S(1)}, bf16[64,640]{1,0:T(8,128)(2,1)S(1)}, u32[]{:S(2)}, u32[]{:S(2)}) collective-permute-start(bf16[64,640]{1,0:T(8,128)(2,1)S(1)} %collective-permute-done.1), channel_id=1, source_target_pairs={{2,0},{0,2},{6,4},{4,6},{10,8},{8,10},{14,12},{12,14},{3,1},{1,3},... | collective-permute-start | bytes 245768 | tf_op jit(solution)/shard_map/ppermute | solution.py:295
  18.0 4.8 %collective-permute-start.4 = (bf16[64,640]{1,0:T(8,128)(2,1)S(1)}, bf16[64,640]{1,0:T(8,128)(2,1)S(1)}, u32[]{:S(2)}, u32[]{:S(2)}) collective-permute-start(bf16[64,640]{1,0:T(8,128)(2,1)S(1)} %collective-permute-done), channel_id=1, source_target_pairs={{2,0},{0,2},{6,4},{4,6},{10,8},{8,10},{14,12},{12,14},{3,1},{1,3},... | collective-permute-start | bytes 245768 | tf_op jit(solution)/shard_map/ppermute | solution.py:295
  22.8 8.7 %collective-permute-start.7 = (bf16[256,640]{1,0:T(8,128)(2,1)S(1)}, bf16[256,640]{1,0:T(8,128)(2,1)S(1)}, u32[]{:S(2)}, u32[]{:S(2)}) collective-permute-start(bf16[256,640]{1,0:T(8,128)(2,1)S(1)} %constant_dynamic-update-slice_fusion.rest_1_), channel_id=1, source_target_pairs={{0,1},{1,0},{2,3},{3,2},{4,5},{5,4},{6,7},{7,6},{8,9},{9,8},{10,11... | collective-permute-start | bytes 983048 | tf_op jit(solution)/shard_map/ppermute | solution.py:300
  22.8 4.9 %collective-permute-start.6 = (bf16[64,640]{1,0:T(8,128)(2,1)S(1)}, bf16[64,640]{1,0:T(8,128)(2,1)S(1)}, u32[]{:S(2)}, u32[]{:S(2)}) collective-permute-start(bf16[64,640]{1,0:T(8,128)(2,1)S(1)} %collective-permute-done.2), channel_id=1, source_target_pairs={{2,0},{0,2},{6,4},{4,6},{10,8},{8,10},{14,12},{12,14},{3,1},{1,3},... | collective-permute-start | bytes 245768 | tf_op jit(solution)/shard_map/ppermute | solution.py:295
  27.8 3.8 %collective-permute-start.8 = (bf16[192,640]{1,0:T(8,128)(2,1)S(1)}, bf16[192,640]{1,0:T(8,128)(2,1)S(1)}, u32[]{:S(2)}, u32[]{:S(2)}) collective-permute-start(bf16[192,640]{1,0:T(8,128)(2,1)S(1)} %constant_dynamic-update-slice_fusion.4.rest_2_), channel_id=1, source_target_pairs={{0,1},{1,0},{2,3},{3,2},{4,5},{5,4},{6,7},{7,6},{8,9},{9,8},{10,11... | collective-permute-start | bytes 737288 | tf_op jit(solution)/shard_map/ppermute | solution.py:301
  27.9 1.1 %copy-start.1 = (bf16[64,6144]{1,0:T(8,128)(2,1)S(1)}, bf16[64,6144]{1,0:T(8,128)(2,1)}, u32[]{:S(2)}) copy-start(bf16[64,6144]{1,0:T(8,128)(2,1)} %queries.3) | copy-start | bytes 2359300
  29.0 1.6 %copy-start.3 = (bf16[16,128,512]{2,1,0:T(8,128)(2,1)S(1)}, bf16[16,128,512]{2,1,0:T(8,128)(2,1)}, u32[]{:S(2)}) copy-start(bf16[16,128,512]{2,1,0:T(8,128)(2,1)} %key_up.1) | copy-start | bytes 6291460
  30.6 1.6 %copy-start.4 = (bf16[16,512,128]{2,1,0:T(8,128)(2,1)S(1)}, bf16[16,512,128]{2,1,0:T(8,128)(2,1)}, u32[]{:S(2)}) copy-start(bf16[16,512,128]{2,1,0:T(8,128)(2,1)} %value_up.1) | copy-start | bytes 6291460
  32.2 4.8 %copy-start.2 = (bf16[64,6144]{1,0:T(8,128)(2,1)S(1)}, bf16[64,6144]{1,0:T(8,128)(2,1)}, u32[]{:S(2)}) copy-start(bf16[64,6144]{1,0:T(8,128)(2,1)} %queries.3) | copy-start | bytes 2359300
  36.1 9.1 %collective-permute-start.9 = (bf16[64,2048]{1,0:T(8,128)(2,1)S(1)}, bf16[64,2048]{1,0:T(8,128)(2,1)S(1)}, u32[]{:S(2)}, u32[]{:S(2)}) collective-permute-start(bf16[64,2048]{1,0:T(8,128)(2,1)S(1)} %attend.2.refs_0_), channel_id=1, source_target_pairs={{0,4},{4,8},{8,12},{12,14},{14,10},{10,6},{6,2},{2,0},{1,5},{5,9},... | collective-permute-start | bytes 786440 | tf_op jit(solution)/shard_map/ppermute | solution.py:327
  37.9 36.9 %copy-start = (bf16[2048,896]{1,0:T(8,128)(2,1)S(1)}, bf16[2048,896]{1,0:T(8,128)(2,1)}, u32[]{:S(2)}) copy-start(bf16[2048,896]{1,0:T(8,128)(2,1)} %refs_2_.3) | copy-start | bytes 11010052
  41.9 9.2 %collective-permute-start.15 = (bf16[64,2048]{1,0:T(8,128)(2,1)S(1)}, bf16[64,2048]{1,0:T(8,128)(2,1)S(1)}, u32[]{:S(2)}, u32[]{:S(2)}) collective-permute-start(bf16[64,2048]{1,0:T(8,128)(2,1)S(1)} %attend.3.refs_1_), channel_id=1, source_target_pairs={{4,0},{8,4},{12,8},{14,12},{10,14},{6,10},{2,6},{0,2},{5,1},{9,5},... | collective-permute-start | bytes 786440 | tf_op jit(solution)/shard_map/ppermute | solution.py:331
  43.2 13.6 %collective-permute-start.20 = (bf16[64,2048]{1,0:T(8,128)(2,1)S(1)}, bf16[64,2048]{1,0:T(8,128)(2,1)S(1)}, u32[]{:S(2)}, u32[]{:S(2)}) collective-permute-start(bf16[64,2048]{1,0:T(8,128)(2,1)S(1)} %attend.2.refs_0_), channel_id=1, source_target_pairs={{4,0},{8,4},{12,8},{14,12},{10,14},{6,10},{2,6},{0,2},{5,1},{9,5},... | collective-permute-start | bytes 786440 | tf_op jit(solution)/shard_map/ppermute | solution.py:329
  44.4 13.6 %collective-permute-start.23 = (bf16[64,2048]{1,0:T(8,128)(2,1)S(1)}, bf16[64,2048]{1,0:T(8,128)(2,1)S(1)}, u32[]{:S(2)}, u32[]{:S(2)}) collective-permute-start(bf16[64,2048]{1,0:T(8,128)(2,1)S(1)} %attend.3.refs_1_), channel_id=1, source_target_pairs={{0,4},{4,8},{8,12},{12,14},{14,10},{10,6},{6,2},{2,0},{1,5},{5,9},... | collective-permute-start | bytes 786440 | tf_op jit(solution)/shard_map/ppermute | solution.py:330
  45.2 13.6 %collective-permute-start.10 = (bf16[64,2048]{1,0:T(8,128)(2,1)S(1)}, bf16[64,2048]{1,0:T(8,128)(2,1)S(1)}, u32[]{:S(2)}, u32[]{:S(2)}) collective-permute-start(bf16[64,2048]{1,0:T(8,128)(2,1)S(1)} %collective-permute-done.9.refs_0_), channel_id=1, source_target_pairs={{0,4},{4,8},{8,12},{12,14},{14,10},{10,6},{6,2},{2,0},{1,5},{5,9},... | collective-permute-start | bytes 786440 | tf_op jit(solution)/shard_map/ppermute | solution.py:327
  51.2 11.2 %collective-permute-start.16 = (bf16[64,2048]{1,0:T(8,128)(2,1)S(1)}, bf16[64,2048]{1,0:T(8,128)(2,1)S(1)}, u32[]{:S(2)}, u32[]{:S(2)}) collective-permute-start(bf16[64,2048]{1,0:T(8,128)(2,1)S(1)} %collective-permute-done.15.refs_3_), channel_id=1, source_target_pairs={{4,0},{8,4},{12,8},{14,12},{10,14},{6,10},{2,6},{0,2},{5,1},{9,5},... | collective-permute-start | bytes 786440 | tf_op jit(solution)/shard_map/ppermute | solution.py:331
  56.8 11.2 %collective-permute-start.21 = (bf16[64,2048]{1,0:T(8,128)(2,1)S(1)}, bf16[64,2048]{1,0:T(8,128)(2,1)S(1)}, u32[]{:S(2)}, u32[]{:S(2)}) collective-permute-start(bf16[64,2048]{1,0:T(8,128)(2,1)S(1)} %collective-permute-done.20.refs_1_), channel_id=1, source_target_pairs={{4,0},{8,4},{12,8},{14,12},{10,14},{6,10},{2,6},{0,2},{5,1},{9,5},... | collective-permute-start | bytes 786440 | tf_op jit(solution)/shard_map/ppermute | solution.py:329
  58.0 11.2 %collective-permute-start.24 = (bf16[64,2048]{1,0:T(8,128)(2,1)S(1)}, bf16[64,2048]{1,0:T(8,128)(2,1)S(1)}, u32[]{:S(2)}, u32[]{:S(2)}) collective-permute-start(bf16[64,2048]{1,0:T(8,128)(2,1)S(1)} %collective-permute-done.23.refs_2_), channel_id=1, source_target_pairs={{0,4},{4,8},{8,12},{12,14},{14,10},{10,6},{6,2},{2,0},{1,5},{5,9},... | collective-permute-start | bytes 786440 | tf_op jit(solution)/shard_map/ppermute | solution.py:330
  58.8 11.3 %collective-permute-start.11 = (bf16[64,2048]{1,0:T(8,128)(2,1)S(1)}, bf16[64,2048]{1,0:T(8,128)(2,1)S(1)}, u32[]{:S(2)}, u32[]{:S(2)}) collective-permute-start(bf16[64,2048]{1,0:T(8,128)(2,1)S(1)} %collective-permute-done.10.refs_0_), channel_id=1, source_target_pairs={{0,4},{4,8},{8,12},{12,14},{14,10},{10,6},{6,2},{2,0},{1,5},{5,9},... | collective-permute-start | bytes 786440 | tf_op jit(solution)/shard_map/ppermute | solution.py:327
  62.4 11.2 %collective-permute-start.17 = (bf16[64,2048]{1,0:T(8,128)(2,1)S(1)}, bf16[64,2048]{1,0:T(8,128)(2,1)S(1)}, u32[]{:S(2)}, u32[]{:S(2)}) collective-permute-start(bf16[64,2048]{1,0:T(8,128)(2,1)S(1)} %collective-permute-done.16.refs_3_), channel_id=1, source_target_pairs={{4,0},{8,4},{12,8},{14,12},{10,14},{6,10},{2,6},{0,2},{5,1},{9,5},... | collective-permute-start | bytes 786440 | tf_op jit(solution)/shard_map/ppermute | solution.py:331
  68.0 12.8 %collective-permute-start.22 = (bf16[64,2048]{1,0:T(8,128)(2,1)S(1)}, bf16[64,2048]{1,0:T(8,128)(2,1)S(1)}, u32[]{:S(2)}, u32[]{:S(2)}) collective-permute-start(bf16[64,2048]{1,0:T(8,128)(2,1)S(1)} %collective-permute-done.21.refs_1_), channel_id=1, source_target_pairs={{4,0},{8,4},{12,8},{14,12},{10,14},{6,10},{2,6},{0,2},{5,1},{9,5},... | collective-permute-start | bytes 786440 | tf_op jit(solution)/shard_map/ppermute | solution.py:329
  69.2 11.6 %collective-permute-start.25 = (bf16[64,2048]{1,0:T(8,128)(2,1)S(1)}, bf16[64,2048]{1,0:T(8,128)(2,1)S(1)}, u32[]{:S(2)}, u32[]{:S(2)}) collective-permute-start(bf16[64,2048]{1,0:T(8,128)(2,1)S(1)} %collective-permute-done.24.refs_2_), channel_id=1, source_target_pairs={{0,4},{4,8},{8,12},{12,14},{14,10},{10,6},{6,2},{2,0},{1,5},{5,9},... | collective-permute-start | bytes 786440 | tf_op jit(solution)/shard_map/ppermute | solution.py:330
  70.2 12.7 %collective-permute-start.12 = (bf16[64,2048]{1,0:T(8,128)(2,1)S(1)}, bf16[64,2048]{1,0:T(8,128)(2,1)S(1)}, u32[]{:S(2)}, u32[]{:S(2)}) collective-permute-start(bf16[64,2048]{1,0:T(8,128)(2,1)S(1)} %collective-permute-done.11.refs_0_), channel_id=1, source_target_pairs={{0,4},{4,8},{8,12},{12,14},{14,10},{10,6},{6,2},{2,0},{1,5},{5,9},... | collective-permute-start | bytes 786440 | tf_op jit(solution)/shard_map/ppermute | solution.py:327
  73.6 10.5 %collective-permute-start.18 = (bf16[64,2048]{1,0:T(8,128)(2,1)S(1)}, bf16[64,2048]{1,0:T(8,128)(2,1)S(1)}, u32[]{:S(2)}, u32[]{:S(2)}) collective-permute-start(bf16[64,2048]{1,0:T(8,128)(2,1)S(1)} %collective-permute-done.17.refs_3_), channel_id=1, source_target_pairs={{4,0},{8,4},{12,8},{14,12},{10,14},{6,10},{2,6},{0,2},{5,1},{9,5},... | collective-permute-start | bytes 786440 | tf_op jit(solution)/shard_map/ppermute | solution.py:331

commit v2 on v1

--- a/solution.py
+++ b/solution.py
@@ -184,17 +184,17 @@
         score = later
 
 
-def attend(query_rows, value_up, keys, rows):
-    heads = value_up.shape[0]
+def attend(query_rows, value_up, keys, rows, blocks):
     step = 8
-    steps = heads // step
+    first, count = blocks
+    heads = count * step
     key_total = sum(key.shape[0] for key in keys)
     return pl.pallas_call(
         functools.partial(attend_kernel, 4 * rows, len(keys)),
-        grid=(steps,),
+        grid=(count,),
         in_specs=[
-            pl.BlockSpec((step * rows, WIDE), lambda i: (i, 0)),
-            pl.BlockSpec((step, KV, VD), lambda i: (i, 0, 0)),
+            pl.BlockSpec((step * rows, WIDE), lambda i: (first + i, 0)),
+            pl.BlockSpec((step, KV, VD), lambda i: (first + i, 0, 0)),
         ]
         + [pl.BlockSpec(key.shape, lambda i: (0, 0)) for key in keys],
         out_specs=pl.BlockSpec((rows, step * VD), lambda i: (0, i)),
@@ -212,18 +212,25 @@
     )(query_rows, value_up, *keys)
 
 
-def project_kernel(count, offsets, *refs):
+def project_kernel(count, offsets, chunks, *refs):
     pieces = len(offsets)
-    firsts, seconds = refs[:pieces], refs[pieces : 2 * pieces]
-    own_weight, other_weight = refs[2 * pieces : 2 * pieces + 2]
+    parts = refs[: pieces * chunks]
+    own_weight, other_weight = refs[pieces * chunks : pieces * chunks + 2]
     out, held, sems = refs[-3:]
-    rows = firsts[0].shape[0]
-
-    def stack(parts):
-        return jnp.concatenate([part[...] for part in parts], 0) if pieces > 1 else parts[0][...]
-
-    product = jnp.dot(stack(firsts), own_weight[...], preferred_element_type=jnp.float32)
-    product += jnp.dot(stack(seconds), other_weight[...], preferred_element_type=jnp.float32)
+    rows = parts[0].shape[0]
+    product = None
+    start = 0
+    for chunk in range(chunks):
+        stack = [parts[piece * chunks + chunk][...] for piece in range(pieces)]
+        stack = jnp.concatenate(stack, 0) if pieces > 1 else stack[0]
+        depth = stack.shape[1]
+        if start < own_weight.shape[0]:
+            weight = own_weight[start : start + depth, :]
+        else:
+            weight = other_weight[...]
+        start += depth
+        part = jnp.dot(stack, weight, preferred_element_type=jnp.float32)
+        product = part if product is None else product + part
     held[...] = product.astype(jnp.bfloat16)
     block = lax.axis_index("seq")
     half = block // 2
@@ -240,35 +247,53 @@
         copy.wait()
 
 
-def project(count, offsets, firsts, seconds, own_weight, other_weight, mixed):
-    rows, depth = firsts[0].shape
-    columns = own_weight.shape[1]
-    pieces = len(offsets)
-    operands = [*firsts, *seconds, own_weight, other_weight]
+def project(count, pieces, own_weight, other_weight, mixed):
+    offsets = [offset for offset, _ in pieces]
+    operands = [part for _, parts in pieces for part in parts]
+    chunks = len(operands) // len(pieces)
+    rows = operands[0].shape[0]
+    depth, columns = own_weight.shape
+    operands += [own_weight, other_weight]
     aliases = {}
+    vmem = pl.BlockSpec(memory_space=pltpu.VMEM)
+    anywhere = pl.BlockSpec(memory_space=pl.ANY)
+    specs = [vmem] * len(operands)
     if mixed is not None:
         aliases = {len(operands): 0}
         operands.append(mixed)
-    vmem = pl.BlockSpec(memory_space=pltpu.VMEM)
-    anywhere = pl.BlockSpec(memory_space=pl.ANY)
+        specs.append(anywhere)
     return pl.pallas_call(
-        functools.partial(project_kernel, count, offsets),
-        in_specs=[vmem] * (2 * pieces + 2) + [anywhere] * len(aliases),
+        functools.partial(project_kernel, count, offsets, chunks),
+        in_specs=specs,
         out_specs=anywhere,
         out_shape=jax.ShapeDtypeStruct((count, 1, rows, columns), jnp.bfloat16),
         scratch_shapes=[
-            pltpu.VMEM((pieces * rows, columns), jnp.bfloat16),
-            pltpu.SemaphoreType.DMA((pieces,)),
+            pltpu.VMEM((len(pieces) * rows, columns), jnp.bfloat16),
+            pltpu.SemaphoreType.DMA((len(pieces),)),
         ],
         input_output_aliases=aliases,
         compiler_params=pltpu.CompilerParams(vmem_limit_bytes=8 << 20),
         cost_estimate=pl.CostEstimate(
-            flops=4 * pieces * rows * depth * columns,
+            flops=4 * len(pieces) * rows * depth * columns,
             bytes_accessed=4 * depth * columns,
             transcendentals=0,
         ),
         name="project",
     )(*operands)
+
+
+def touch_kernel(value, out):
+    out[...] = jnp.zeros_like(out)
+
+
+def touch(value):
+    return pl.pallas_call(
+        touch_kernel,
+        in_specs=[pl.BlockSpec(memory_space=pltpu.VMEM)],
+        out_shape=jax.ShapeDtypeStruct((8, 128), jnp.float32),
+        compiler_params=pltpu.CompilerParams(vmem_limit_bytes=8 << 20, has_side_effects=True),
+        name="touch",
+    )(value)
 
 
 def gather_plan(count):
@@ -282,6 +307,26 @@
     return moves
 
 
+def ring_order(steps):
+    right = ["a1", "b1", "a2", "c1"]
+    left = ["a1", "b1", "a2", "c1"]
+    for step in range(2, steps - 1):
+        right += [f"b{step}", f"c{step}", f"a{step + 1}"]
+        left += [f"b{step}", f"a{step + 1}", f"c{step}"]
+    step = steps - 1
+    right += [f"c{step}", f"b{step}", f"c{steps}"]
+    left += [f"b{step}", f"a{steps}", f"c{step}", f"b{steps}"]
+    names = []
+    for i in range(len(left)):
+        names += ["r" + right[i]] if i < len(right) else []
+        names.append("l" + left[i])
+    return names
+
+
+def send(value, axis, pairs):
+    return lax.ppermute(value, axis, pairs)
+
+
 def layer(queries, latents, latent_gain, key_up, value_up, out_weight):
     seq_count = lax.axis_size("seq")
     head_count = lax.axis_size("head")
@@ -292,48 +337,53 @@
     own_keys, half_keys = prepare(latents.T, latent_gain.reshape(1, KV))
     slots = {0: half_keys}
     for slot, bit in gather_plan(seq_count):
-        slots[slot | bit] = lax.ppermute(slots[slot], "seq", [(d ^ bit, d) for d in everyone])
+        slots[slot | bit] = send(slots[slot], "seq", [(d ^ bit, d) for d in everyone])
     near = [m for m in range(1, seq_count) if m % 2 == 0] + [1]
     far = [m for m in range(2, seq_count) if m % 2 == 1]
     near_keys = jnp.concatenate([slots[m] for m in near], 0)
     far_keys = jnp.concatenate([slots[m] for m in far], 0)
-    near_swap = lax.ppermute(near_keys, "head", swap_pairs)
-    far_swap = lax.ppermute(far_keys, "head", swap_pairs)
+    near_swap = send(near_keys, "head", swap_pairs)
+    far_swap = send(far_keys, "head", swap_pairs)
     keys = [own_keys, near_keys, far_keys, near_swap, far_swap]
 
-    key_other = lax.ppermute(key_up, "head", swap_pairs)
-    value_other = lax.ppermute(value_up, "head", swap_pairs)
-    weight_other = lax.ppermute(out_weight, "head", swap_pairs)
+    key_other = send(key_up, "head", swap_pairs)
+    value_other = send(value_up, "head", swap_pairs)
+    weight_other = send(out_weight, "head", swap_pairs)
     rows_a = lift(queries, key_up, False)
-    heads_a = attend(rows_a, value_up, keys, rows)
+    touch(value_up)
     rows_b = lift(queries, key_other, True)
-    heads_b = attend(rows_b, value_other, keys, rows)
+    blocks = key_up.shape[0] // 8
+    first = blocks // 2
+    chunks = {}
+    chunks["a"] = attend(rows_a, value_up, keys, rows, (0, first))
+    chunks["b"] = attend(rows_a, value_up, keys, rows, (first, blocks - first))
+    chunks["c"] = attend(rows_b, value_other, keys, rows, (0, blocks))
 
     order = list(range(0, seq_count, 2)) + list(range(seq_count - 1, 0, -2))
     right = [(order[i], order[(i + 1) % seq_count]) for i in everyone]
     left = [(b, a) for a, b in right]
     steps = seq_count // 2
+    held = {way + chunk + "0": value for chunk, value in chunks.items() for way in "rl"}
+    for step in range(1, steps + 1):
+        for name in ring_order(steps):
+            if name[2:] == str(step):
+                value = held[name[:2] + str(step - 1)]
+                held[name] = send(value, "seq", right if name[0] == "r" else left)
 
     def put(mixed, *pieces):
-        firsts, seconds, offsets = zip(*pieces)
-        return project(
-            seq_count, offsets, firsts, seconds, out_weight, weight_other, mixed
-        )
-
-    right_a, right_b, left_a, left_b = heads_a, heads_b, heads_a, heads_b
-    mixed = put(None, (heads_a, heads_b, 0))
-    for step in range(1, steps + 1):
-        last = step == steps
-        right_a = lax.ppermute(right_a, "seq", right)
-        if not last:
-            left_a = lax.ppermute(left_a, "seq", left)
-            right_b = lax.ppermute(right_b, "seq", right)
-        left_b = lax.ppermute(left_b, "seq", left)
-        if last:
-            mixed = put(mixed, (right_a, left_b, step))
-        else:
-            mixed = put(mixed, (right_a, right_b, -step), (left_a, left_b, step))
-    return mixed
+        return project(seq_count, pieces, out_weight, weight_other, mixed)
+
+    def from_way(way, step):
+        return [held[f"{way}{chunk}{step}"] for chunk in "abc"]
+
+    mixed = put(None, (0, from_way("r", 0)))
+    for step in range(1, steps - 1):
+        mixed = put(mixed, (-step, from_way("r", step)), (step, from_way("l", step)))
+    step = steps - 1
+    mixed = put(mixed, (-step, from_way("r", step)))
+    mixed = put(mixed, (step, from_way("l", step)))
+    final = [held[f"la{steps}"], held[f"lb{steps}"], held[f"rc{steps}"]]
+    return put(mixed, (steps, final))
 
 
 def solution(mesh):

time: 86.5 us -> 87.3 us (level)
  starting transfers between devices: 27.8 us -> 36 us
  waiting for transfers between devices: 33.1 us -> 25.3 us
  Pallas kernels: 20 us -> 22.6 us
  local copies, waits for them, and re-layouts: 5.03 us -> 2.83 us
    ppermute x26 -> x33, starting transfers between devices: 27.8 us -> 36 us  [send(): return lax.ppermute(value, axis, pairs)]
    ppermute x26 -> x33, waiting for transfers between devices: 33.1 us -> 25.3 us  [send(): return lax.ppermute(value, axis, pairs)]
    pallas_call x5 -> x7, Pallas kernels: 9.92 us -> 12.6 us  [the longest x6 12 us: project(): pl.pallas_call(functools.partial(project_kernel, count, offsets, chunks),...]
    unnamed x19, local copies, waits for them, and re-layouts: 5 us -> 2.8 us
    pallas_call x2 -> x3, Pallas kernels: 7.9 us -> 7.87 us  [attend(): pl.pallas_call(functools.partial(attend_kernel, 4 * rows, len(keys)), gri...]
  transfers between devices with their start and end apart: 26 -> 33, of which waited for: 11 -> 11; matrix products, arithmetic and copies ran while one was open for 0% -> 0% of each run, Pallas kernels for 21% -> 24%
where the time goes in v2:
time: 87.3 us; the launch traced here: 87.1 us
  starting transfers between devices  36 us (41%)
  waiting for transfers between devices  25.3 us (29%)
  Pallas kernels  22.6 us (26%)
  local copies, waits for them, and re-layouts  2.83 us (3%)
    ppermute x33, starting transfers between devices, send(): return lax.ppermute(value, axis, pairs)  36 us
    ppermute x33, waiting for transfers between devices, send(): return lax.ppermute(value, axis, pairs)  25.3 us
    pallas_call x6, Pallas kernels, project(): pl.pallas_call(functools.partial(project_kernel, count, offsets, chunks),...  12 us
    pallas_call x3, Pallas kernels, attend(): pl.pallas_call(functools.partial(attend_kernel, 4 * rows, len(keys)), gri...  7.87 us
    unnamed x19, local copies, waits for them, and re-layouts  2.8 us
    pallas_call x2, Pallas kernels, lift(): pl.pallas_call(lift_kernel, grid=(steps,), in_specs=[pl.BlockSpec((rows,...  1.88 us
  transfers between devices with their start and end apart: 33, of which 11 were waited for; matrix products, arithmetic and copies ran while one was open for 0% of the time, Pallas kernels for 24%

profile of v2, /device:TPU:0, one launch (start us, length us, event | category | flops | bytes accessed | tf_op | source)
XLA Modules:
  0.0 87.1 jit_solution(4421466997322017906)
XLA Ops:
  0.0 0.5 collective-permute-start.23
  0.5 0.0 collective-permute-start.17
  0.5 0.5 collective-permute-start.18
  1.0 0.9 %copy-done.5 = bf16[128,576]{0,1:T(8,128)(2,1)S(1)} copy-done((bf16[128,576]{0,1:T(8,128)(2,1)S(1)}, bf16[128,576]{0,1:T(8,128)(2,1)}, u32[]{:S(2)}) %copy-start.5) | copy-done | bytes 147480
  1.9 0.7 copy-done.6
  2.6 0.3 prepare.1
  2.9 3.6 %collective-permute-start.1 = (bf16[64,640]{1,0:T(8,128)(2,1)S(1)}, bf16[64,640]{1,0:T(8,128)(2,1)S(1)}, u32[]{:S(2)}, u32[]{:S(2)}) collective-permute-start(bf16[64,640]{1,0:T(8,128)(2,1)S(1)} %get-tuple-element.8), channel_id=1, source_target_pairs={{8,0},{10,2},{12,4},{14,6},{0,8},{2,10},{4,12},{6,14},{9,1},{11,3}... | collective-permute-start | bytes 245768 | tf_op jit(solution)/shard_map/ppermute | solution.py:327
  6.5 1.6 %collective-permute-start = (bf16[64,640]{1,0:T(8,128)(2,1)S(1)}, bf16[64,640]{1,0:T(8,128)(2,1)S(1)}, u32[]{:S(2)}, u32[]{:S(2)}) collective-permute-start(bf16[64,640]{1,0:T(8,128)(2,1)S(1)} %get-tuple-element.8), channel_id=1, source_target_pairs={{4,0},{6,2},{0,4},{2,6},{12,8},{14,10},{8,12},{10,14},{5,1},{7,3},... | collective-permute-start | bytes 245768 | tf_op jit(solution)/shard_map/ppermute | solution.py:327
  8.1 3.4 %collective-permute-done.1 = bf16[64,640]{1,0:T(8,128)(2,1)S(1)} collective-permute-done((bf16[64,640]{1,0:T(8,128)(2,1)S(1)}, bf16[64,640]{1,0:T(8,128)(2,1)S(1)}, u32[]{:S(2)}, u32[]{:S(2)}) %collective-permute-start.1) | collective-permute-done | bytes 81952 | tf_op jit(solution)/shard_map/ppermute | solution.py:327
  11.5 1.6 %collective-permute-start.3 = (bf16[64,640]{1,0:T(8,128)(2,1)S(1)}, bf16[64,640]{1,0:T(8,128)(2,1)S(1)}, u32[]{:S(2)}, u32[]{:S(2)}) collective-permute-start(bf16[64,640]{1,0:T(8,128)(2,1)S(1)} %get-tuple-element.8), channel_id=1, source_target_pairs={{2,0},{0,2},{6,4},{4,6},{10,8},{8,10},{14,12},{12,14},{3,1},{1,3},... | collective-permute-start | bytes 245768 | tf_op jit(solution)/shard_map/ppermute | solution.py:327
  13.1 0.0 collective-permute-done
  13.1 0.6 collective-permute-start.2
  13.7 3.8 %collective-permute-done.2 = bf16[64,640]{1,0:T(8,128)(2,1)S(1)} collective-permute-done((bf16[64,640]{1,0:T(8,128)(2,1)S(1)}, bf16[64,640]{1,0:T(8,128)(2,1)S(1)}, u32[]{:S(2)}, u32[]{:S(2)}) %collective-permute-start.2) | collective-permute-done | bytes 81952 | tf_op jit(solution)/shard_map/ppermute | solution.py:327
  17.5 0.5 collective-permute-start.5
  18.0 0.0 collective-permute-done.3
  18.0 1.6 %collective-permute-start.4 = (bf16[64,640]{1,0:T(8,128)(2,1)S(1)}, bf16[64,640]{1,0:T(8,128)(2,1)S(1)}, u32[]{:S(2)}, u32[]{:S(2)}) collective-permute-start(bf16[64,640]{1,0:T(8,128)(2,1)S(1)} %collective-permute-done), channel_id=1, source_target_pairs={{2,0},{0,2},{6,4},{4,6},{10,8},{8,10},{14,12},{12,14},{3,1},{1,3},... | collective-permute-start | bytes 245768 | tf_op jit(solution)/shard_map/ppermute | solution.py:327
  19.6 3.2 %collective-permute-done.4 = bf16[64,640]{1,0:T(8,128)(2,1)S(1)} collective-permute-done((bf16[64,640]{1,0:T(8,128)(2,1)S(1)}, bf16[64,640]{1,0:T(8,128)(2,1)S(1)}, u32[]{:S(2)}, u32[]{:S(2)}) %collective-permute-start.4) | collective-permute-done | bytes 81952 | tf_op jit(solution)/shard_map/ppermute | solution.py:327
  22.8 1.3 %collective-permute-start.6 = (bf16[64,640]{1,0:T(8,128)(2,1)S(1)}, bf16[64,640]{1,0:T(8,128)(2,1)S(1)}, u32[]{:S(2)}, u32[]{:S(2)}) collective-permute-start(bf16[64,640]{1,0:T(8,128)(2,1)S(1)} %collective-permute-done.2), channel_id=1, source_target_pairs={{2,0},{0,2},{6,4},{4,6},{10,8},{8,10},{14,12},{12,14},{3,1},{1,3},... | collective-permute-start | bytes 245768 | tf_op jit(solution)/shard_map/ppermute | solution.py:327
  24.2 3.6 %collective-permute-done.6 = bf16[64,640]{1,0:T(8,128)(2,1)S(1)} collective-permute-done((bf16[64,640]{1,0:T(8,128)(2,1)S(1)}, bf16[64,640]{1,0:T(8,128)(2,1)S(1)}, u32[]{:S(2)}, u32[]{:S(2)}) %collective-permute-start.6) | collective-permute-done | bytes 81952 | tf_op jit(solution)/shard_map/ppermute | solution.py:327
  27.8 0.1 collective-permute-start.8
  27.9 0.0 copy-start.2
  27.9 1.1 %copy-done.2 = bf16[64,6144]{1,0:T(8,128)(2,1)S(1)} copy-done((bf16[64,6144]{1,0:T(8,128)(2,1)S(1)}, bf16[64,6144]{1,0:T(8,128)(2,1)}, u32[]{:S(2)}) %copy-start.2) | copy-done | bytes 786456
  29.0 0.9 %lift.3.query_rows = bf16[1024,640]{1,0:T(8,128)(2,1)S(1)} custom-call(bf16[64,6144]{1,0:T(8,128)(2,1)S(1)} %copy-done.2, bf16[16,128,512]{2,1,0:T(8,128)(2,1)S(1)} %collective-permute-done.17.key_up), custom_call_target="tpu_custom_call" | custom-call | flops 134217728 | bytes 3801088 | tf_op jit(solution)/shard_map/lift/pallas_call | solution.py:114
  30.0 0.0 copy-start.3
  30.0 0.0 copy-start.4
  30.0 4.0 %attend.5.refs_2_ = bf16[64,2048]{1,0:T(8,128)(2,1)S(1)} custom-call(bf16[1024,640]{1,0:T(8,128)(2,1)S(1)} %lift.3.query_rows, bf16[16,512,128]{2,1,0:T(8,128)(2,1)S(1)} %collective-permute-done.18.value_up, bf16[128,640]{1,0:T(8,128)(2,1)S(1)} %get-tuple-element.7.rest_0_, bf16[256,640]{1,0:T(8,128)(2,1)S(1)} %constant_dynamic-update-slice_fusion.rest_1_, ...), custom_call_target="tpu_custom_call" | custom-call | flops 2550136832 | bytes 4980736 | tf_op jit(solution)/shard_map/attend/pallas_call | solution.py:192
  34.0 0.0 copy-start.1
  34.0 0.8 collective-permute-start.19
  34.8 0.9 %lift.2.query_rows = bf16[1024,640]{1,0:T(8,128)(2,1)S(1)} custom-call(bf16[64,6144]{1,0:T(8,128)(2,1)S(1)} %copy-done.3, bf16[16,128,512]{2,1,0:T(8,128)(2,1)S(1)} %copy-done.4), custom_call_target="tpu_custom_call" | custom-call | flops 134217728 | bytes 3801088 | tf_op jit(solution)/shard_map/lift/pallas_call | solution.py:114
  35.8 2.0 %attend.4.refs_1_ = bf16[64,1024]{1,0:T(8,128)(2,1)S(1)} custom-call(bf16[1024,640]{1,0:T(8,128)(2,1)S(1)} %lift.2.query_rows, bf16[16,512,128]{2,1,0:T(8,128)(2,1)S(1)} %copy-done.1, bf16[128,640]{1,0:T(8,128)(2,1)S(1)} %get-tuple-element.7.rest_0_, bf16[256,640]{1,0:T(8,128)(2,1)S(1)} %constant_dynamic-update-slice_fusion.rest_1_, ...), custom_call_target="tpu_custom_call" | custom-call | flops 1275068416 | bytes 3145728 | tf_op jit(solution)/shard_map/attend/pallas_call | solution.py:192
  37.8 1.3 %collective-permute-start.13 = (bf16[64,1024]{1,0:T(8,128)(2,1)S(1)}, bf16[64,1024]{1,0:T(8,128)(2,1)S(1)}, u32[]{:S(2)}, u32[]{:S(2)}) collective-permute-start(bf16[64,1024]{1,0:T(8,128)(2,1)S(1)} %attend.4.refs_1_), channel_id=1, source_target_pairs={{4,0},{8,4},{12,8},{14,12},{10,14},{6,10},{2,6},{0,2},{5,1},{9,5},... | collective-permute-start | bytes 393224 | tf_op jit(solution)/shard_map/ppermute | solution.py:327
  39.0 0.8 collective-permute-start.30
  39.8 1.2 %collective-permute-start.24 = (bf16[64,2048]{1,0:T(8,128)(2,1)S(1)}, bf16[64,2048]{1,0:T(8,128)(2,1)S(1)}, u32[]{:S(2)}, u32[]{:S(2)}) collective-permute-start(bf16[64,2048]{1,0:T(8,128)(2,1)S(1)} %attend.5.refs_2_), channel_id=1, source_target_pairs={{4,0},{8,4},{12,8},{14,12},{10,14},{6,10},{2,6},{0,2},{5,1},{9,5},... | collective-permute-start | bytes 786440 | tf_op jit(solution)/shard_map/ppermute | solution.py:327
  41.1 2.0 %attend.3.refs_0_ = bf16[64,1024]{1,0:T(8,128)(2,1)S(1)} custom-call(bf16[1024,640]{1,0:T(8,128)(2,1)S(1)} %lift.2.query_rows, bf16[16,512,128]{2,1,0:T(8,128)(2,1)S(1)} %copy-done.1, bf16[128,640]{1,0:T(8,128)(2,1)S(1)} %get-tuple-element.7.rest_0_, bf16[256,640]{1,0:T(8,128)(2,1)S(1)} %constant_dynamic-update-slice_fusion.rest_1_, ...), custom_call_target="tpu_custom_call" | custom-call | flops 1275068416 | bytes 3145728 | tf_op jit(solution)/shard_map/attend/pallas_call | solution.py:192
  43.0 1.1 %collective-permute-done.13.refs_4_ = bf16[64,1024]{1,0:T(8,128)(2,1)S(1)} collective-permute-done((bf16[64,1024]{1,0:T(8,128)(2,1)S(1)}, bf16[64,1024]{1,0:T(8,128)(2,1)S(1)}, u32[]{:S(2)}, u32[]{:S(2)}) %collective-permute-start.13) | collective-permute-done | bytes 131104 | tf_op jit(solution)/shard_map/ppermute | solution.py:327
  44.2 1.7 %collective-permute-start.27 = (bf16[64,1024]{1,0:T(8,128)(2,1)S(1)}, bf16[64,1024]{1,0:T(8,128)(2,1)S(1)}, u32[]{:S(2)}, u32[]{:S(2)}) collective-permute-start(bf16[64,1024]{1,0:T(8,128)(2,1)S(1)} %attend.3.refs_0_), channel_id=1, source_target_pairs={{0,4},{4,8},{8,12},{12,14},{14,10},{10,6},{6,2},{2,0},{1,5},{5,9},... | collective-permute-start | bytes 393224 | tf_op jit(solution)/shard_map/ppermute | solution.py:327
  45.9 2.0 %collective-permute-start.20 = (bf16[64,2048]{1,0:T(8,128)(2,1)S(1)}, bf16[64,2048]{1,0:T(8,128)(2,1)S(1)}, u32[]{:S(2)}, u32[]{:S(2)}) collective-permute-start(bf16[64,2048]{1,0:T(8,128)(2,1)S(1)} %collective-permute-done.19.refs_2_), channel_id=1, source_target_pairs={{0,4},{4,8},{8,12},{12,14},{14,10},{10,6},{6,2},{2,0},{1,5},{5,9},... | collective-permute-start | bytes 786440 | tf_op jit(solution)/shard_map/ppermute | solution.py:327
  47.9 0.0 collective-permute-start.9
  47.9 2.6 %collective-permute-done.27.refs_0_ = bf16[64,1024]{1,0:T(8,128)(2,1)S(1)} collective-permute-done((bf16[64,1024]{1,0:T(8,128)(2,1)S(1)}, bf16[64,1024]{1,0:T(8,128)(2,1)S(1)}, u32[]{:S(2)}, u32[]{:S(2)}) %collective-permute-start.27) | collective-permute-done | bytes 131104 | tf_op jit(solution)/shard_map/ppermute | solution.py:327
  50.5 1.2 %collective-permute-start.14 = (bf16[64,1024]{1,0:T(8,128)(2,1)S(1)}, bf16[64,1024]{1,0:T(8,128)(2,1)S(1)}, u32[]{:S(2)}, u32[]{:S(2)}) collective-permute-start(bf16[64,1024]{1,0:T(8,128)(2,1)S(1)} %collective-permute-done.13.refs_4_), channel_id=1, source_target_pairs={{4,0},{8,4},{12,8},{14,12},{10,14},{6,10},{2,6},{0,2},{5,1},{9,5},... | collective-permute-start | bytes 393224 | tf_op jit(solution)/shard_map/ppermute | solution.py:327
  51.8 1.5 %collective-permute-done.9.refs_3_ = bf16[64,1024]{1,0:T(8,128)(2,1)S(1)} collective-permute-done((bf16[64,1024]{1,0:T(8,128)(2,1)S(1)}, bf16[64,1024]{1,0:T(8,128)(2,1)S(1)}, u32[]{:S(2)}, u32[]{:S(2)}) %collective-permute-start.9) | collective-permute-done | bytes 131104 | tf_op jit(solution)/shard_map/ppermute | solution.py:327
  53.3 1.9 %collective-permute-start.31 = (bf16[64,1024]{1,0:T(8,128)(2,1)S(1)}, bf16[64,1024]{1,0:T(8,128)(2,1)S(1)}, u32[]{:S(2)}, u32[]{:S(2)}) collective-permute-start(bf16[64,1024]{1,0:T(8,128)(2,1)S(1)} %collective-permute-done.30.refs_1_), channel_id=1, source_target_pairs={{0,4},{4,8},{8,12},{12,14},{14,10},{10,6},{6,2},{2,0},{1,5},{5,9},... | collective-permute-start | bytes 393224 | tf_op jit(solution)/shard_map/ppermute | solution.py:327
  55.2 0.1 collective-permute-start.25
  55.3 0.3 collective-permute-done.14.refs_4_
  55.7 2.5 %collective-permute-start.10 = (bf16[64,1024]{1,0:T(8,128)(2,1)S(1)}, bf16[64,1024]{1,0:T(8,128)(2,1)S(1)}, u32[]{:S(2)}, u32[]{:S(2)}) collective-permute-start(bf16[64,1024]{1,0:T(8,128)(2,1)S(1)} %collective-permute-done.9.refs_3_), channel_id=1, source_target_pairs={{4,0},{8,4},{12,8},{14,12},{10,14},{6,10},{2,6},{0,2},{5,1},{9,5},... | collective-permute-start | bytes 393224 | tf_op jit(solution)/shard_map/ppermute | solution.py:327
  58.2 1.4 %collective-permute-done.31.refs_1_ = bf16[64,1024]{1,0:T(8,128)(2,1)S(1)} collective-permute-done((bf16[64,1024]{1,0:T(8,128)(2,1)S(1)}, bf16[64,1024]{1,0:T(8,128)(2,1)S(1)}, u32[]{:S(2)}, u32[]{:S(2)}) %collective-permute-start.31) | collective-permute-done | bytes 131104 | tf_op jit(solution)/shard_map/ppermute | solution.py:327
  59.6 2.0 %collective-permute-start.28 = (bf16[64,1024]{1,0:T(8,128)(2,1)S(1)}, bf16[64,1024]{1,0:T(8,128)(2,1)S(1)}, u32[]{:S(2)}, u32[]{:S(2)}) collective-permute-start(bf16[64,1024]{1,0:T(8,128)(2,1)S(1)} %collective-permute-done.27.refs_0_), channel_id=1, source_target_pairs={{0,4},{4,8},{8,12},{12,14},{14,10},{10,6},{6,2},{2,0},{1,5},{5,9},... | collective-permute-start | bytes 393224 | tf_op jit(solution)/shard_map/ppermute | solution.py:327
  61.6 2.3 %collective-permute-done.10.refs_3_ = bf16[64,1024]{1,0:T(8,128)(2,1)S(1)} collective-permute-done((bf16[64,1024]{1,0:T(8,128)(2,1)S(1)}, bf16[64,1024]{1,0:T(8,128)(2,1)S(1)}, u32[]{:S(2)}, u32[]{:S(2)}) %collective-permute-start.10) | collective-permute-done | bytes 131104 | tf_op jit(solution)/shard_map/ppermute | solution.py:327
  63.9 1.7 %collective-permute-start.32 = (bf16[64,1024]{1,0:T(8,128)(2,1)S(1)}, bf16[64,1024]{1,0:T(8,128)(2,1)S(1)}, u32[]{:S(2)}, u32[]{:S(2)}) collective-permute-start(bf16[64,1024]{1,0:T(8,128)(2,1)S(1)} %collective-permute-done.31.refs_1_), channel_id=1, source_target_pairs={{0,4},{4,8},{8,12},{12,14},{14,10},{10,6},{6,2},{2,0},{1,5},{5,9},... | collective-permute-start | bytes 393224 | tf_op jit(solution)/shard_map/ppermute | solution.py:327
  65.7 0.6 touch.1
  66.3 1.8 %collective-permute-done.28.refs_0_ = bf16[64,1024]{1,0:T(8,128)(2,1)S(1)} collective-permute-done((bf16[64,1024]{1,0:T(8,128)(2,1)S(1)}, bf16[64,1024]{1,0:T(8,128)(2,1)S(1)}, u32[]{:S(2)}, u32[]{:S(2)}) %collective-permute-start.28) | collective-permute-done | bytes 131104 | tf_op jit(solution)/shard_map/ppermute | solution.py:327
  68.1 1.0 %collective-permute-start.15 = (bf16[64,1024]{1,0:T(8,128)(2,1)S(1)}, bf16[64,1024]{1,0:T(8,128)(2,1)S(1)}, u32[]{:S(2)}, u32[]{:S(2)}) collective-permute-start(bf16[64,1024]{1,0:T(8,128)(2,1)S(1)} %collective-permute-done.14.refs_4_), channel_id=1, source_target_pairs={{4,0},{8,4},{12,8},{14,12},{10,14},{6,10},{2,6},{0,2},{5,1},{9,5},... | collective-permute-start | bytes 393224 | tf_op jit(solution)/shard_map/ppermute | solution.py:327
  69.1 0.8 collective-permute-start.11
  69.9 0.8 collective-permute-start.26
  70.7 2.0 %project.6.refs_8_ = bf16[8,1,64,896]{3,2,1,0:T(8,128)(2,1)} custom-call(bf16[64,1024]{1,0:T(8,128)(2,1)S(1)} %attend.3.refs_0_, bf16[64,1024]{1,0:T(8,128)(2,1)S(1)} %attend.4.refs_1_, bf16[64,2048]{1,0:T(8,128)(2,1)S(1)} %attend.5.refs_2_, bf16[2048,896]{1,0:T(8,128)(2,1)S(1)} %copy-done, bf16[2048,896]{1,0:T(8,128)(2,1)S(1)} %collective-permute-done.23.refs_4_.refs_7_), custom_call_target="tpu_custom_call" | custom-call | flops 469762048 | bytes 7340032 | tf_op jit(solution)/shard_map/project/pallas_call | solution.py:265
  72.7 1.2 %collective-permute-start.29 = (bf16[64,1024]{1,0:T(8,128)(2,1)S(1)}, bf16[64,1024]{1,0:T(8,128)(2,1)S(1)}, u32[]{:S(2)}, u32[]{:S(2)}) collective-permute-start(bf16[64,1024]{1,0:T(8,128)(2,1)S(1)} %collective-permute-done.28.refs_0_), channel_id=1, source_target_pairs={{0,4},{4,8},{8,12},{12,14},{14,10},{10,6},{6,2},{2,0},{1,5},{5,9},... | collective-permute-start | bytes 393224 | tf_op jit(solution)/shard_map/ppermute | solution.py:327
  74.0 1.2 %collective-permute-start.22 = (bf16[64,2048]{1,0:T(8,128)(2,1)S(1)}, bf16[64,2048]{1,0:T(8,128)(2,1)S(1)}, u32[]{:S(2)}, u32[]{:S(2)}) collective-permute-start(bf16[64,2048]{1,0:T(8,128)(2,1)S(1)} %collective-permute-done.21.refs_2_), channel_id=1, source_target_pairs={{0,4},{4,8},{8,12},{12,14},{14,10},{10,6},{6,2},{2,0},{1,5},{5,9},... | collective-permute-start | bytes 786440 | tf_op jit(solution)/shard_map/ppermute | solution.py:327
  75.2 2.0 %project.7.refs_8_ = bf16[8,1,64,896]{3,2,1,0:T(8,128)(2,1)} custom-call(bf16[64,1024]{1,0:T(8,128)(2,1)S(1)} %collective-permute-done.27.refs_0_, bf16[64,1024]{1,0:T(8,128)(2,1)S(1)} %collective-permute-done.30.refs_1_, bf16[64,2048]{1,0:T(8,128)(2,1)S(1)} %collective-permute-done.19.refs_2_, ...), custom_call_target="tpu_custom_call", output_to_operand_aliasing={{}: (8, {})} | custom-call | flops 939524096 | bytes 7340032 | tf_op jit(solution)/shard_map/project/pallas_call | solution.py:265
  77.2 0.8 collective-permute-start.16
  78.1 0.8 collective-permute-start.12
  78.9 2.0 %project.8.refs_5_ = bf16[8,1,64,896]{3,2,1,0:T(8,128)(2,1)} custom-call(bf16[64,1024]{1,0:T(8,128)(2,1)S(1)} %collective-permute-done.28.refs_0_, bf16[64,1024]{1,0:T(8,128)(2,1)S(1)} %collective-permute-done.31.refs_1_, bf16[64,2048]{1,0:T(8,128)(2,1)S(1)} %collective-permute-done.20.refs_2_, ...), custom_call_target="tpu_custom_call", output_to_operand_aliasing={{}: (8, {})} | custom-call | flops 939524096 | bytes 7340032 | tf_op jit(solution)/shard_map/project/pallas_call | solution.py:265
  80.9 2.0 %project.9.refs_5_ = bf16[8,1,64,896]{3,2,1,0:T(8,128)(2,1)} custom-call(bf16[64,1024]{1,0:T(8,128)(2,1)S(1)} %collective-permute-done.29.refs_0_, bf16[64,1024]{1,0:T(8,128)(2,1)S(1)} %collective-permute-done.32.refs_1_, bf16[64,2048]{1,0:T(8,128)(2,1)S(1)} %collective-permute-done.21.refs_2_, ...), custom_call_target="tpu_custom_call", output_to_operand_aliasing={{}: (5, {})} | custom-call | flops 469762048 | bytes 7340032 | tf_op jit(solution)/shard_map/project/pallas_call | solution.py:265
  82.9 2.0 %project.10.refs_5_ = bf16[8,1,64,896]{3,2,1,0:T(8,128)(2,1)} custom-call(bf16[64,1024]{1,0:T(8,128)(2,1)S(1)} %collective-permute-done.11.refs_0_, bf16[64,1024]{1,0:T(8,128)(2,1)S(1)} %collective-permute-done.15.refs_1_, bf16[64,2048]{1,0:T(8,128)(2,1)S(1)} %collective-permute-done.26.refs_2_, ...), custom_call_target="tpu_custom_call", output_to_operand_aliasing={{}: (5, {})} | custom-call | flops 469762048 | bytes 7340032 | tf_op jit(solution)/shard_map/project/pallas_call | solution.py:265
  85.0 2.0 %project.11 = bf16[8,1,64,896]{3,2,1,0:T(8,128)(2,1)} custom-call(bf16[64,1024]{1,0:T(8,128)(2,1)S(1)} %collective-permute-done.12.refs_0_, bf16[64,1024]{1,0:T(8,128)(2,1)S(1)} %collective-permute-done.16.refs_1_, bf16[64,2048]{1,0:T(8,128)(2,1)S(1)} %collective-permute-done.22.refs_2_, ...), custom_call_target="tpu_custom_call", output_to_operand_aliasing={{}: (5, {})} | custom-call | flops 469762048 | bytes 7340032 | tf_op jit(solution)/shard_map/project/pallas_call | solution.py:265
  (36 shorter events, 0.2 us)
Async XLA Ops:
  0.0 69.9 %collective-permute-start.23 = (bf16[2048,896]{1,0:T(8,128)(2,1)}, bf16[2048,896]{1,0:T(8,128)(2,1)S(1)}, u32[]{:S(2)}, u32[]{:S(2)}) collective-permute-start(bf16[2048,896]{1,0:T(8,128)(2,1)} %refs_3_.7), channel_id=1, source_target_pairs={{0,1},{1,0},{2,3},{3,2},{4,5},{5,4},{6,7},{7,6},{8,9},{9,8},{10,11... | collective-permute-start | bytes 11010056 | tf_op jit(solution)/shard_map/ppermute | solution.py:327
  0.5 27.4 %collective-permute-start.17 = (bf16[16,128,512]{2,1,0:T(8,128)(2,1)}, bf16[16,128,512]{2,1,0:T(8,128)(2,1)S(1)}, u32[]{:S(2)}, u32[]{:S(2)}) collective-permute-start(bf16[16,128,512]{2,1,0:T(8,128)(2,1)} %key_up.1), channel_id=1, source_target_pairs={{0,1},{1,0},{2,3},{3,2},{4,5},{5,4},{6,7},{7,6},{8,9},{9,8},{10,11... | collective-permute-start | bytes 6291464 | tf_op jit(solution)/shard_map/ppermute | solution.py:327
  0.5 29.5 %collective-permute-start.18 = (bf16[16,512,128]{2,1,0:T(8,128)(2,1)}, bf16[16,512,128]{2,1,0:T(8,128)(2,1)S(1)}, u32[]{:S(2)}, u32[]{:S(2)}) collective-permute-start(bf16[16,512,128]{2,1,0:T(8,128)(2,1)} %value_up.3), channel_id=1, source_target_pairs={{0,1},{1,0},{2,3},{3,2},{4,5},{5,4},{6,7},{7,6},{8,9},{9,8},{10,11... | collective-permute-start | bytes 6291464 | tf_op jit(solution)/shard_map/ppermute | solution.py:327
  1.0 0.9 %copy-start.5 = (bf16[128,576]{0,1:T(8,128)(2,1)S(1)}, bf16[128,576]{0,1:T(8,128)(2,1)}, u32[]{:S(2)}) copy-start(bf16[128,576]{0,1:T(8,128)(2,1)} %param.7) | copy-start | bytes 442372
  1.9 0.7 copy-start.6
  2.9 8.6 %collective-permute-start.1 = (bf16[64,640]{1,0:T(8,128)(2,1)S(1)}, bf16[64,640]{1,0:T(8,128)(2,1)S(1)}, u32[]{:S(2)}, u32[]{:S(2)}) collective-permute-start(bf16[64,640]{1,0:T(8,128)(2,1)S(1)} %get-tuple-element.8), channel_id=1, source_target_pairs={{8,0},{10,2},{12,4},{14,6},{0,8},{2,10},{4,12},{6,14},{9,1},{11,3}... | collective-permute-start | bytes 245768 | tf_op jit(solution)/shard_map/ppermute | solution.py:327
  6.5 6.5 %collective-permute-start = (bf16[64,640]{1,0:T(8,128)(2,1)S(1)}, bf16[64,640]{1,0:T(8,128)(2,1)S(1)}, u32[]{:S(2)}, u32[]{:S(2)}) collective-permute-start(bf16[64,640]{1,0:T(8,128)(2,1)S(1)} %get-tuple-element.8), channel_id=1, source_target_pairs={{4,0},{6,2},{0,4},{2,6},{12,8},{14,10},{8,12},{10,14},{5,1},{7,3},... | collective-permute-start | bytes 245768 | tf_op jit(solution)/shard_map/ppermute | solution.py:327
  11.5 6.5 %collective-permute-start.3 = (bf16[64,640]{1,0:T(8,128)(2,1)S(1)}, bf16[64,640]{1,0:T(8,128)(2,1)S(1)}, u32[]{:S(2)}, u32[]{:S(2)}) collective-permute-start(bf16[64,640]{1,0:T(8,128)(2,1)S(1)} %get-tuple-element.8), channel_id=1, source_target_pairs={{2,0},{0,2},{6,4},{4,6},{10,8},{8,10},{14,12},{12,14},{3,1},{1,3},... | collective-permute-start | bytes 245768 | tf_op jit(solution)/shard_map/ppermute | solution.py:327
  13.1 4.4 %collective-permute-start.2 = (bf16[64,640]{1,0:T(8,128)(2,1)S(1)}, bf16[64,640]{1,0:T(8,128)(2,1)S(1)}, u32[]{:S(2)}, u32[]{:S(2)}) collective-permute-start(bf16[64,640]{1,0:T(8,128)(2,1)S(1)} %collective-permute-done.1), channel_id=1, source_target_pairs={{4,0},{6,2},{0,4},{2,6},{12,8},{14,10},{8,12},{10,14},{5,1},{7,3},... | collective-permute-start | bytes 245768 | tf_op jit(solution)/shard_map/ppermute | solution.py:327
  17.5 5.3 %collective-permute-start.5 = (bf16[64,640]{1,0:T(8,128)(2,1)S(1)}, bf16[64,640]{1,0:T(8,128)(2,1)S(1)}, u32[]{:S(2)}, u32[]{:S(2)}) collective-permute-start(bf16[64,640]{1,0:T(8,128)(2,1)S(1)} %collective-permute-done.1), channel_id=1, source_target_pairs={{2,0},{0,2},{6,4},{4,6},{10,8},{8,10},{14,12},{12,14},{3,1},{1,3},... | collective-permute-start | bytes 245768 | tf_op jit(solution)/shard_map/ppermute | solution.py:327
  18.0 4.8 %collective-permute-start.4 = (bf16[64,640]{1,0:T(8,128)(2,1)S(1)}, bf16[64,640]{1,0:T(8,128)(2,1)S(1)}, u32[]{:S(2)}, u32[]{:S(2)}) collective-permute-start(bf16[64,640]{1,0:T(8,128)(2,1)S(1)} %collective-permute-done), channel_id=1, source_target_pairs={{2,0},{0,2},{6,4},{4,6},{10,8},{8,10},{14,12},{12,14},{3,1},{1,3},... | collective-permute-start | bytes 245768 | tf_op jit(solution)/shard_map/ppermute | solution.py:327
  22.8 7.1 %collective-permute-start.7 = (bf16[256,640]{1,0:T(8,128)(2,1)S(1)}, bf16[256,640]{1,0:T(8,128)(2,1)S(1)}, u32[]{:S(2)}, u32[]{:S(2)}) collective-permute-start(bf16[256,640]{1,0:T(8,128)(2,1)S(1)} %constant_dynamic-update-slice_fusion.rest_1_), channel_id=1, source_target_pairs={{0,1},{1,0},{2,3},{3,2},{4,5},{5,4},{6,7},{7,6},{8,9},{9,8},{10,11... | collective-permute-start | bytes 983048 | tf_op jit(solution)/shard_map/ppermute | solution.py:327
  22.8 4.9 %collective-permute-start.6 = (bf16[64,640]{1,0:T(8,128)(2,1)S(1)}, bf16[64,640]{1,0:T(8,128)(2,1)S(1)}, u32[]{:S(2)}, u32[]{:S(2)}) collective-permute-start(bf16[64,640]{1,0:T(8,128)(2,1)S(1)} %collective-permute-done.2), channel_id=1, source_target_pairs={{2,0},{0,2},{6,4},{4,6},{10,8},{8,10},{14,12},{12,14},{3,1},{1,3},... | collective-permute-start | bytes 245768 | tf_op jit(solution)/shard_map/ppermute | solution.py:327
  27.8 2.2 %collective-permute-start.8 = (bf16[192,640]{1,0:T(8,128)(2,1)S(1)}, bf16[192,640]{1,0:T(8,128)(2,1)S(1)}, u32[]{:S(2)}, u32[]{:S(2)}) collective-permute-start(bf16[192,640]{1,0:T(8,128)(2,1)S(1)} %constant_dynamic-update-slice_fusion.4.rest_2_), channel_id=1, source_target_pairs={{0,1},{1,0},{2,3},{3,2},{4,5},{5,4},{6,7},{7,6},{8,9},{9,8},{10,11... | collective-permute-start | bytes 737288 | tf_op jit(solution)/shard_map/ppermute | solution.py:327
  27.9 1.1 %copy-start.2 = (bf16[64,6144]{1,0:T(8,128)(2,1)S(1)}, bf16[64,6144]{1,0:T(8,128)(2,1)}, u32[]{:S(2)}) copy-start(bf16[64,6144]{1,0:T(8,128)(2,1)} %queries.3) | copy-start | bytes 2359300
  30.0 4.9 %copy-start.3 = (bf16[64,6144]{1,0:T(8,128)(2,1)S(1)}, bf16[64,6144]{1,0:T(8,128)(2,1)}, u32[]{:S(2)}) copy-start(bf16[64,6144]{1,0:T(8,128)(2,1)} %queries.3) | copy-start | bytes 2359300
  30.0 4.8 %copy-start.4 = (bf16[16,128,512]{2,1,0:T(8,128)(2,1)S(1)}, bf16[16,128,512]{2,1,0:T(8,128)(2,1)}, u32[]{:S(2)}) copy-start(bf16[16,128,512]{2,1,0:T(8,128)(2,1)} %key_up.1) | copy-start | bytes 6291460
  34.0 1.8 %copy-start.1 = (bf16[16,512,128]{2,1,0:T(8,128)(2,1)S(1)}, bf16[16,512,128]{2,1,0:T(8,128)(2,1)}, u32[]{:S(2)}) copy-start(bf16[16,512,128]{2,1,0:T(8,128)(2,1)} %value_up.3) | copy-start | bytes 6291460
  34.0 11.9 %collective-permute-start.19 = (bf16[64,2048]{1,0:T(8,128)(2,1)S(1)}, bf16[64,2048]{1,0:T(8,128)(2,1)S(1)}, u32[]{:S(2)}, u32[]{:S(2)}) collective-permute-start(bf16[64,2048]{1,0:T(8,128)(2,1)S(1)} %attend.5.refs_2_), channel_id=1, source_target_pairs={{0,4},{4,8},{8,12},{12,14},{14,10},{10,6},{6,2},{2,0},{1,5},{5,9},... | collective-permute-start | bytes 786440 | tf_op jit(solution)/shard_map/ppermute | solution.py:327
  37.8 6.4 %collective-permute-start.13 = (bf16[64,1024]{1,0:T(8,128)(2,1)S(1)}, bf16[64,1024]{1,0:T(8,128)(2,1)S(1)}, u32[]{:S(2)}, u32[]{:S(2)}) collective-permute-start(bf16[64,1024]{1,0:T(8,128)(2,1)S(1)} %attend.4.refs_1_), channel_id=1, source_target_pairs={{4,0},{8,4},{12,8},{14,12},{10,14},{6,10},{2,6},{0,2},{5,1},{9,5},... | collective-permute-start | bytes 393224 | tf_op jit(solution)/shard_map/ppermute | solution.py:327
  39.0 8.9 %collective-permute-start.30 = (bf16[64,1024]{1,0:T(8,128)(2,1)S(1)}, bf16[64,1024]{1,0:T(8,128)(2,1)S(1)}, u32[]{:S(2)}, u32[]{:S(2)}) collective-permute-start(bf16[64,1024]{1,0:T(8,128)(2,1)S(1)} %attend.4.refs_1_), channel_id=1, source_target_pairs={{0,4},{4,8},{8,12},{12,14},{14,10},{10,6},{6,2},{2,0},{1,5},{5,9},... | collective-permute-start | bytes 393224 | tf_op jit(solution)/shard_map/ppermute | solution.py:327
  39.8 15.4 %collective-permute-start.24 = (bf16[64,2048]{1,0:T(8,128)(2,1)S(1)}, bf16[64,2048]{1,0:T(8,128)(2,1)S(1)}, u32[]{:S(2)}, u32[]{:S(2)}) collective-permute-start(bf16[64,2048]{1,0:T(8,128)(2,1)S(1)} %attend.5.refs_2_), channel_id=1, source_target_pairs={{4,0},{8,4},{12,8},{14,12},{10,14},{6,10},{2,6},{0,2},{5,1},{9,5},... | collective-permute-start | bytes 786440 | tf_op jit(solution)/shard_map/ppermute | solution.py:327
  41.1 29.6 %copy-start = (bf16[2048,896]{1,0:T(8,128)(2,1)S(1)}, bf16[2048,896]{1,0:T(8,128)(2,1)}, u32[]{:S(2)}) copy-start(bf16[2048,896]{1,0:T(8,128)(2,1)} %refs_3_.7) | copy-start | bytes 11010052
  44.2 6.4 %collective-permute-start.27 = (bf16[64,1024]{1,0:T(8,128)(2,1)S(1)}, bf16[64,1024]{1,0:T(8,128)(2,1)S(1)}, u32[]{:S(2)}, u32[]{:S(2)}) collective-permute-start(bf16[64,1024]{1,0:T(8,128)(2,1)S(1)} %attend.3.refs_0_), channel_id=1, source_target_pairs={{0,4},{4,8},{8,12},{12,14},{14,10},{10,6},{6,2},{2,0},{1,5},{5,9},... | collective-permute-start | bytes 393224 | tf_op jit(solution)/shard_map/ppermute | solution.py:327
  45.9 12.3 %collective-permute-start.20 = (bf16[64,2048]{1,0:T(8,128)(2,1)S(1)}, bf16[64,2048]{1,0:T(8,128)(2,1)S(1)}, u32[]{:S(2)}, u32[]{:S(2)}) collective-permute-start(bf16[64,2048]{1,0:T(8,128)(2,1)S(1)} %collective-permute-done.19.refs_2_), channel_id=1, source_target_pairs={{0,4},{4,8},{8,12},{12,14},{14,10},{10,6},{6,2},{2,0},{1,5},{5,9},... | collective-permute-start | bytes 786440 | tf_op jit(solution)/shard_map/ppermute | solution.py:327
  47.9 5.4 %collective-permute-start.9 = (bf16[64,1024]{1,0:T(8,128)(2,1)S(1)}, bf16[64,1024]{1,0:T(8,128)(2,1)S(1)}, u32[]{:S(2)}, u32[]{:S(2)}) collective-permute-start(bf16[64,1024]{1,0:T(8,128)(2,1)S(1)} %attend.3.refs_0_), channel_id=1, source_target_pairs={{4,0},{8,4},{12,8},{14,12},{10,14},{6,10},{2,6},{0,2},{5,1},{9,5},... | collective-permute-start | bytes 393224 | tf_op jit(solution)/shard_map/ppermute | solution.py:327
  50.5 5.1 %collective-permute-start.14 = (bf16[64,1024]{1,0:T(8,128)(2,1)S(1)}, bf16[64,1024]{1,0:T(8,128)(2,1)S(1)}, u32[]{:S(2)}, u32[]{:S(2)}) collective-permute-start(bf16[64,1024]{1,0:T(8,128)(2,1)S(1)} %collective-permute-done.13.refs_4_), channel_id=1, source_target_pairs={{4,0},{8,4},{12,8},{14,12},{10,14},{6,10},{2,6},{0,2},{5,1},{9,5},... | collective-permute-start | bytes 393224 | tf_op jit(solution)/shard_map/ppermute | solution.py:327
  53.3 6.3 %collective-permute-start.31 = (bf16[64,1024]{1,0:T(8,128)(2,1)S(1)}, bf16[64,1024]{1,0:T(8,128)(2,1)S(1)}, u32[]{:S(2)}, u32[]{:S(2)}) collective-permute-start(bf16[64,1024]{1,0:T(8,128)(2,1)S(1)} %collective-permute-done.30.refs_1_), channel_id=1, source_target_pairs={{0,4},{4,8},{8,12},{12,14},{14,10},{10,6},{6,2},{2,0},{1,5},{5,9},... | collective-permute-start | bytes 393224 | tf_op jit(solution)/shard_map/ppermute | solution.py:327
  55.2 13.9 %collective-permute-start.25 = (bf16[64,2048]{1,0:T(8,128)(2,1)S(1)}, bf16[64,2048]{1,0:T(8,128)(2,1)S(1)}, u32[]{:S(2)}, u32[]{:S(2)}) collective-permute-start(bf16[64,2048]{1,0:T(8,128)(2,1)S(1)} %collective-permute-done.24.refs_5_), channel_id=1, source_target_pairs={{4,0},{8,4},{12,8},{14,12},{10,14},{6,10},{2,6},{0,2},{5,1},{9,5},... | collective-permute-start | bytes 786440 | tf_op jit(solution)/shard_map/ppermute | solution.py:327
  55.7 8.3 %collective-permute-start.10 = (bf16[64,1024]{1,0:T(8,128)(2,1)S(1)}, bf16[64,1024]{1,0:T(8,128)(2,1)S(1)}, u32[]{:S(2)}, u32[]{:S(2)}) collective-permute-start(bf16[64,1024]{1,0:T(8,128)(2,1)S(1)} %collective-permute-done.9.refs_3_), channel_id=1, source_target_pairs={{4,0},{8,4},{12,8},{14,12},{10,14},{6,10},{2,6},{0,2},{5,1},{9,5},... | collective-permute-start | bytes 393224 | tf_op jit(solution)/shard_map/ppermute | solution.py:327
  58.2 15.8 %collective-permute-start.21 = (bf16[64,2048]{1,0:T(8,128)(2,1)S(1)}, bf16[64,2048]{1,0:T(8,128)(2,1)S(1)}, u32[]{:S(2)}, u32[]{:S(2)}) collective-permute-start(bf16[64,2048]{1,0:T(8,128)(2,1)S(1)} %collective-permute-done.20.refs_2_), channel_id=1, source_target_pairs={{0,4},{4,8},{8,12},{12,14},{14,10},{10,6},{6,2},{2,0},{1,5},{5,9},... | collective-permute-start | bytes 786440 | tf_op jit(solution)/shard_map/ppermute | solution.py:327
  59.6 8.5 %collective-permute-start.28 = (bf16[64,1024]{1,0:T(8,128)(2,1)S(1)}, bf16[64,1024]{1,0:T(8,128)(2,1)S(1)}, u32[]{:S(2)}, u32[]{:S(2)}) collective-permute-start(bf16[64,1024]{1,0:T(8,128)(2,1)S(1)} %collective-permute-done.27.refs_0_), channel_id=1, source_target_pairs={{0,4},{4,8},{8,12},{12,14},{14,10},{10,6},{6,2},{2,0},{1,5},{5,9},... | collective-permute-start | bytes 393224 | tf_op jit(solution)/shard_map/ppermute | solution.py:327
  63.9 8.8 %collective-permute-start.32 = (bf16[64,1024]{1,0:T(8,128)(2,1)S(1)}, bf16[64,1024]{1,0:T(8,128)(2,1)S(1)}, u32[]{:S(2)}, u32[]{:S(2)}) collective-permute-start(bf16[64,1024]{1,0:T(8,128)(2,1)S(1)} %collective-permute-done.31.refs_1_), channel_id=1, source_target_pairs={{0,4},{4,8},{8,12},{12,14},{14,10},{10,6},{6,2},{2,0},{1,5},{5,9},... | collective-permute-start | bytes 393224 | tf_op jit(solution)/shard_map/ppermute | solution.py:327
  68.1 9.1 %collective-permute-start.15 = (bf16[64,1024]{1,0:T(8,128)(2,1)S(1)}, bf16[64,1024]{1,0:T(8,128)(2,1)S(1)}, u32[]{:S(2)}, u32[]{:S(2)}) collective-permute-start(bf16[64,1024]{1,0:T(8,128)(2,1)S(1)} %collective-permute-done.14.refs_4_), channel_id=1, source_target_pairs={{4,0},{8,4},{12,8},{14,12},{10,14},{6,10},{2,6},{0,2},{5,1},{9,5},... | collective-permute-start | bytes 393224 | tf_op jit(solution)/shard_map/ppermute | solution.py:327
  69.1 9.0 %collective-permute-start.11 = (bf16[64,1024]{1,0:T(8,128)(2,1)S(1)}, bf16[64,1024]{1,0:T(8,128)(2,1)S(1)}, u32[]{:S(2)}, u32[]{:S(2)}) collective-permute-start(bf16[64,1024]{1,0:T(8,128)(2,1)S(1)} %collective-permute-done.10.refs_3_), channel_id=1, source_target_pairs={{4,0},{8,4},{12,8},{14,12},{10,14},{6,10},{2,6},{0,2},{5,1},{9,5},... | collective-permute-start | bytes 393224 | tf_op jit(solution)/shard_map/ppermute | solution.py:327
  69.9 13.0 %collective-permute-start.26 = (bf16[64,2048]{1,0:T(8,128)(2,1)S(1)}, bf16[64,2048]{1,0:T(8,128)(2,1)S(1)}, u32[]{:S(2)}, u32[]{:S(2)}) collective-permute-start(bf16[64,2048]{1,0:T(8,128)(2,1)S(1)} %collective-permute-done.25.refs_5_), channel_id=1, source_target_pairs={{4,0},{8,4},{12,8},{14,12},{10,14},{6,10},{2,6},{0,2},{5,1},{9,5},... | collective-permute-start | bytes 786440 | tf_op jit(solution)/shard_map/ppermute | solution.py:327
  72.7 8.1 %collective-permute-start.29 = (bf16[64,1024]{1,0:T(8,128)(2,1)S(1)}, bf16[64,1024]{1,0:T(8,128)(2,1)S(1)}, u32[]{:S(2)}, u32[]{:S(2)}) collective-permute-start(bf16[64,1024]{1,0:T(8,128)(2,1)S(1)} %collective-permute-done.28.refs_0_), channel_id=1, source_target_pairs={{0,4},{4,8},{8,12},{12,14},{14,10},{10,6},{6,2},{2,0},{1,5},{5,9},... | collective-permute-start | bytes 393224 | tf_op jit(solution)/shard_map/ppermute | solution.py:327
  74.0 11.0 %collective-permute-start.22 = (bf16[64,2048]{1,0:T(8,128)(2,1)S(1)}, bf16[64,2048]{1,0:T(8,128)(2,1)S(1)}, u32[]{:S(2)}, u32[]{:S(2)}) collective-permute-start(bf16[64,2048]{1,0:T(8,128)(2,1)S(1)} %collective-permute-done.21.refs_2_), channel_id=1, source_target_pairs={{0,4},{4,8},{8,12},{12,14},{14,10},{10,6},{6,2},{2,0},{1,5},{5,9},... | collective-permute-start | bytes 786440 | tf_op jit(solution)/shard_map/ppermute | solution.py:327
  77.2 7.7 %collective-permute-start.16 = (bf16[64,1024]{1,0:T(8,128)(2,1)S(1)}, bf16[64,1024]{1,0:T(8,128)(2,1)S(1)}, u32[]{:S(2)}, u32[]{:S(2)}) collective-permute-start(bf16[64,1024]{1,0:T(8,128)(2,1)S(1)} %collective-permute-done.15.refs_1_), channel_id=1, source_target_pairs={{4,0},{8,4},{12,8},{14,12},{10,14},{6,10},{2,6},{0,2},{5,1},{9,5},... | collective-permute-start | bytes 393224 | tf_op jit(solution)/shard_map/ppermute | solution.py:327
  78.1 6.9 %collective-permute-start.12 = (bf16[64,1024]{1,0:T(8,128)(2,1)S(1)}, bf16[64,1024]{1,0:T(8,128)(2,1)S(1)}, u32[]{:S(2)}, u32[]{:S(2)}) collective-permute-start(bf16[64,1024]{1,0:T(8,128)(2,1)S(1)} %collective-permute-done.11.refs_0_), channel_id=1, source_target_pairs={{4,0},{8,4},{12,8},{14,12},{10,14},{6,10},{2,6},{0,2},{5,1},{9,5},... | collective-permute-start | bytes 393224 | tf_op jit(solution)/shard_map/ppermute | solution.py:327

commit v3 on v2

--- a/solution.py
+++ b/solution.py
@@ -212,25 +212,27 @@
     )(query_rows, value_up, *keys)
 
 
-def project_kernel(count, offsets, chunks, *refs):
-    pieces = len(offsets)
+def project_kernel(count, offsets, rows_of, finish, added, *refs):
+    pieces, chunks = len(offsets), len(rows_of)
     parts = refs[: pieces * chunks]
-    own_weight, other_weight = refs[pieces * chunks : pieces * chunks + 2]
+    weight = refs[pieces * chunks]
+    product = None
+    for chunk, start in enumerate(rows_of):
+        stack = [parts[piece * chunks + chunk][...] for piece in range(pieces)]
+        stack = jnp.concatenate(stack, 0) if pieces > 1 else stack[0]
+        part = jnp.dot(
+            stack,
+            weight[start : start + stack.shape[1], :],
+            preferred_element_type=jnp.float32,
+        )
+        product = part if product is None else product + part
+    if added:
+        product += refs[pieces * chunks + 1][...]
+    if not finish:
+        refs[-1][...] = product
+        return
     out, held, sems = refs[-3:]
     rows = parts[0].shape[0]
-    product = None
-    start = 0
-    for chunk in range(chunks):
-        stack = [parts[piece * chunks + chunk][...] for piece in range(pieces)]
-        stack = jnp.concatenate(stack, 0) if pieces > 1 else stack[0]
-        depth = stack.shape[1]
-        if start < own_weight.shape[0]:
-            weight = own_weight[start : start + depth, :]
-        else:
-            weight = other_weight[...]
-        start += depth
-        part = jnp.dot(stack, weight, preferred_element_type=jnp.float32)
-        product = part if product is None else product + part
     held[...] = product.astype(jnp.bfloat16)
     block = lax.axis_index("seq")
     half = block // 2
@@ -247,35 +249,45 @@
         copy.wait()
 
 
-def project(count, pieces, own_weight, other_weight, mixed):
+def project(count, pieces, rows_of, weight, earlier=None, mixed=None, finish=True):
     offsets = [offset for offset, _ in pieces]
     operands = [part for _, parts in pieces for part in parts]
-    chunks = len(operands) // len(pieces)
     rows = operands[0].shape[0]
-    depth, columns = own_weight.shape
-    operands += [own_weight, other_weight]
+    columns = weight.shape[1]
+    total = len(pieces) * rows
+    operands.append(weight)
+    if earlier is not None:
+        operands.append(earlier)
     aliases = {}
     vmem = pl.BlockSpec(memory_space=pltpu.VMEM)
     anywhere = pl.BlockSpec(memory_space=pl.ANY)
     specs = [vmem] * len(operands)
-    if mixed is not None:
+    if finish and mixed is not None:
         aliases = {len(operands): 0}
         operands.append(mixed)
         specs.append(anywhere)
+    if finish:
+        shape = jax.ShapeDtypeStruct((count, 1, rows, columns), jnp.bfloat16)
+        scratch = [
+            pltpu.VMEM((total, columns), jnp.bfloat16),
+            pltpu.SemaphoreType.DMA((len(pieces),)),
+        ]
+    else:
+        shape = jax.ShapeDtypeStruct((total, columns), jnp.float32)
+        scratch = []
     return pl.pallas_call(
-        functools.partial(project_kernel, count, offsets, chunks),
+        functools.partial(
+            project_kernel, count, offsets, rows_of, finish, earlier is not None
+        ),
         in_specs=specs,
-        out_specs=anywhere,
-        out_shape=jax.ShapeDtypeStruct((count, 1, rows, columns), jnp.bfloat16),
-        scratch_shapes=[
-            pltpu.VMEM((len(pieces) * rows, columns), jnp.bfloat16),
-            pltpu.SemaphoreType.DMA((len(pieces),)),
-        ],
+        out_specs=anywhere if finish else vmem,
+        out_shape=shape,
+        scratch_shapes=scratch,
         input_output_aliases=aliases,
         compiler_params=pltpu.CompilerParams(vmem_limit_bytes=8 << 20),
         cost_estimate=pl.CostEstimate(
-            flops=4 * len(pieces) * rows * depth * columns,
-            bytes_accessed=4 * depth * columns,
+            flops=2 * total * weight.shape[0] * columns,
+            bytes_accessed=2 * weight.shape[0] * columns,
             transcendentals=0,
         ),
         name="project",
@@ -308,23 +320,9 @@
 
 
 def ring_order(steps):
-    right = ["a1", "b1", "a2", "c1"]
-    left = ["a1", "b1", "a2", "c1"]
-    for step in range(2, steps - 1):
-        right += [f"b{step}", f"c{step}", f"a{step + 1}"]
-        left += [f"b{step}", f"a{step + 1}", f"c{step}"]
-    step = steps - 1
-    right += [f"c{step}", f"b{step}", f"c{steps}"]
-    left += [f"b{step}", f"a{steps}", f"c{step}", f"b{steps}"]
-    names = []
-    for i in range(len(left)):
-        names += ["r" + right[i]] if i < len(right) else []
-        names.append("l" + left[i])
-    return names
-
-
-def send(value, axis, pairs):
-    return lax.ppermute(value, axis, pairs)
+    return [
+        way + chunk + str(step) for step in range(1, steps + 1) for chunk in "ab" for way in "rl"
+    ]
 
 
 def layer(queries, latents, latent_gain, key_up, value_up, out_weight):
@@ -337,53 +335,64 @@
     own_keys, half_keys = prepare(latents.T, latent_gain.reshape(1, KV))
     slots = {0: half_keys}
     for slot, bit in gather_plan(seq_count):
-        slots[slot | bit] = send(slots[slot], "seq", [(d ^ bit, d) for d in everyone])
+        slots[slot | bit] = lax.ppermute(slots[slot], "seq", [(d ^ bit, d) for d in everyone])
     near = [m for m in range(1, seq_count) if m % 2 == 0] + [1]
     far = [m for m in range(2, seq_count) if m % 2 == 1]
     near_keys = jnp.concatenate([slots[m] for m in near], 0)
     far_keys = jnp.concatenate([slots[m] for m in far], 0)
-    near_swap = send(near_keys, "head", swap_pairs)
-    far_swap = send(far_keys, "head", swap_pairs)
+    near_swap = lax.ppermute(near_keys, "head", swap_pairs)
+    far_swap = lax.ppermute(far_keys, "head", swap_pairs)
     keys = [own_keys, near_keys, far_keys, near_swap, far_swap]
 
-    key_other = send(key_up, "head", swap_pairs)
-    value_other = send(value_up, "head", swap_pairs)
-    weight_other = send(out_weight, "head", swap_pairs)
+    key_other = lax.ppermute(key_up, "head", swap_pairs)
+    value_other = lax.ppermute(value_up, "head", swap_pairs)
+    weight_other = lax.ppermute(out_weight, "head", swap_pairs)
     rows_a = lift(queries, key_up, False)
     touch(value_up)
     rows_b = lift(queries, key_other, True)
-    blocks = key_up.shape[0] // 8
-    first = blocks // 2
+    blocks = (0, key_up.shape[0] // 8)
     chunks = {}
-    chunks["a"] = attend(rows_a, value_up, keys, rows, (0, first))
-    chunks["b"] = attend(rows_a, value_up, keys, rows, (first, blocks - first))
-    chunks["c"] = attend(rows_b, value_other, keys, rows, (0, blocks))
+    chunks["a"] = attend(rows_a, value_up, keys, rows, blocks)
+    chunks["b"] = attend(rows_b, value_other, keys, rows, blocks)
 
     order = list(range(0, seq_count, 2)) + list(range(seq_count - 1, 0, -2))
     right = [(order[i], order[(i + 1) % seq_count]) for i in everyone]
     left = [(b, a) for a, b in right]
     steps = seq_count // 2
     held = {way + chunk + "0": value for chunk, value in chunks.items() for way in "rl"}
-    for step in range(1, steps + 1):
-        for name in ring_order(steps):
-            if name[2:] == str(step):
-                value = held[name[:2] + str(step - 1)]
-                held[name] = send(value, "seq", right if name[0] == "r" else left)
+    middle = chunks["a"].shape[1] // 2
+    for name in ring_order(steps):
+        step = int(name[2:])
+        value = held[name[:2] + str(step - 1)]
+        if step == steps:
+            value = value[:, :middle] if name[0] == "r" else value[:, middle:]
+        held[name] = lax.ppermute(value, "seq", right if name[0] == "r" else left)
 
     def put(mixed, *pieces):
-        return project(seq_count, pieces, out_weight, weight_other, mixed)
-
-    def from_way(way, step):
-        return [held[f"{way}{chunk}{step}"] for chunk in "abc"]
-
-    mixed = put(None, (0, from_way("r", 0)))
-    for step in range(1, steps - 1):
-        mixed = put(mixed, (-step, from_way("r", step)), (step, from_way("l", step)))
-    step = steps - 1
-    mixed = put(mixed, (-step, from_way("r", step)))
-    mixed = put(mixed, (step, from_way("l", step)))
-    final = [held[f"la{steps}"], held[f"lb{steps}"], held[f"rc{steps}"]]
-    return put(mixed, (steps, final))
+        earlier = project(
+            seq_count,
+            [(offset, [held[f"{way}a{at}"]]) for offset, way, at in pieces],
+            (0,),
+            out_weight,
+            finish=False,
+        )
+        return project(
+            seq_count,
+            [(offset, [held[f"{way}b{at}"]]) for offset, way, at in pieces],
+            (0,),
+            weight_other,
+            earlier,
+            mixed,
+        )
+
+    mixed = put(None, (0, "r", 0))
+    for step in range(1, steps):
+        mixed = put(mixed, (-step, "r", step), (step, "l", step))
+    ends = (0, middle)
+    pieces = [(steps, [held[f"ra{steps}"], held[f"la{steps}"]])]
+    earlier = project(seq_count, pieces, ends, out_weight, finish=False)
+    pieces = [(steps, [held[f"rb{steps}"], held[f"lb{steps}"]])]
+    return project(seq_count, pieces, ends, weight_other, earlier, mixed)
 
 
 def solution(mesh):

time: 87.3 us -> 88.1 us (level)
  starting transfers between devices: 36 us -> 28.6 us
  waiting for transfers between devices: 25.3 us -> 32.4 us
  local copies, waits for them, and re-layouts: 2.83 us -> 5.07 us
  Pallas kernels: 22.6 us -> 21.3 us
    ppermute x33 -> x28, starting transfers between devices: 36 us -> 28.6 us  [the longest x16 16.7 us: layer(): held[name] = lax.ppermute(value, 'seq', right if name[0] == 'r' else left)]
    ppermute x33 -> x28, waiting for transfers between devices: 25.3 us -> 32.4 us  [the longest x16 18.4 us: layer(): held[name] = lax.ppermute(value, 'seq', right if name[0] == 'r' else left)]
    unnamed x19, local copies, waits for them, and re-layouts: 2.8 us -> 5 us
    pallas_call x6 -> x10, Pallas kernels: 12 us -> 10.7 us  [project(): pl.pallas_call(functools.partial(project_kernel, count, offsets, rows_of,...]
    pallas_call x3 -> x2, Pallas kernels: 7.87 us -> 7.91 us  [attend(): pl.pallas_call(functools.partial(attend_kernel, 4 * rows, len(keys)), gri...]
  transfers between devices with their start and end apart: 33 -> 28, of which waited for: 11 -> 10; matrix products, arithmetic and copies ran while one was open for 0% -> 0% of each run, Pallas kernels for 24% -> 23%
where the time goes in v3:
time: 88.1 us; the launch traced here: 87.8 us
  waiting for transfers between devices  32.4 us (37%)
  starting transfers between devices  28.6 us (32%)
  Pallas kernels  21.3 us (24%)
  local copies, waits for them, and re-layouts  5.07 us (6%)
    ppermute x16, waiting for transfers between devices, layer(): held[name] = lax.ppermute(value, 'seq', right if name[0] == 'r' else left)  18.4 us
    ppermute x16, starting transfers between devices, layer(): held[name] = lax.ppermute(value, 'seq', right if name[0] == 'r' else left)  16.7 us
    ppermute x7, waiting for transfers between devices, layer(): lax.ppermute(slots[slot], 'seq', [(d ^ bit, d) for d in everyone])  14 us
    ppermute x7, starting transfers between devices, layer(): lax.ppermute(slots[slot], 'seq', [(d ^ bit, d) for d in everyone])  10.8 us
    pallas_call x10, Pallas kernels, project(): pl.pallas_call(functools.partial(project_kernel, count, offsets, rows_of,...  10.7 us
    pallas_call x2, Pallas kernels, attend(): pl.pallas_call(functools.partial(attend_kernel, 4 * rows, len(keys)), gri...  7.91 us
    unnamed x19, local copies, waits for them, and re-layouts  5 us
    pallas_call x2, Pallas kernels, lift(): pl.pallas_call(lift_kernel, grid=(steps,), in_specs=[pl.BlockSpec((rows,...  1.88 us
  transfers between devices with their start and end apart: 28, of which 10 were waited for; matrix products, arithmetic and copies ran while one was open for 0% of the time, Pallas kernels for 23%

profile of v3, /device:TPU:0, one launch (start us, length us, event | category | flops | bytes accessed | tf_op | source)
XLA Modules:
  0.0 87.8 jit_solution(11347091527054581040)
XLA Ops:
  0.0 0.5 collective-permute-start.19
  0.5 0.0 collective-permute-start
  0.5 0.5 collective-permute-start.1
  1.0 0.9 %copy-done.5 = bf16[128,576]{0,1:T(8,128)(2,1)S(1)} copy-done((bf16[128,576]{0,1:T(8,128)(2,1)S(1)}, bf16[128,576]{0,1:T(8,128)(2,1)}, u32[]{:S(2)}) %copy-start.5) | copy-done | bytes 147480
  1.9 0.7 copy-done.6
  2.6 0.3 prepare.1
  2.9 3.6 %collective-permute-start.3 = (bf16[64,640]{1,0:T(8,128)(2,1)S(1)}, bf16[64,640]{1,0:T(8,128)(2,1)S(1)}, u32[]{:S(2)}, u32[]{:S(2)}) collective-permute-start(bf16[64,640]{1,0:T(8,128)(2,1)S(1)} %get-tuple-element.8), channel_id=1, source_target_pairs={{8,0},{10,2},{12,4},{14,6},{0,8},{2,10},{4,12},{6,14},{9,1},{11,3}... | collective-permute-start | bytes 245768 | tf_op jit(solution)/shard_map/ppermute | solution.py:338
  6.5 1.6 %collective-permute-start.2 = (bf16[64,640]{1,0:T(8,128)(2,1)S(1)}, bf16[64,640]{1,0:T(8,128)(2,1)S(1)}, u32[]{:S(2)}, u32[]{:S(2)}) collective-permute-start(bf16[64,640]{1,0:T(8,128)(2,1)S(1)} %get-tuple-element.8), channel_id=1, source_target_pairs={{4,0},{6,2},{0,4},{2,6},{12,8},{14,10},{8,12},{10,14},{5,1},{7,3},... | collective-permute-start | bytes 245768 | tf_op jit(solution)/shard_map/ppermute | solution.py:338
  8.1 3.4 %collective-permute-done.3 = bf16[64,640]{1,0:T(8,128)(2,1)S(1)} collective-permute-done((bf16[64,640]{1,0:T(8,128)(2,1)S(1)}, bf16[64,640]{1,0:T(8,128)(2,1)S(1)}, u32[]{:S(2)}, u32[]{:S(2)}) %collective-permute-start.3) | collective-permute-done | bytes 81952 | tf_op jit(solution)/shard_map/ppermute | solution.py:338
  11.5 1.6 %collective-permute-start.5 = (bf16[64,640]{1,0:T(8,128)(2,1)S(1)}, bf16[64,640]{1,0:T(8,128)(2,1)S(1)}, u32[]{:S(2)}, u32[]{:S(2)}) collective-permute-start(bf16[64,640]{1,0:T(8,128)(2,1)S(1)} %get-tuple-element.8), channel_id=1, source_target_pairs={{2,0},{0,2},{6,4},{4,6},{10,8},{8,10},{14,12},{12,14},{3,1},{1,3},... | collective-permute-start | bytes 245768 | tf_op jit(solution)/shard_map/ppermute | solution.py:338
  13.1 0.0 collective-permute-done.2
  13.1 0.6 collective-permute-start.4
  13.7 3.8 %collective-permute-done.4 = bf16[64,640]{1,0:T(8,128)(2,1)S(1)} collective-permute-done((bf16[64,640]{1,0:T(8,128)(2,1)S(1)}, bf16[64,640]{1,0:T(8,128)(2,1)S(1)}, u32[]{:S(2)}, u32[]{:S(2)}) %collective-permute-start.4) | collective-permute-done | bytes 81952 | tf_op jit(solution)/shard_map/ppermute | solution.py:338
  17.5 0.5 collective-permute-start.7
  18.0 0.0 collective-permute-done.5
  18.0 1.6 %collective-permute-start.6 = (bf16[64,640]{1,0:T(8,128)(2,1)S(1)}, bf16[64,640]{1,0:T(8,128)(2,1)S(1)}, u32[]{:S(2)}, u32[]{:S(2)}) collective-permute-start(bf16[64,640]{1,0:T(8,128)(2,1)S(1)} %collective-permute-done.2), channel_id=1, source_target_pairs={{2,0},{0,2},{6,4},{4,6},{10,8},{8,10},{14,12},{12,14},{3,1},{1,3},... | collective-permute-start | bytes 245768 | tf_op jit(solution)/shard_map/ppermute | solution.py:338
  19.6 3.2 %collective-permute-done.6 = bf16[64,640]{1,0:T(8,128)(2,1)S(1)} collective-permute-done((bf16[64,640]{1,0:T(8,128)(2,1)S(1)}, bf16[64,640]{1,0:T(8,128)(2,1)S(1)}, u32[]{:S(2)}, u32[]{:S(2)}) %collective-permute-start.6) | collective-permute-done | bytes 81952 | tf_op jit(solution)/shard_map/ppermute | solution.py:338
  22.8 0.0 collective-permute-start.9
  22.8 1.3 %collective-permute-start.8 = (bf16[64,640]{1,0:T(8,128)(2,1)S(1)}, bf16[64,640]{1,0:T(8,128)(2,1)S(1)}, u32[]{:S(2)}, u32[]{:S(2)}) collective-permute-start(bf16[64,640]{1,0:T(8,128)(2,1)S(1)} %collective-permute-done.4), channel_id=1, source_target_pairs={{2,0},{0,2},{6,4},{4,6},{10,8},{8,10},{14,12},{12,14},{3,1},{1,3},... | collective-permute-start | bytes 245768 | tf_op jit(solution)/shard_map/ppermute | solution.py:338
  24.2 3.6 %collective-permute-done.8 = bf16[64,640]{1,0:T(8,128)(2,1)S(1)} collective-permute-done((bf16[64,640]{1,0:T(8,128)(2,1)S(1)}, bf16[64,640]{1,0:T(8,128)(2,1)S(1)}, u32[]{:S(2)}, u32[]{:S(2)}) %collective-permute-start.8) | collective-permute-done | bytes 81952 | tf_op jit(solution)/shard_map/ppermute | solution.py:338
  27.8 0.1 collective-permute-start.10
  27.9 0.0 copy-start.1
  27.9 1.1 %copy-done.1 = bf16[64,6144]{1,0:T(8,128)(2,1)S(1)} copy-done((bf16[64,6144]{1,0:T(8,128)(2,1)S(1)}, bf16[64,6144]{1,0:T(8,128)(2,1)}, u32[]{:S(2)}) %copy-start.1) | copy-done | bytes 786456
  29.0 1.6 %copy-done.3 = bf16[16,128,512]{2,1,0:T(8,128)(2,1)S(1)} copy-done((bf16[16,128,512]{2,1,0:T(8,128)(2,1)S(1)}, bf16[16,128,512]{2,1,0:T(8,128)(2,1)}, u32[]{:S(2)}) %copy-start.3) | copy-done | bytes 2097176
  30.6 0.9 %lift.3.query_rows = bf16[1024,640]{1,0:T(8,128)(2,1)S(1)} custom-call(bf16[64,6144]{1,0:T(8,128)(2,1)S(1)} %copy-done.1, bf16[16,128,512]{2,1,0:T(8,128)(2,1)S(1)} %copy-done.3), custom_call_target="tpu_custom_call" | custom-call | flops 134217728 | bytes 3801088 | tf_op jit(solution)/shard_map/lift/pallas_call | solution.py:114
  31.6 0.6 copy-done.4
  32.2 3.9 %attend.3.refs_0_ = bf16[64,2048]{1,0:T(8,128)(2,1)S(1)} custom-call(bf16[1024,640]{1,0:T(8,128)(2,1)S(1)} %lift.3.query_rows, bf16[16,512,128]{2,1,0:T(8,128)(2,1)S(1)} %copy-done.4, bf16[128,640]{1,0:T(8,128)(2,1)S(1)} %get-tuple-element.7.rest_0_, bf16[256,640]{1,0:T(8,128)(2,1)S(1)} %constant_dynamic-update-slice_fusion.rest_1_, ...), custom_call_target="tpu_custom_call" | custom-call | flops 2550136832 | bytes 4980736 | tf_op jit(solution)/shard_map/attend/pallas_call | solution.py:192
  36.1 0.9 collective-permute-start.20
  37.0 1.2 %collective-permute-start.24 = (bf16[64,2048]{1,0:T(8,128)(2,1)S(1)}, bf16[64,2048]{1,0:T(8,128)(2,1)S(1)}, u32[]{:S(2)}, u32[]{:S(2)}) collective-permute-start(bf16[64,2048]{1,0:T(8,128)(2,1)S(1)} %attend.3.refs_0_), channel_id=1, source_target_pairs={{4,0},{8,4},{12,8},{14,12},{10,14},{6,10},{2,6},{0,2},{5,1},{9,5},... | collective-permute-start | bytes 786440 | tf_op jit(solution)/shard_map/ppermute | solution.py:369
  38.2 0.9 %lift.2.query_rows = bf16[1024,640]{1,0:T(8,128)(2,1)S(1)} custom-call(bf16[64,6144]{1,0:T(8,128)(2,1)S(1)} %copy-done.2, bf16[16,128,512]{2,1,0:T(8,128)(2,1)S(1)} %collective-permute-done.key_up), custom_call_target="tpu_custom_call" | custom-call | flops 134217728 | bytes 3801088 | tf_op jit(solution)/shard_map/lift/pallas_call | solution.py:114
  39.2 0.0 copy-start
  39.2 4.0 %attend.2.refs_0_ = bf16[64,2048]{1,0:T(8,128)(2,1)S(1)} custom-call(bf16[1024,640]{1,0:T(8,128)(2,1)S(1)} %lift.2.query_rows, bf16[16,512,128]{2,1,0:T(8,128)(2,1)S(1)} %collective-permute-done.1.value_up, bf16[128,640]{1,0:T(8,128)(2,1)S(1)} %get-tuple-element.7.rest_0_, bf16[256,640]{1,0:T(8,128)(2,1)S(1)} %constant_dynamic-update-slice_fusion.rest_1_, ...), custom_call_target="tpu_custom_call" | custom-call | flops 2550136832 | bytes 4980736 | tf_op jit(solution)/shard_map/attend/pallas_call | solution.py:192
  43.2 0.9 collective-permute-start.11
  44.0 1.2 %collective-permute-start.15 = (bf16[64,2048]{1,0:T(8,128)(2,1)S(1)}, bf16[64,2048]{1,0:T(8,128)(2,1)S(1)}, u32[]{:S(2)}, u32[]{:S(2)}) collective-permute-start(bf16[64,2048]{1,0:T(8,128)(2,1)S(1)} %attend.2.refs_0_), channel_id=1, source_target_pairs={{4,0},{8,4},{12,8},{14,12},{10,14},{6,10},{2,6},{0,2},{5,1},{9,5},... | collective-permute-start | bytes 786440 | tf_op jit(solution)/shard_map/ppermute | solution.py:369
  45.2 0.8 collective-permute-start.21
  46.0 1.2 %collective-permute-start.25 = (bf16[64,2048]{1,0:T(8,128)(2,1)S(1)}, bf16[64,2048]{1,0:T(8,128)(2,1)S(1)}, u32[]{:S(2)}, u32[]{:S(2)}) collective-permute-start(bf16[64,2048]{1,0:T(8,128)(2,1)S(1)} %collective-permute-done.24.refs_1_), channel_id=1, source_target_pairs={{4,0},{8,4},{12,8},{14,12},{10,14},{6,10},{2,6},{0,2},{5,1},{9,5},... | collective-permute-start | bytes 786440 | tf_op jit(solution)/shard_map/ppermute | solution.py:369
  47.3 5.1 %collective-permute-done.11.refs_0_ = bf16[64,2048]{1,0:T(8,128)(2,1)S(1)} collective-permute-done((bf16[64,2048]{1,0:T(8,128)(2,1)S(1)}, bf16[64,2048]{1,0:T(8,128)(2,1)S(1)}, u32[]{:S(2)}, u32[]{:S(2)}) %collective-permute-start.11) | collective-permute-done | bytes 262176 | tf_op jit(solution)/shard_map/ppermute | solution.py:369
  52.4 0.8 collective-permute-start.12
  53.2 1.2 %collective-permute-start.16 = (bf16[64,2048]{1,0:T(8,128)(2,1)S(1)}, bf16[64,2048]{1,0:T(8,128)(2,1)S(1)}, u32[]{:S(2)}, u32[]{:S(2)}) collective-permute-start(bf16[64,2048]{1,0:T(8,128)(2,1)S(1)} %collective-permute-done.15.refs_1_), channel_id=1, source_target_pairs={{4,0},{8,4},{12,8},{14,12},{10,14},{6,10},{2,6},{0,2},{5,1},{9,5},... | collective-permute-start | bytes 786440 | tf_op jit(solution)/shard_map/ppermute | solution.py:369
  54.4 3.6 %collective-permute-done.21.refs_0_ = bf16[64,2048]{1,0:T(8,128)(2,1)S(1)} collective-permute-done((bf16[64,2048]{1,0:T(8,128)(2,1)S(1)}, bf16[64,2048]{1,0:T(8,128)(2,1)S(1)}, u32[]{:S(2)}, u32[]{:S(2)}) %collective-permute-start.21) | collective-permute-done | bytes 262176 | tf_op jit(solution)/shard_map/ppermute | solution.py:369
  58.0 0.8 collective-permute-start.22
  58.8 0.0 collective-permute-done.25.refs_1_
  58.8 1.2 %collective-permute-start.26 = (bf16[64,2048]{1,0:T(8,128)(2,1)S(1)}, bf16[64,2048]{1,0:T(8,128)(2,1)S(1)}, u32[]{:S(2)}, u32[]{:S(2)}) collective-permute-start(bf16[64,2048]{1,0:T(8,128)(2,1)S(1)} %collective-permute-done.25.refs_1_), channel_id=1, source_target_pairs={{4,0},{8,4},{12,8},{14,12},{10,14},{6,10},{2,6},{0,2},{5,1},{9,5},... | collective-permute-start | bytes 786440 | tf_op jit(solution)/shard_map/ppermute | solution.py:369
  60.0 3.6 %collective-permute-done.12.refs_0_ = bf16[64,2048]{1,0:T(8,128)(2,1)S(1)} collective-permute-done((bf16[64,2048]{1,0:T(8,128)(2,1)S(1)}, bf16[64,2048]{1,0:T(8,128)(2,1)S(1)}, u32[]{:S(2)}, u32[]{:S(2)}) %collective-permute-start.12) | collective-permute-done | bytes 262176 | tf_op jit(solution)/shard_map/ppermute | solution.py:369
  63.6 0.8 collective-permute-start.13
  64.4 1.2 %collective-permute-start.17 = (bf16[64,2048]{1,0:T(8,128)(2,1)S(1)}, bf16[64,2048]{1,0:T(8,128)(2,1)S(1)}, u32[]{:S(2)}, u32[]{:S(2)}) collective-permute-start(bf16[64,2048]{1,0:T(8,128)(2,1)S(1)} %collective-permute-done.16.refs_1_), channel_id=1, source_target_pairs={{4,0},{8,4},{12,8},{14,12},{10,14},{6,10},{2,6},{0,2},{5,1},{9,5},... | collective-permute-start | bytes 786440 | tf_op jit(solution)/shard_map/ppermute | solution.py:369
  65.7 0.6 touch.1
  66.3 0.7 project.14.refs_2_
  67.0 2.3 %collective-permute-done.22.refs_0_ = bf16[64,2048]{1,0:T(8,128)(2,1)S(1)} collective-permute-done((bf16[64,2048]{1,0:T(8,128)(2,1)S(1)}, bf16[64,2048]{1,0:T(8,128)(2,1)S(1)}, u32[]{:S(2)}, u32[]{:S(2)}) %collective-permute-start.22) | collective-permute-done | bytes 262176 | tf_op jit(solution)/shard_map/ppermute | solution.py:369
  69.3 0.9 collective-permute-start.23
  70.1 1.3 %collective-permute-start.27 = (bf16[64,1024]{1,0:T(8,128)(2,1)S(1)}, bf16[64,1024]{1,0:T(8,128)(2,1)S(1)}, u32[]{:S(2)}, u32[]{:S(2)}) collective-permute-start(bf16[64,1024]{1,0:T(8,128)(2,1)S(1)} %slice.19), channel_id=1, source_target_pairs={{4,0},{8,4},{12,8},{14,12},{10,14},{6,10},{2,6},{0,2},{5,1},{9,5},... | collective-permute-start | bytes 393224 | tf_op jit(solution)/shard_map/ppermute | solution.py:369
  71.4 0.7 project.13.refs_3_
  72.1 0.7 project.12.refs_3_
  72.9 0.7 project.11.refs_3_
  73.6 3.1 %collective-permute-done.23.refs_0_ = bf16[64,1024]{1,0:T(8,128)(2,1)S(1)} collective-permute-done((bf16[64,1024]{1,0:T(8,128)(2,1)S(1)}, bf16[64,1024]{1,0:T(8,128)(2,1)S(1)}, u32[]{:S(2)}, u32[]{:S(2)}) %collective-permute-start.23) | collective-permute-done | bytes 131104 | tf_op jit(solution)/shard_map/ppermute | solution.py:369
  76.6 0.8 collective-permute-done.27.refs_1_
  77.4 0.7 project.10.refs_3_
  78.2 1.8 %collective-permute-start.14 = (bf16[64,1024]{1,0:T(8,128)(2,1)S(1)}, bf16[64,1024]{1,0:T(8,128)(2,1)S(1)}, u32[]{:S(2)}, u32[]{:S(2)}) collective-permute-start(bf16[64,1024]{1,0:T(8,128)(2,1)S(1)} %slice.16), channel_id=1, source_target_pairs={{0,4},{4,8},{8,12},{12,14},{14,10},{10,6},{6,2},{2,0},{1,5},{5,9},... | collective-permute-start | bytes 393224 | tf_op jit(solution)/shard_map/ppermute | solution.py:369
  80.0 0.5 collective-permute-start.18
  80.5 1.4 %project.15.refs_4_ = bf16[8,1,64,896]{3,2,1,0:T(8,128)(2,1)} custom-call(bf16[64,2048]{1,0:T(8,128)(2,1)S(1)} %attend.2.refs_0_, bf16[2048,896]{1,0:T(8,128)(2,1)S(1)} %collective-permute-done.19.refs_1_.refs_2_, f32[64,896]{1,0:T(8,128)S(1)} %project.14.refs_2_), custom_call_target="tpu_custom_call" | custom-call | flops 234881024 | bytes 3670016 | tf_op jit(solution)/shard_map/project/pallas_call | solution.py:278
  81.9 1.4 %project.16.refs_4_ = bf16[8,1,64,896]{3,2,1,0:T(8,128)(2,1)} custom-call(bf16[64,2048]{1,0:T(8,128)(2,1)S(1)} %collective-permute-done.11.refs_0_, bf16[64,2048]{1,0:T(8,128)(2,1)S(1)} %collective-permute-done.15.refs_1_, bf16[2048,896]{1,0:T(8,128)(2,1)S(1)} %collective-permute-done.19.refs_1_.refs_2_, ...), custom_call_target="tpu_custom_call", output_to_operand_aliasing={{}: (4, {})} | custom-call | flops 469762048 | bytes 3670016 | tf_op jit(solution)/shard_map/project/pallas_call | solution.py:278
  83.3 1.4 %project.17.refs_4_ = bf16[8,1,64,896]{3,2,1,0:T(8,128)(2,1)} custom-call(bf16[64,2048]{1,0:T(8,128)(2,1)S(1)} %collective-permute-done.12.refs_0_, bf16[64,2048]{1,0:T(8,128)(2,1)S(1)} %collective-permute-done.16.refs_1_, bf16[2048,896]{1,0:T(8,128)(2,1)S(1)} %collective-permute-done.19.refs_1_.refs_2_, ...), custom_call_target="tpu_custom_call", output_to_operand_aliasing={{}: (4, {})} | custom-call | flops 469762048 | bytes 3670016 | tf_op jit(solution)/shard_map/project/pallas_call | solution.py:278
  84.8 1.4 %project.18.refs_4_ = bf16[8,1,64,896]{3,2,1,0:T(8,128)(2,1)} custom-call(bf16[64,2048]{1,0:T(8,128)(2,1)S(1)} %collective-permute-done.13.refs_0_, bf16[64,2048]{1,0:T(8,128)(2,1)S(1)} %collective-permute-done.17.refs_1_, bf16[2048,896]{1,0:T(8,128)(2,1)S(1)} %collective-permute-done.19.refs_1_.refs_2_, ...), custom_call_target="tpu_custom_call", output_to_operand_aliasing={{}: (4, {})} | custom-call | flops 469762048 | bytes 3670016 | tf_op jit(solution)/shard_map/project/pallas_call | solution.py:278
  86.2 1.4 %project.19 = bf16[8,1,64,896]{3,2,1,0:T(8,128)(2,1)} custom-call(bf16[64,1024]{1,0:T(8,128)(2,1)S(1)} %collective-permute-done.14.refs_0_, bf16[64,1024]{1,0:T(8,128)(2,1)S(1)} %collective-permute-done.18.refs_1_, bf16[2048,896]{1,0:T(8,128)(2,1)S(1)} %collective-permute-done.19.refs_1_.refs_2_, ...), custom_call_target="tpu_custom_call", output_to_operand_aliasing={{}: (4, {})} | custom-call | flops 234881024 | bytes 3670016 | tf_op jit(solution)/shard_map/project/pallas_call | solution.py:278
  (33 shorter events, 0.2 us)
Async XLA Ops:
  0.0 80.5 %collective-permute-start.19 = (bf16[2048,896]{1,0:T(8,128)(2,1)}, bf16[2048,896]{1,0:T(8,128)(2,1)S(1)}, u32[]{:S(2)}, u32[]{:S(2)}) collective-permute-start(bf16[2048,896]{1,0:T(8,128)(2,1)} %refs_1_.1), channel_id=1, source_target_pairs={{0,1},{1,0},{2,3},{3,2},{4,5},{5,4},{6,7},{7,6},{8,9},{9,8},{10,11... | collective-permute-start | bytes 11010056 | tf_op jit(solution)/shard_map/ppermute | solution.py:349
  0.5 37.7 %collective-permute-start = (bf16[16,128,512]{2,1,0:T(8,128)(2,1)}, bf16[16,128,512]{2,1,0:T(8,128)(2,1)S(1)}, u32[]{:S(2)}, u32[]{:S(2)}) collective-permute-start(bf16[16,128,512]{2,1,0:T(8,128)(2,1)} %key_up.1), channel_id=1, source_target_pairs={{0,1},{1,0},{2,3},{3,2},{4,5},{5,4},{6,7},{7,6},{8,9},{9,8},{10,11... | collective-permute-start | bytes 6291464 | tf_op jit(solution)/shard_map/ppermute | solution.py:347
  0.5 38.7 %collective-permute-start.1 = (bf16[16,512,128]{2,1,0:T(8,128)(2,1)}, bf16[16,512,128]{2,1,0:T(8,128)(2,1)S(1)}, u32[]{:S(2)}, u32[]{:S(2)}) collective-permute-start(bf16[16,512,128]{2,1,0:T(8,128)(2,1)} %value_up.1), channel_id=1, source_target_pairs={{0,1},{1,0},{2,3},{3,2},{4,5},{5,4},{6,7},{7,6},{8,9},{9,8},{10,11... | collective-permute-start | bytes 6291464 | tf_op jit(solution)/shard_map/ppermute | solution.py:348
  1.0 0.9 %copy-start.5 = (bf16[128,576]{0,1:T(8,128)(2,1)S(1)}, bf16[128,576]{0,1:T(8,128)(2,1)}, u32[]{:S(2)}) copy-start(bf16[128,576]{0,1:T(8,128)(2,1)} %param.7) | copy-start | bytes 442372
  1.9 0.7 copy-start.6
  2.9 8.6 %collective-permute-start.3 = (bf16[64,640]{1,0:T(8,128)(2,1)S(1)}, bf16[64,640]{1,0:T(8,128)(2,1)S(1)}, u32[]{:S(2)}, u32[]{:S(2)}) collective-permute-start(bf16[64,640]{1,0:T(8,128)(2,1)S(1)} %get-tuple-element.8), channel_id=1, source_target_pairs={{8,0},{10,2},{12,4},{14,6},{0,8},{2,10},{4,12},{6,14},{9,1},{11,3}... | collective-permute-start | bytes 245768 | tf_op jit(solution)/shard_map/ppermute | solution.py:338
  6.5 6.5 %collective-permute-start.2 = (bf16[64,640]{1,0:T(8,128)(2,1)S(1)}, bf16[64,640]{1,0:T(8,128)(2,1)S(1)}, u32[]{:S(2)}, u32[]{:S(2)}) collective-permute-start(bf16[64,640]{1,0:T(8,128)(2,1)S(1)} %get-tuple-element.8), channel_id=1, source_target_pairs={{4,0},{6,2},{0,4},{2,6},{12,8},{14,10},{8,12},{10,14},{5,1},{7,3},... | collective-permute-start | bytes 245768 | tf_op jit(solution)/shard_map/ppermute | solution.py:338
  11.5 6.5 %collective-permute-start.5 = (bf16[64,640]{1,0:T(8,128)(2,1)S(1)}, bf16[64,640]{1,0:T(8,128)(2,1)S(1)}, u32[]{:S(2)}, u32[]{:S(2)}) collective-permute-start(bf16[64,640]{1,0:T(8,128)(2,1)S(1)} %get-tuple-element.8), channel_id=1, source_target_pairs={{2,0},{0,2},{6,4},{4,6},{10,8},{8,10},{14,12},{12,14},{3,1},{1,3},... | collective-permute-start | bytes 245768 | tf_op jit(solution)/shard_map/ppermute | solution.py:338
  13.1 4.4 %collective-permute-start.4 = (bf16[64,640]{1,0:T(8,128)(2,1)S(1)}, bf16[64,640]{1,0:T(8,128)(2,1)S(1)}, u32[]{:S(2)}, u32[]{:S(2)}) collective-permute-start(bf16[64,640]{1,0:T(8,128)(2,1)S(1)} %collective-permute-done.3), channel_id=1, source_target_pairs={{4,0},{6,2},{0,4},{2,6},{12,8},{14,10},{8,12},{10,14},{5,1},{7,3},... | collective-permute-start | bytes 245768 | tf_op jit(solution)/shard_map/ppermute | solution.py:338
  17.5 5.3 %collective-permute-start.7 = (bf16[64,640]{1,0:T(8,128)(2,1)S(1)}, bf16[64,640]{1,0:T(8,128)(2,1)S(1)}, u32[]{:S(2)}, u32[]{:S(2)}) collective-permute-start(bf16[64,640]{1,0:T(8,128)(2,1)S(1)} %collective-permute-done.3), channel_id=1, source_target_pairs={{2,0},{0,2},{6,4},{4,6},{10,8},{8,10},{14,12},{12,14},{3,1},{1,3},... | collective-permute-start | bytes 245768 | tf_op jit(solution)/shard_map/ppermute | solution.py:338
  18.0 4.8 %collective-permute-start.6 = (bf16[64,640]{1,0:T(8,128)(2,1)S(1)}, bf16[64,640]{1,0:T(8,128)(2,1)S(1)}, u32[]{:S(2)}, u32[]{:S(2)}) collective-permute-start(bf16[64,640]{1,0:T(8,128)(2,1)S(1)} %collective-permute-done.2), channel_id=1, source_target_pairs={{2,0},{0,2},{6,4},{4,6},{10,8},{8,10},{14,12},{12,14},{3,1},{1,3},... | collective-permute-start | bytes 245768 | tf_op jit(solution)/shard_map/ppermute | solution.py:338
  22.8 8.7 %collective-permute-start.9 = (bf16[256,640]{1,0:T(8,128)(2,1)S(1)}, bf16[256,640]{1,0:T(8,128)(2,1)S(1)}, u32[]{:S(2)}, u32[]{:S(2)}) collective-permute-start(bf16[256,640]{1,0:T(8,128)(2,1)S(1)} %constant_dynamic-update-slice_fusion.rest_1_), channel_id=1, source_target_pairs={{0,1},{1,0},{2,3},{3,2},{4,5},{5,4},{6,7},{7,6},{8,9},{9,8},{10,11... | collective-permute-start | bytes 983048 | tf_op jit(solution)/shard_map/ppermute | solution.py:343
  22.8 4.9 %collective-permute-start.8 = (bf16[64,640]{1,0:T(8,128)(2,1)S(1)}, bf16[64,640]{1,0:T(8,128)(2,1)S(1)}, u32[]{:S(2)}, u32[]{:S(2)}) collective-permute-start(bf16[64,640]{1,0:T(8,128)(2,1)S(1)} %collective-permute-done.4), channel_id=1, source_target_pairs={{2,0},{0,2},{6,4},{4,6},{10,8},{8,10},{14,12},{12,14},{3,1},{1,3},... | collective-permute-start | bytes 245768 | tf_op jit(solution)/shard_map/ppermute | solution.py:338
  27.8 3.8 %collective-permute-start.10 = (bf16[192,640]{1,0:T(8,128)(2,1)S(1)}, bf16[192,640]{1,0:T(8,128)(2,1)S(1)}, u32[]{:S(2)}, u32[]{:S(2)}) collective-permute-start(bf16[192,640]{1,0:T(8,128)(2,1)S(1)} %constant_dynamic-update-slice_fusion.4.rest_2_), channel_id=1, source_target_pairs={{0,1},{1,0},{2,3},{3,2},{4,5},{5,4},{6,7},{7,6},{8,9},{9,8},{10,11... | collective-permute-start | bytes 737288 | tf_op jit(solution)/shard_map/ppermute | solution.py:344
  27.9 1.1 %copy-start.1 = (bf16[64,6144]{1,0:T(8,128)(2,1)S(1)}, bf16[64,6144]{1,0:T(8,128)(2,1)}, u32[]{:S(2)}) copy-start(bf16[64,6144]{1,0:T(8,128)(2,1)} %queries.3) | copy-start | bytes 2359300
  29.0 1.6 %copy-start.3 = (bf16[16,128,512]{2,1,0:T(8,128)(2,1)S(1)}, bf16[16,128,512]{2,1,0:T(8,128)(2,1)}, u32[]{:S(2)}) copy-start(bf16[16,128,512]{2,1,0:T(8,128)(2,1)} %key_up.1) | copy-start | bytes 6291460
  30.6 1.6 %copy-start.4 = (bf16[16,512,128]{2,1,0:T(8,128)(2,1)S(1)}, bf16[16,512,128]{2,1,0:T(8,128)(2,1)}, u32[]{:S(2)}) copy-start(bf16[16,512,128]{2,1,0:T(8,128)(2,1)} %value_up.1) | copy-start | bytes 6291460
  32.2 6.0 %copy-start.2 = (bf16[64,6144]{1,0:T(8,128)(2,1)S(1)}, bf16[64,6144]{1,0:T(8,128)(2,1)}, u32[]{:S(2)}) copy-start(bf16[64,6144]{1,0:T(8,128)(2,1)} %queries.3) | copy-start | bytes 2359300
  36.1 9.1 %collective-permute-start.20 = (bf16[64,2048]{1,0:T(8,128)(2,1)S(1)}, bf16[64,2048]{1,0:T(8,128)(2,1)S(1)}, u32[]{:S(2)}, u32[]{:S(2)}) collective-permute-start(bf16[64,2048]{1,0:T(8,128)(2,1)S(1)} %attend.3.refs_0_), channel_id=1, source_target_pairs={{0,4},{4,8},{8,12},{12,14},{14,10},{10,6},{6,2},{2,0},{1,5},{5,9},... | collective-permute-start | bytes 786440 | tf_op jit(solution)/shard_map/ppermute | solution.py:369
  37.0 9.1 %collective-permute-start.24 = (bf16[64,2048]{1,0:T(8,128)(2,1)S(1)}, bf16[64,2048]{1,0:T(8,128)(2,1)S(1)}, u32[]{:S(2)}, u32[]{:S(2)}) collective-permute-start(bf16[64,2048]{1,0:T(8,128)(2,1)S(1)} %attend.3.refs_0_), channel_id=1, source_target_pairs={{4,0},{8,4},{12,8},{14,12},{10,14},{6,10},{2,6},{0,2},{5,1},{9,5},... | collective-permute-start | bytes 786440 | tf_op jit(solution)/shard_map/ppermute | solution.py:369
  39.2 27.1 %copy-start = (bf16[2048,896]{1,0:T(8,128)(2,1)S(1)}, bf16[2048,896]{1,0:T(8,128)(2,1)}, u32[]{:S(2)}) copy-start(bf16[2048,896]{1,0:T(8,128)(2,1)} %refs_1_.1) | copy-start | bytes 11010052
  43.2 9.2 %collective-permute-start.11 = (bf16[64,2048]{1,0:T(8,128)(2,1)S(1)}, bf16[64,2048]{1,0:T(8,128)(2,1)S(1)}, u32[]{:S(2)}, u32[]{:S(2)}) collective-permute-start(bf16[64,2048]{1,0:T(8,128)(2,1)S(1)} %attend.2.refs_0_), channel_id=1, source_target_pairs={{0,4},{4,8},{8,12},{12,14},{14,10},{10,6},{6,2},{2,0},{1,5},{5,9},... | collective-permute-start | bytes 786440 | tf_op jit(solution)/shard_map/ppermute | solution.py:369
  44.0 9.2 %collective-permute-start.15 = (bf16[64,2048]{1,0:T(8,128)(2,1)S(1)}, bf16[64,2048]{1,0:T(8,128)(2,1)S(1)}, u32[]{:S(2)}, u32[]{:S(2)}) collective-permute-start(bf16[64,2048]{1,0:T(8,128)(2,1)S(1)} %attend.2.refs_0_), channel_id=1, source_target_pairs={{4,0},{8,4},{12,8},{14,12},{10,14},{6,10},{2,6},{0,2},{5,1},{9,5},... | collective-permute-start | bytes 786440 | tf_op jit(solution)/shard_map/ppermute | solution.py:369
  45.2 12.8 %collective-permute-start.21 = (bf16[64,2048]{1,0:T(8,128)(2,1)S(1)}, bf16[64,2048]{1,0:T(8,128)(2,1)S(1)}, u32[]{:S(2)}, u32[]{:S(2)}) collective-permute-start(bf16[64,2048]{1,0:T(8,128)(2,1)S(1)} %collective-permute-done.20.refs_0_), channel_id=1, source_target_pairs={{0,4},{4,8},{8,12},{12,14},{14,10},{10,6},{6,2},{2,0},{1,5},{5,9},... | collective-permute-start | bytes 786440 | tf_op jit(solution)/shard_map/ppermute | solution.py:369
  46.0 12.8 %collective-permute-start.25 = (bf16[64,2048]{1,0:T(8,128)(2,1)S(1)}, bf16[64,2048]{1,0:T(8,128)(2,1)S(1)}, u32[]{:S(2)}, u32[]{:S(2)}) collective-permute-start(bf16[64,2048]{1,0:T(8,128)(2,1)S(1)} %collective-permute-done.24.refs_1_), channel_id=1, source_target_pairs={{4,0},{8,4},{12,8},{14,12},{10,14},{6,10},{2,6},{0,2},{5,1},{9,5},... | collective-permute-start | bytes 786440 | tf_op jit(solution)/shard_map/ppermute | solution.py:369
  52.4 11.2 %collective-permute-start.12 = (bf16[64,2048]{1,0:T(8,128)(2,1)S(1)}, bf16[64,2048]{1,0:T(8,128)(2,1)S(1)}, u32[]{:S(2)}, u32[]{:S(2)}) collective-permute-start(bf16[64,2048]{1,0:T(8,128)(2,1)S(1)} %collective-permute-done.11.refs_0_), channel_id=1, source_target_pairs={{0,4},{4,8},{8,12},{12,14},{14,10},{10,6},{6,2},{2,0},{1,5},{5,9},... | collective-permute-start | bytes 786440 | tf_op jit(solution)/shard_map/ppermute | solution.py:369
  53.2 11.2 %collective-permute-start.16 = (bf16[64,2048]{1,0:T(8,128)(2,1)S(1)}, bf16[64,2048]{1,0:T(8,128)(2,1)S(1)}, u32[]{:S(2)}, u32[]{:S(2)}) collective-permute-start(bf16[64,2048]{1,0:T(8,128)(2,1)S(1)} %collective-permute-done.15.refs_1_), channel_id=1, source_target_pairs={{4,0},{8,4},{12,8},{14,12},{10,14},{6,10},{2,6},{0,2},{5,1},{9,5},... | collective-permute-start | bytes 786440 | tf_op jit(solution)/shard_map/ppermute | solution.py:369
  58.0 11.2 %collective-permute-start.22 = (bf16[64,2048]{1,0:T(8,128)(2,1)S(1)}, bf16[64,2048]{1,0:T(8,128)(2,1)S(1)}, u32[]{:S(2)}, u32[]{:S(2)}) collective-permute-start(bf16[64,2048]{1,0:T(8,128)(2,1)S(1)} %collective-permute-done.21.refs_0_), channel_id=1, source_target_pairs={{0,4},{4,8},{8,12},{12,14},{14,10},{10,6},{6,2},{2,0},{1,5},{5,9},... | collective-permute-start | bytes 786440 | tf_op jit(solution)/shard_map/ppermute | solution.py:369
  58.8 11.3 %collective-permute-start.26 = (bf16[64,2048]{1,0:T(8,128)(2,1)S(1)}, bf16[64,2048]{1,0:T(8,128)(2,1)S(1)}, u32[]{:S(2)}, u32[]{:S(2)}) collective-permute-start(bf16[64,2048]{1,0:T(8,128)(2,1)S(1)} %collective-permute-done.25.refs_1_), channel_id=1, source_target_pairs={{4,0},{8,4},{12,8},{14,12},{10,14},{6,10},{2,6},{0,2},{5,1},{9,5},... | collective-permute-start | bytes 786440 | tf_op jit(solution)/shard_map/ppermute | solution.py:369
  63.6 14.5 %collective-permute-start.13 = (bf16[64,2048]{1,0:T(8,128)(2,1)S(1)}, bf16[64,2048]{1,0:T(8,128)(2,1)S(1)}, u32[]{:S(2)}, u32[]{:S(2)}) collective-permute-start(bf16[64,2048]{1,0:T(8,128)(2,1)S(1)} %collective-permute-done.12.refs_0_), channel_id=1, source_target_pairs={{0,4},{4,8},{8,12},{12,14},{14,10},{10,6},{6,2},{2,0},{1,5},{5,9},... | collective-permute-start | bytes 786440 | tf_op jit(solution)/shard_map/ppermute | solution.py:369
  64.4 15.5 %collective-permute-start.17 = (bf16[64,2048]{1,0:T(8,128)(2,1)S(1)}, bf16[64,2048]{1,0:T(8,128)(2,1)S(1)}, u32[]{:S(2)}, u32[]{:S(2)}) collective-permute-start(bf16[64,2048]{1,0:T(8,128)(2,1)S(1)} %collective-permute-done.16.refs_1_), channel_id=1, source_target_pairs={{4,0},{8,4},{12,8},{14,12},{10,14},{6,10},{2,6},{0,2},{5,1},{9,5},... | collective-permute-start | bytes 786440 | tf_op jit(solution)/shard_map/ppermute | solution.py:369
  69.3 7.4 %collective-permute-start.23 = (bf16[64,1024]{1,0:T(8,128)(2,1)S(1)}, bf16[64,1024]{1,0:T(8,128)(2,1)S(1)}, u32[]{:S(2)}, u32[]{:S(2)}) collective-permute-start(bf16[64,1024]{1,0:T(8,128)(2,1)S(1)} %slice.18), channel_id=1, source_target_pairs={{0,4},{4,8},{8,12},{12,14},{14,10},{10,6},{6,2},{2,0},{1,5},{5,9},... | collective-permute-start | bytes 393224 | tf_op jit(solution)/shard_map/ppermute | solution.py:369
  70.1 7.3 %collective-permute-start.27 = (bf16[64,1024]{1,0:T(8,128)(2,1)S(1)}, bf16[64,1024]{1,0:T(8,128)(2,1)S(1)}, u32[]{:S(2)}, u32[]{:S(2)}) collective-permute-start(bf16[64,1024]{1,0:T(8,128)(2,1)S(1)} %slice.19), channel_id=1, source_target_pairs={{4,0},{8,4},{12,8},{14,12},{10,14},{6,10},{2,6},{0,2},{5,1},{9,5},... | collective-permute-start | bytes 393224 | tf_op jit(solution)/shard_map/ppermute | solution.py:369
  78.2 8.0 %collective-permute-start.14 = (bf16[64,1024]{1,0:T(8,128)(2,1)S(1)}, bf16[64,1024]{1,0:T(8,128)(2,1)S(1)}, u32[]{:S(2)}, u32[]{:S(2)}) collective-permute-start(bf16[64,1024]{1,0:T(8,128)(2,1)S(1)} %slice.16), channel_id=1, source_target_pairs={{0,4},{4,8},{8,12},{12,14},{14,10},{10,6},{6,2},{2,0},{1,5},{5,9},... | collective-permute-start | bytes 393224 | tf_op jit(solution)/shard_map/ppermute | solution.py:369
  80.0 6.2 %collective-permute-start.18 = (bf16[64,1024]{1,0:T(8,128)(2,1)S(1)}, bf16[64,1024]{1,0:T(8,128)(2,1)S(1)}, u32[]{:S(2)}, u32[]{:S(2)}) collective-permute-start(bf16[64,1024]{1,0:T(8,128)(2,1)S(1)} %slice.17), channel_id=1, source_target_pairs={{4,0},{8,4},{12,8},{14,12},{10,14},{6,10},{2,6},{0,2},{5,1},{9,5},... | collective-permute-start | bytes 393224 | tf_op jit(solution)/shard_map/ppermute | solution.py:369

commit v4 on v3

--- a/solution.py
+++ b/solution.py
@@ -130,12 +130,14 @@
     )(queries, key_up)
 
 
-def attend_kernel(part, groups, query_rows, value_up, *rest):
-    groups, (out, keys) = rest[:groups], rest[groups:]
+def attend_kernel(part, groups, own, earlier, finish, query_rows, *refs):
+    refs = list(refs)
+    value_up = refs.pop(0) if finish else None
+    old_sums, old_stats = (refs.pop(0), refs.pop(0)) if earlier else (None, None)
+    groups, refs = refs[:groups], refs[groups:]
+    keys = refs[-1]
     total = query_rows.shape[0]
-    heads = value_up.shape[0]
-    rows = total // heads
-    own = groups[0].shape[0]
+    rows = total // 8
 
     @pl.when(pl.program_id(0) == 0)
     def _():
@@ -155,17 +157,31 @@
             preferred_element_type=jnp.float32,
         )
 
-    def finish(i, score):
-        query_pos = offset + lax.rem(lax.broadcasted_iota(jnp.int32, (part, own), 0), rows)
-        key_pos = lax.broadcasted_iota(jnp.int32, (part, own), 1)
-        diagonal = jnp.where(key_pos <= query_pos, score[:, :own], HIDDEN)
-        score = jnp.concatenate([diagonal, score[:, own:]], 1)
+    def complete(i, score):
+        here = slice(i * part, (i + 1) * part)
+        if own:
+            query_pos = offset + lax.rem(lax.broadcasted_iota(jnp.int32, (part, own), 0), rows)
+            key_pos = lax.broadcasted_iota(jnp.int32, (part, own), 1)
+            diagonal = jnp.where(key_pos <= query_pos, score[:, :own], HIDDEN)
+            score = jnp.concatenate([diagonal, score[:, own:]], 1)
         peak = jnp.max(score, axis=-1, keepdims=True)
+        if earlier:
+            old_peak = old_stats[here, :1]
+            peak = jnp.maximum(peak, old_peak)
+            carry = jnp.exp2((old_peak - peak) * factor)
         probs = jnp.exp2((score - peak) * factor)
         totals = jnp.sum(probs, axis=-1, keepdims=True)
         sums = jnp.dot(
             probs.astype(jnp.bfloat16), keys[:, :KV], preferred_element_type=jnp.float32
         )
+        if earlier:
+            totals += old_stats[here, 128:129] * carry
+            sums += old_sums[here, :] * carry
+        if not finish:
+            refs[0][here, :] = sums
+            refs[1][here, :128] = jnp.broadcast_to(peak, (part, 128))
+            refs[1][here, 128:] = jnp.broadcast_to(totals, (part, 128))
+            return
         latent_out = (sums / totals).astype(jnp.bfloat16)
         for j in range(part // rows):
             head = i * (part // rows) + j
@@ -174,31 +190,47 @@
                 value_up[head],
                 preferred_element_type=jnp.float32,
             )
-            out[:, head * VD : (head + 1) * VD] = piece.astype(jnp.bfloat16)
+            refs[0][:, head * VD : (head + 1) * VD] = piece.astype(jnp.bfloat16)
 
     count = total // part
     score = score_rows(0)
     for i in range(count):
         later = score_rows(i + 1) if i + 1 < count else None
-        finish(i, score)
+        complete(i, score)
         score = later
 
 
-def attend(query_rows, value_up, keys, rows, blocks):
+def attend(query_rows, keys, rows, blocks, own=0, value_up=None, earlier=()):
     step = 8
     first, count = blocks
     heads = count * step
     key_total = sum(key.shape[0] for key in keys)
+    finish = value_up is not None
+    operands, specs = [query_rows], [pl.BlockSpec((step * rows, WIDE), lambda i: (first + i, 0))]
+    if finish:
+        operands.append(value_up)
+        specs.append(pl.BlockSpec((step, KV, VD), lambda i: (first + i, 0, 0)))
+    for value in earlier:
+        operands.append(value)
+        specs.append(pl.BlockSpec((step * rows, value.shape[1]), lambda i: (i, 0)))
+    operands += keys
+    specs += [pl.BlockSpec(key.shape, lambda i: (0, 0)) for key in keys]
+    if finish:
+        outs = jax.ShapeDtypeStruct((rows, heads * VD), jnp.bfloat16)
+        out_specs = pl.BlockSpec((rows, step * VD), lambda i: (0, i))
+    else:
+        outs = [jax.ShapeDtypeStruct((heads * rows, width), jnp.float32) for width in (KV, 256)]
+        out_specs = [
+            pl.BlockSpec((step * rows, width), lambda i: (i, 0)) for width in (KV, 256)
+        ]
     return pl.pallas_call(
-        functools.partial(attend_kernel, 4 * rows, len(keys)),
+        functools.partial(
+            attend_kernel, 4 * rows, len(keys), own, bool(earlier), finish
+        ),
         grid=(count,),
-        in_specs=[
-            pl.BlockSpec((step * rows, WIDE), lambda i: (first + i, 0)),
-            pl.BlockSpec((step, KV, VD), lambda i: (first + i, 0, 0)),
-        ]
-        + [pl.BlockSpec(key.shape, lambda i: (0, 0)) for key in keys],
-        out_specs=pl.BlockSpec((rows, step * VD), lambda i: (0, i)),
-        out_shape=jax.ShapeDtypeStruct((rows, heads * VD), jnp.bfloat16),
+        in_specs=specs,
+        out_specs=out_specs,
+        out_shape=outs,
         scratch_shapes=[pltpu.VMEM((key_total, WIDE), jnp.bfloat16)],
         cost_estimate=pl.CostEstimate(
             flops=2 * heads * rows * (key_total * (WIDE + KV) + KV * VD),
@@ -206,10 +238,10 @@
             transcendentals=heads * rows * key_total,
         ),
         compiler_params=pltpu.CompilerParams(
-            vmem_limit_bytes=(12 << 20) + 16 * key_total * WIDE
+            vmem_limit_bytes=(16 << 20) + 16 * key_total * WIDE
         ),
         name="attend",
-    )(query_rows, value_up, *keys)
+    )(*operands)
 
 
 def project_kernel(count, offsets, rows_of, finish, added, *refs):
@@ -294,20 +326,6 @@
     )(*operands)
 
 
-def touch_kernel(value, out):
-    out[...] = jnp.zeros_like(out)
-
-
-def touch(value):
-    return pl.pallas_call(
-        touch_kernel,
-        in_specs=[pl.BlockSpec(memory_space=pltpu.VMEM)],
-        out_shape=jax.ShapeDtypeStruct((8, 128), jnp.float32),
-        compiler_params=pltpu.CompilerParams(vmem_limit_bytes=8 << 20, has_side_effects=True),
-        name="touch",
-    )(value)
-
-
 def gather_plan(count):
     moves = []
     bit = count // 2
@@ -320,8 +338,10 @@
 
 
 def ring_order(steps):
-    return [
-        way + chunk + str(step) for step in range(1, steps + 1) for chunk in "ab" for way in "rl"
+    names = ["ra1", "la1", "rx1", "lx1", "ry1", "ly1"]
+    names += ["ra2", "la2", "rb2", "lb2"]
+    return names + [
+        way + chunk + str(step) for step in range(3, steps + 1) for chunk in "ab" for way in "rl"
     ]
 
 
@@ -342,31 +362,39 @@
     far_keys = jnp.concatenate([slots[m] for m in far], 0)
     near_swap = lax.ppermute(near_keys, "head", swap_pairs)
     far_swap = lax.ppermute(far_keys, "head", swap_pairs)
-    keys = [own_keys, near_keys, far_keys, near_swap, far_swap]
 
     key_other = lax.ppermute(key_up, "head", swap_pairs)
     value_other = lax.ppermute(value_up, "head", swap_pairs)
     weight_other = lax.ppermute(out_weight, "head", swap_pairs)
     rows_a = lift(queries, key_up, False)
-    touch(value_up)
     rows_b = lift(queries, key_other, True)
-    blocks = (0, key_up.shape[0] // 8)
-    chunks = {}
-    chunks["a"] = attend(rows_a, value_up, keys, rows, blocks)
-    chunks["b"] = attend(rows_b, value_other, keys, rows, blocks)
+    count = key_up.shape[0] // 8
+    early = [own_keys, near_keys, near_swap] + [slots[m] for m in far[:-1]]
+    late = [slots[far[-1]], far_swap]
+    keys = [own_keys, near_keys, near_swap, far_keys, far_swap]
+    own = own_keys.shape[0]
+    running = attend(rows_a, early, rows, (0, count), own)
+    heads_a = attend(rows_a, late, rows, (0, count), 0, value_up, running)
+    heads_x = attend(rows_b, keys, rows, (0, count // 2), own, value_other)
+    heads_y = attend(rows_b, keys, rows, (count // 2, count - count // 2), own, value_other)
 
     order = list(range(0, seq_count, 2)) + list(range(seq_count - 1, 0, -2))
     right = [(order[i], order[(i + 1) % seq_count]) for i in everyone]
     left = [(b, a) for a, b in right]
     steps = seq_count // 2
-    held = {way + chunk + "0": value for chunk, value in chunks.items() for way in "rl"}
-    middle = chunks["a"].shape[1] // 2
+    held = {way + "a0": heads_a for way in "rl"}
+    for way in "rl":
+        held[way + "x0"], held[way + "y0"] = heads_x, heads_y
+    middle = heads_a.shape[1] // 2
     for name in ring_order(steps):
         step = int(name[2:])
         value = held[name[:2] + str(step - 1)]
         if step == steps:
             value = value[:, :middle] if name[0] == "r" else value[:, middle:]
         held[name] = lax.ppermute(value, "seq", right if name[0] == "r" else left)
+        if name[1:] == "y1":
+            parts = [held[name[0] + "x1"], held[name]]
+            held[name[0] + "b1"] = jnp.concatenate(parts, 1)
 
     def put(mixed, *pieces):
         earlier = project(
@@ -385,7 +413,9 @@
             mixed,
         )
 
-    mixed = put(None, (0, "r", 0))
+    earlier = project(seq_count, [(0, [heads_a])], (0,), out_weight, finish=False)
+    pieces = [(0, [heads_x, heads_y])]
+    mixed = project(seq_count, pieces, (0, middle), weight_other, earlier)
     for step in range(1, steps):
         mixed = put(mixed, (-step, "r", step), (step, "l", step))
     ends = (0, middle)

time: 88.1 us -> 91.2 us (1.035)
  starting transfers between devices: 28.6 us -> 33.9 us
  waiting for transfers between devices: 32.4 us -> 30.2 us
    ppermute x16 -> x18, starting transfers between devices: 16.7 us -> 22 us  [layer(): held[name] = lax.ppermute(value, 'seq', right if name[0] == 'r' else left)]
    ppermute x16 -> x18, waiting for transfers between devices: 18.4 us -> 16.2 us  [layer(): held[name] = lax.ppermute(value, 'seq', right if name[0] == 'r' else left)]
    pallas_call x3 -> x4, Pallas kernels: 8.5 us -> 9.11 us  [attend(): pl.pallas_call(functools.partial(attend_kernel, 4 * rows, len(keys), own,...]
    unnamed x19 -> x21, local copies, waits for them, and re-layouts: 5 us -> 4.41 us
  transfers between devices with their start and end apart: 28 -> 30, of which waited for: 10 -> 11; matrix products, arithmetic and copies ran while one was open for 0% -> 0% of each run, Pallas kernels for 23% -> 23%
where the time goes in v4:
time: 91.2 us; the launch traced here: 91 us
  starting transfers between devices  33.9 us (37%)
  waiting for transfers between devices  30.2 us (33%)
  Pallas kernels  21.9 us (24%)
  local copies, waits for them, and re-layouts  4.49 us (5%)
    ppermute x18, starting transfers between devices, layer(): held[name] = lax.ppermute(value, 'seq', right if name[0] == 'r' else left)  22 us
    ppermute x18, waiting for transfers between devices, layer(): held[name] = lax.ppermute(value, 'seq', right if name[0] == 'r' else left)  16.2 us
    ppermute x7, waiting for transfers between devices, layer(): lax.ppermute(slots[slot], 'seq', [(d ^ bit, d) for d in everyone])  14 us
    ppermute x7, starting transfers between devices, layer(): lax.ppermute(slots[slot], 'seq', [(d ^ bit, d) for d in everyone])  10.8 us
    pallas_call x10, Pallas kernels, project(): pl.pallas_call(functools.partial(project_kernel, count, offsets, rows_of,...  10.7 us
    pallas_call x4, Pallas kernels, attend(): pl.pallas_call(functools.partial(attend_kernel, 4 * rows, len(keys), own,...  9.11 us
    unnamed x21, local copies, waits for them, and re-layouts  4.41 us
    pallas_call x2, Pallas kernels, lift(): pl.pallas_call(lift_kernel, grid=(steps,), in_specs=[pl.BlockSpec((rows,...  1.88 us
  transfers between devices with their start and end apart: 30, of which 11 were waited for; matrix products, arithmetic and copies ran while one was open for 0% of the time, Pallas kernels for 23%

profile of v4, /device:TPU:0, one launch (start us, length us, event | category | flops | bytes accessed | tf_op | source)
XLA Modules:
  0.0 91.0 jit_solution(15351920050613795481)
XLA Ops:
  0.0 0.5 collective-permute-start.21
  0.5 0.0 collective-permute-start
  0.5 0.5 collective-permute-start.1
  1.0 0.9 copy-done.5
  1.9 0.7 copy-done.6
  2.6 0.3 prepare.1
  2.9 3.6 %collective-permute-start.3 = (bf16[64,640]{1,0:T(8,128)(2,1)S(1)}, bf16[64,640]{1,0:T(8,128)(2,1)S(1)}, u32[]{:S(2)}, u32[]{:S(2)}) collective-permute-start(bf16[64,640]{1,0:T(8,128)(2,1)S(1)} %get-tuple-element.10), channel_id=1, source_target_pairs={{8,0},{10,2},{12,4},{14,6},{0,8},{2,10},{4,12},{6,14},{9,1},{11,3}... | collective-permute-start | bytes 245768 | tf_op jit(solution)/shard_map/ppermute | solution.py:358
  6.5 1.6 %collective-permute-start.2 = (bf16[64,640]{1,0:T(8,128)(2,1)S(1)}, bf16[64,640]{1,0:T(8,128)(2,1)S(1)}, u32[]{:S(2)}, u32[]{:S(2)}) collective-permute-start(bf16[64,640]{1,0:T(8,128)(2,1)S(1)} %get-tuple-element.10), channel_id=1, source_target_pairs={{4,0},{6,2},{0,4},{2,6},{12,8},{14,10},{8,12},{10,14},{5,1},{7,3},... | collective-permute-start | bytes 245768 | tf_op jit(solution)/shard_map/ppermute | solution.py:358
  8.1 3.4 %collective-permute-done.3 = bf16[64,640]{1,0:T(8,128)(2,1)S(1)} collective-permute-done((bf16[64,640]{1,0:T(8,128)(2,1)S(1)}, bf16[64,640]{1,0:T(8,128)(2,1)S(1)}, u32[]{:S(2)}, u32[]{:S(2)}) %collective-permute-start.3) | collective-permute-done | bytes 81952 | tf_op jit(solution)/shard_map/ppermute | solution.py:358
  11.5 1.6 %collective-permute-start.5 = (bf16[64,640]{1,0:T(8,128)(2,1)S(1)}, bf16[64,640]{1,0:T(8,128)(2,1)S(1)}, u32[]{:S(2)}, u32[]{:S(2)}) collective-permute-start(bf16[64,640]{1,0:T(8,128)(2,1)S(1)} %get-tuple-element.10), channel_id=1, source_target_pairs={{2,0},{0,2},{6,4},{4,6},{10,8},{8,10},{14,12},{12,14},{3,1},{1,3},... | collective-permute-start | bytes 245768 | tf_op jit(solution)/shard_map/ppermute | solution.py:358
  13.1 0.6 collective-permute-start.4
  13.7 3.8 %collective-permute-done.4 = bf16[64,640]{1,0:T(8,128)(2,1)S(1)} collective-permute-done((bf16[64,640]{1,0:T(8,128)(2,1)S(1)}, bf16[64,640]{1,0:T(8,128)(2,1)S(1)}, u32[]{:S(2)}, u32[]{:S(2)}) %collective-permute-start.4) | collective-permute-done | bytes 81952 | tf_op jit(solution)/shard_map/ppermute | solution.py:358
  17.5 0.5 collective-permute-start.8
  18.0 1.6 %collective-permute-start.7 = (bf16[64,640]{1,0:T(8,128)(2,1)S(1)}, bf16[64,640]{1,0:T(8,128)(2,1)S(1)}, u32[]{:S(2)}, u32[]{:S(2)}) collective-permute-start(bf16[64,640]{1,0:T(8,128)(2,1)S(1)} %collective-permute-done.2), channel_id=1, source_target_pairs={{2,0},{0,2},{6,4},{4,6},{10,8},{8,10},{14,12},{12,14},{3,1},{1,3},... | collective-permute-start | bytes 245768 | tf_op jit(solution)/shard_map/ppermute | solution.py:358
  19.6 3.2 %collective-permute-done.7.refs_3_ = bf16[64,640]{1,0:T(8,128)(2,1)S(1)} collective-permute-done((bf16[64,640]{1,0:T(8,128)(2,1)S(1)}, bf16[64,640]{1,0:T(8,128)(2,1)S(1)}, u32[]{:S(2)}, u32[]{:S(2)}) %collective-permute-start.7) | collective-permute-done | bytes 81952 | tf_op jit(solution)/shard_map/ppermute | solution.py:358
  22.8 1.3 %collective-permute-start.9 = (bf16[64,640]{1,0:T(8,128)(2,1)S(1)}, bf16[64,640]{1,0:T(8,128)(2,1)S(1)}, u32[]{:S(2)}, u32[]{:S(2)}) collective-permute-start(bf16[64,640]{1,0:T(8,128)(2,1)S(1)} %collective-permute-done.4), channel_id=1, source_target_pairs={{2,0},{0,2},{6,4},{4,6},{10,8},{8,10},{14,12},{12,14},{3,1},{1,3},... | collective-permute-start | bytes 245768 | tf_op jit(solution)/shard_map/ppermute | solution.py:358
  24.2 3.6 %collective-permute-done.9.refs_3_ = bf16[64,640]{1,0:T(8,128)(2,1)S(1)} collective-permute-done((bf16[64,640]{1,0:T(8,128)(2,1)S(1)}, bf16[64,640]{1,0:T(8,128)(2,1)S(1)}, u32[]{:S(2)}, u32[]{:S(2)}) %collective-permute-start.9) | collective-permute-done | bytes 81952 | tf_op jit(solution)/shard_map/ppermute | solution.py:358
  27.8 0.1 collective-permute-start.10
  27.9 0.0 copy-start.1
  27.9 1.1 %copy-done.1 = bf16[64,6144]{1,0:T(8,128)(2,1)S(1)} copy-done((bf16[64,6144]{1,0:T(8,128)(2,1)S(1)}, bf16[64,6144]{1,0:T(8,128)(2,1)}, u32[]{:S(2)}) %copy-start.1) | copy-done | bytes 786456
  29.0 1.6 %copy-done.4 = bf16[16,128,512]{2,1,0:T(8,128)(2,1)S(1)} copy-done((bf16[16,128,512]{2,1,0:T(8,128)(2,1)S(1)}, bf16[16,128,512]{2,1,0:T(8,128)(2,1)}, u32[]{:S(2)}) %copy-start.4) | copy-done | bytes 2097176
  30.6 0.9 %lift.3.query_rows = bf16[1024,640]{1,0:T(8,128)(2,1)S(1)} custom-call(bf16[64,6144]{1,0:T(8,128)(2,1)S(1)} %copy-done.1, bf16[16,128,512]{2,1,0:T(8,128)(2,1)S(1)} %copy-done.4), custom_call_target="tpu_custom_call" | custom-call | flops 134217728 | bytes 3801088 | tf_op jit(solution)/shard_map/lift/pallas_call | solution.py:114
  31.5 0.0 copy-start.3
  31.6 2.7 %attend.6 = (f32[1024,512]{1,0:T(8,128)S(1)}, f32[1024,256]{1,0:T(8,128)S(1)}) custom-call(bf16[1024,640]{1,0:T(8,128)(2,1)S(1)} %lift.3.query_rows, bf16[128,640]{1,0:T(8,128)(2,1)S(1)} %get-tuple-element.9.refs_1_.refs_0_, bf16[256,640]{1,0:T(8,128)(2,1)S(1)} %constant_dynamic-update-slice_fusion.refs_2_.refs_1_, ...), custom_call_target="tpu_custom_call" | custom-call | flops 1946157056 | bytes 4653056 | tf_op jit(solution)/shard_map/attend/pallas_call | solution.py:226
  34.2 0.0 copy-start.2
  34.2 2.6 %attend.7.refs_0_ = bf16[64,2048]{1,0:T(8,128)(2,1)S(1)} custom-call(bf16[1024,640]{1,0:T(8,128)(2,1)S(1)} %lift.3.query_rows, bf16[16,512,128]{2,1,0:T(8,128)(2,1)S(1)} %copy-done.3, f32[1024,512]{1,0:T(8,128)S(1)} %get-tuple-element.11.refs_1_, f32[1024,256]{1,0:T(8,128)S(1)} %get-tuple-element.12.refs_2_, ...), custom_call_target="tpu_custom_call" | custom-call | flops 738197504 | bytes 3997696 | tf_op jit(solution)/shard_map/attend/pallas_call | solution.py:226
  36.8 0.9 collective-permute-start.22
  37.7 1.2 %collective-permute-start.26 = (bf16[64,2048]{1,0:T(8,128)(2,1)S(1)}, bf16[64,2048]{1,0:T(8,128)(2,1)S(1)}, u32[]{:S(2)}, u32[]{:S(2)}) collective-permute-start(bf16[64,2048]{1,0:T(8,128)(2,1)S(1)} %attend.7.refs_0_), channel_id=1, source_target_pairs={{4,0},{8,4},{12,8},{14,12},{10,14},{6,10},{2,6},{0,2},{5,1},{9,5},... | collective-permute-start | bytes 786440 | tf_op jit(solution)/shard_map/ppermute | solution.py:394
  38.9 0.9 %lift.2.query_rows = bf16[1024,640]{1,0:T(8,128)(2,1)S(1)} custom-call(bf16[64,6144]{1,0:T(8,128)(2,1)S(1)} %copy-done.2, bf16[16,128,512]{2,1,0:T(8,128)(2,1)S(1)} %collective-permute-done.key_up), custom_call_target="tpu_custom_call" | custom-call | flops 134217728 | bytes 3801088 | tf_op jit(solution)/shard_map/lift/pallas_call | solution.py:114
  39.9 1.9 %attend.4.refs_0_ = bf16[64,1024]{1,0:T(8,128)(2,1)S(1)} custom-call(bf16[1024,640]{1,0:T(8,128)(2,1)S(1)} %lift.2.query_rows, bf16[16,512,128]{2,1,0:T(8,128)(2,1)S(1)} %collective-permute-done.1.refs_0_, bf16[128,640]{1,0:T(8,128)(2,1)S(1)} %get-tuple-element.9.refs_1_.refs_0_, bf16[256,640]{1,0:T(8,128)(2,1)S(1)} %constant_dynamic-update-slice_fusion.refs_2_.refs_1_, ...), custom_call_target="tpu_custom_call" | custom-call | flops 1275068416 | bytes 3145728 | tf_op jit(solution)/shard_map/attend/pallas_call | solution.py:226
  41.8 1.3 %collective-permute-start.16 = (bf16[64,1024]{1,0:T(8,128)(2,1)S(1)}, bf16[64,1024]{1,0:T(8,128)(2,1)S(1)}, u32[]{:S(2)}, u32[]{:S(2)}) collective-permute-start(bf16[64,1024]{1,0:T(8,128)(2,1)S(1)} %attend.4.refs_0_), channel_id=1, source_target_pairs={{4,0},{8,4},{12,8},{14,12},{10,14},{6,10},{2,6},{0,2},{5,1},{9,5},... | collective-permute-start | bytes 393224 | tf_op jit(solution)/shard_map/ppermute | solution.py:394
  43.1 2.0 %attend.5.refs_1_ = bf16[64,1024]{1,0:T(8,128)(2,1)S(1)} custom-call(bf16[1024,640]{1,0:T(8,128)(2,1)S(1)} %lift.2.query_rows, bf16[16,512,128]{2,1,0:T(8,128)(2,1)S(1)} %collective-permute-done.1.refs_0_, bf16[128,640]{1,0:T(8,128)(2,1)S(1)} %get-tuple-element.9.refs_1_.refs_0_, bf16[256,640]{1,0:T(8,128)(2,1)S(1)} %constant_dynamic-update-slice_fusion.refs_2_.refs_1_, ...), custom_call_target="tpu_custom_call" | custom-call | flops 1275068416 | bytes 3145728 | tf_op jit(solution)/shard_map/attend/pallas_call | solution.py:226
  45.1 0.7 collective-permute-start.17
  45.7 1.4 %collective-permute-start.23 = (bf16[64,2048]{1,0:T(8,128)(2,1)S(1)}, bf16[64,2048]{1,0:T(8,128)(2,1)S(1)}, u32[]{:S(2)}, u32[]{:S(2)}) collective-permute-start(bf16[64,2048]{1,0:T(8,128)(2,1)S(1)} %collective-permute-done.22.refs_0_), channel_id=1, source_target_pairs={{0,4},{4,8},{8,12},{12,14},{14,10},{10,6},{6,2},{2,0},{1,5},{5,9},... | collective-permute-start | bytes 786440 | tf_op jit(solution)/shard_map/ppermute | solution.py:394
  47.1 0.9 %collective-permute-start.27 = (bf16[64,2048]{1,0:T(8,128)(2,1)S(1)}, bf16[64,2048]{1,0:T(8,128)(2,1)S(1)}, u32[]{:S(2)}, u32[]{:S(2)}) collective-permute-start(bf16[64,2048]{1,0:T(8,128)(2,1)S(1)} %collective-permute-done.26.refs_1_), channel_id=1, source_target_pairs={{4,0},{8,4},{12,8},{14,12},{10,14},{6,10},{2,6},{0,2},{5,1},{9,5},... | collective-permute-start | bytes 786440 | tf_op jit(solution)/shard_map/ppermute | solution.py:394
  48.1 1.6 %collective-permute-done.16 = bf16[64,1024]{1,0:T(8,128)(2,1)S(1)} collective-permute-done((bf16[64,1024]{1,0:T(8,128)(2,1)S(1)}, bf16[64,1024]{1,0:T(8,128)(2,1)S(1)}, u32[]{:S(2)}, u32[]{:S(2)}) %collective-permute-start.16) | collective-permute-done | bytes 131104 | tf_op jit(solution)/shard_map/ppermute | solution.py:394
  49.6 1.7 %collective-permute-start.11 = (bf16[64,1024]{1,0:T(8,128)(2,1)S(1)}, bf16[64,1024]{1,0:T(8,128)(2,1)S(1)}, u32[]{:S(2)}, u32[]{:S(2)}) collective-permute-start(bf16[64,1024]{1,0:T(8,128)(2,1)S(1)} %attend.4.refs_0_), channel_id=1, source_target_pairs={{0,4},{4,8},{8,12},{12,14},{14,10},{10,6},{6,2},{2,0},{1,5},{5,9},... | collective-permute-start | bytes 393224 | tf_op jit(solution)/shard_map/ppermute | solution.py:394
  51.4 1.1 %collective-permute-done.17 = bf16[64,1024]{1,0:T(8,128)(2,1)S(1)} collective-permute-done((bf16[64,1024]{1,0:T(8,128)(2,1)S(1)}, bf16[64,1024]{1,0:T(8,128)(2,1)S(1)}, u32[]{:S(2)}, u32[]{:S(2)}) %collective-permute-start.17) | collective-permute-done | bytes 131104 | tf_op jit(solution)/shard_map/ppermute | solution.py:394
  52.5 1.7 %collective-permute-start.12 = (bf16[64,1024]{1,0:T(8,128)(2,1)S(1)}, bf16[64,1024]{1,0:T(8,128)(2,1)S(1)}, u32[]{:S(2)}, u32[]{:S(2)}) collective-permute-start(bf16[64,1024]{1,0:T(8,128)(2,1)S(1)} %attend.5.refs_1_), channel_id=1, source_target_pairs={{0,4},{4,8},{8,12},{12,14},{14,10},{10,6},{6,2},{2,0},{1,5},{5,9},... | collective-permute-start | bytes 393224 | tf_op jit(solution)/shard_map/ppermute | solution.py:394
  54.2 3.5 %collective-permute-done.11 = bf16[64,1024]{1,0:T(8,128)(2,1)S(1)} collective-permute-done((bf16[64,1024]{1,0:T(8,128)(2,1)S(1)}, bf16[64,1024]{1,0:T(8,128)(2,1)S(1)}, u32[]{:S(2)}, u32[]{:S(2)}) %collective-permute-start.11) | collective-permute-done | bytes 131104 | tf_op jit(solution)/shard_map/ppermute | solution.py:394
  57.7 2.0 %collective-permute-start.18 = (bf16[64,2048]{1,0:T(8,128)(2,1)S(1)}, bf16[64,2048]{1,0:T(8,128)(2,1)S(1)}, u32[]{:S(2)}, u32[]{:S(2)}) collective-permute-start(bf16[64,2048]{1,0:T(8,128)(2,1)S(1)} %constant_dynamic-update-slice_fusion.9.refs_1_), channel_id=1, source_target_pairs={{4,0},{8,4},{12,8},{14,12},{10,14},{6,10},{2,6},{0,2},{5,1},{9,5},... | collective-permute-start | bytes 786440 | tf_op jit(solution)/shard_map/ppermute | solution.py:394
  59.7 0.7 collective-permute-start.13
  60.4 1.2 %collective-permute-start.24 = (bf16[64,2048]{1,0:T(8,128)(2,1)S(1)}, bf16[64,2048]{1,0:T(8,128)(2,1)S(1)}, u32[]{:S(2)}, u32[]{:S(2)}) collective-permute-start(bf16[64,2048]{1,0:T(8,128)(2,1)S(1)} %collective-permute-done.23.refs_0_), channel_id=1, source_target_pairs={{0,4},{4,8},{8,12},{12,14},{14,10},{10,6},{6,2},{2,0},{1,5},{5,9},... | collective-permute-start | bytes 786440 | tf_op jit(solution)/shard_map/ppermute | solution.py:394
  61.6 0.8 collective-permute-start.28
  62.4 3.9 %collective-permute-done.18.refs_1_ = bf16[64,2048]{1,0:T(8,128)(2,1)S(1)} collective-permute-done((bf16[64,2048]{1,0:T(8,128)(2,1)S(1)}, bf16[64,2048]{1,0:T(8,128)(2,1)S(1)}, u32[]{:S(2)}, u32[]{:S(2)}) %collective-permute-start.18) | collective-permute-done | bytes 262176 | tf_op jit(solution)/shard_map/ppermute | solution.py:394
  66.4 2.5 %collective-permute-start.19 = (bf16[64,2048]{1,0:T(8,128)(2,1)S(1)}, bf16[64,2048]{1,0:T(8,128)(2,1)S(1)}, u32[]{:S(2)}, u32[]{:S(2)}) collective-permute-start(bf16[64,2048]{1,0:T(8,128)(2,1)S(1)} %collective-permute-done.18.refs_1_), channel_id=1, source_target_pairs={{4,0},{8,4},{12,8},{14,12},{10,14},{6,10},{2,6},{0,2},{5,1},{9,5},... | collective-permute-start | bytes 786440 | tf_op jit(solution)/shard_map/ppermute | solution.py:394
  68.8 0.1 collective-permute-done.13.refs_0_
  68.9 0.7 collective-permute-start.14
  69.6 0.7 project.14.refs_3_
  70.3 4.2 %collective-permute-done.24.refs_0_ = bf16[64,2048]{1,0:T(8,128)(2,1)S(1)} collective-permute-done((bf16[64,2048]{1,0:T(8,128)(2,1)S(1)}, bf16[64,2048]{1,0:T(8,128)(2,1)S(1)}, u32[]{:S(2)}, u32[]{:S(2)}) %collective-permute-start.24) | collective-permute-done | bytes 262176 | tf_op jit(solution)/shard_map/ppermute | solution.py:394
  74.6 0.7 collective-permute-start.25
  75.3 1.6 %collective-permute-start.29 = (bf16[64,1024]{1,0:T(8,128)(2,1)S(1)}, bf16[64,1024]{1,0:T(8,128)(2,1)S(1)}, u32[]{:S(2)}, u32[]{:S(2)}) collective-permute-start(bf16[64,1024]{1,0:T(8,128)(2,1)S(1)} %slice.19), channel_id=1, source_target_pairs={{4,0},{8,4},{12,8},{14,12},{10,14},{6,10},{2,6},{0,2},{5,1},{9,5},... | collective-permute-start | bytes 393224 | tf_op jit(solution)/shard_map/ppermute | solution.py:394
  76.9 0.7 project.13.refs_3_
  77.6 0.7 project.12.refs_3_
  78.3 0.7 project.11.refs_3_
  79.1 1.7 %collective-permute-done.25.refs_0_ = bf16[64,1024]{1,0:T(8,128)(2,1)S(1)} collective-permute-done((bf16[64,1024]{1,0:T(8,128)(2,1)S(1)}, bf16[64,1024]{1,0:T(8,128)(2,1)S(1)}, u32[]{:S(2)}, u32[]{:S(2)}) %collective-permute-start.25) | collective-permute-done | bytes 131104 | tf_op jit(solution)/shard_map/ppermute | solution.py:394
  80.8 0.7 project.10.refs_3_
  81.5 1.6 %collective-permute-start.20 = (bf16[64,1024]{1,0:T(8,128)(2,1)S(1)}, bf16[64,1024]{1,0:T(8,128)(2,1)S(1)}, u32[]{:S(2)}, u32[]{:S(2)}) collective-permute-start(bf16[64,1024]{1,0:T(8,128)(2,1)S(1)} %slice.17), channel_id=1, source_target_pairs={{4,0},{8,4},{12,8},{14,12},{10,14},{6,10},{2,6},{0,2},{5,1},{9,5},... | collective-permute-start | bytes 393224 | tf_op jit(solution)/shard_map/ppermute | solution.py:394
  83.1 0.6 collective-permute-start.15
  83.7 1.4 %project.15.refs_4_ = bf16[8,1,64,896]{3,2,1,0:T(8,128)(2,1)} custom-call(bf16[64,1024]{1,0:T(8,128)(2,1)S(1)} %attend.4.refs_0_, bf16[64,1024]{1,0:T(8,128)(2,1)S(1)} %attend.5.refs_1_, bf16[2048,896]{1,0:T(8,128)(2,1)S(1)} %collective-permute-done.21.refs_2_, f32[64,896]{1,0:T(8,128)S(1)} %project.14.refs_3_), custom_call_target="tpu_custom_call" | custom-call | flops 234881024 | bytes 3670016 | tf_op jit(solution)/shard_map/project/pallas_call | solution.py:310
  85.1 1.4 %project.16.refs_4_ = bf16[8,1,64,896]{3,2,1,0:T(8,128)(2,1)} custom-call(bf16[64,2048]{1,0:T(8,128)(2,1)S(1)} %constant_dynamic-update-slice_fusion.7.refs_0_, bf16[64,2048]{1,0:T(8,128)(2,1)S(1)} %constant_dynamic-update-slice_fusion.9.refs_1_, bf16[2048,896]{1,0:T(8,128)(2,1)S(1)} %collective-permute-done.21.refs_2_, ...), custom_call_target="tpu_custom_call", output_to_operand_aliasing={{}: (4, {})} | custom-call | flops 469762048 | bytes 3670016 | tf_op jit(solution)/shard_map/project/pallas_call | solution.py:310
  86.5 1.4 %project.17.refs_4_ = bf16[8,1,64,896]{3,2,1,0:T(8,128)(2,1)} custom-call(bf16[64,2048]{1,0:T(8,128)(2,1)S(1)} %collective-permute-done.13.refs_0_, bf16[64,2048]{1,0:T(8,128)(2,1)S(1)} %collective-permute-done.18.refs_1_, bf16[2048,896]{1,0:T(8,128)(2,1)S(1)} %collective-permute-done.21.refs_2_, ...), custom_call_target="tpu_custom_call", output_to_operand_aliasing={{}: (4, {})} | custom-call | flops 469762048 | bytes 3670016 | tf_op jit(solution)/shard_map/project/pallas_call | solution.py:310
  87.9 1.4 %project.18.refs_4_ = bf16[8,1,64,896]{3,2,1,0:T(8,128)(2,1)} custom-call(bf16[64,2048]{1,0:T(8,128)(2,1)S(1)} %collective-permute-done.14.refs_0_, bf16[64,2048]{1,0:T(8,128)(2,1)S(1)} %collective-permute-done.19.refs_1_, bf16[2048,896]{1,0:T(8,128)(2,1)S(1)} %collective-permute-done.21.refs_2_, ...), custom_call_target="tpu_custom_call", output_to_operand_aliasing={{}: (4, {})} | custom-call | flops 469762048 | bytes 3670016 | tf_op jit(solution)/shard_map/project/pallas_call | solution.py:310
  89.4 1.4 %project.19 = bf16[8,1,64,896]{3,2,1,0:T(8,128)(2,1)} custom-call(bf16[64,1024]{1,0:T(8,128)(2,1)S(1)} %collective-permute-done.15.refs_0_, bf16[64,1024]{1,0:T(8,128)(2,1)S(1)} %collective-permute-done.20.refs_1_, bf16[2048,896]{1,0:T(8,128)(2,1)S(1)} %collective-permute-done.21.refs_2_, ...), custom_call_target="tpu_custom_call", output_to_operand_aliasing={{}: (4, {})} | custom-call | flops 234881024 | bytes 3670016 | tf_op jit(solution)/shard_map/project/pallas_call | solution.py:310
  (42 shorter events, 0.2 us)
Async XLA Ops:
  0.0 83.7 %collective-permute-start.21 = (bf16[2048,896]{1,0:T(8,128)(2,1)}, bf16[2048,896]{1,0:T(8,128)(2,1)S(1)}, u32[]{:S(2)}, u32[]{:S(2)}) collective-permute-start(bf16[2048,896]{1,0:T(8,128)(2,1)} %refs_1_.1), channel_id=1, source_target_pairs={{0,1},{1,0},{2,3},{3,2},{4,5},{5,4},{6,7},{7,6},{8,9},{9,8},{10,11... | collective-permute-start | bytes 11010056 | tf_op jit(solution)/shard_map/ppermute | solution.py:368
  0.5 38.4 %collective-permute-start = (bf16[16,128,512]{2,1,0:T(8,128)(2,1)}, bf16[16,128,512]{2,1,0:T(8,128)(2,1)S(1)}, u32[]{:S(2)}, u32[]{:S(2)}) collective-permute-start(bf16[16,128,512]{2,1,0:T(8,128)(2,1)} %key_up.1), channel_id=1, source_target_pairs={{0,1},{1,0},{2,3},{3,2},{4,5},{5,4},{6,7},{7,6},{8,9},{9,8},{10,11... | collective-permute-start | bytes 6291464 | tf_op jit(solution)/shard_map/ppermute | solution.py:366
  0.5 39.3 %collective-permute-start.1 = (bf16[16,512,128]{2,1,0:T(8,128)(2,1)}, bf16[16,512,128]{2,1,0:T(8,128)(2,1)S(1)}, u32[]{:S(2)}, u32[]{:S(2)}) collective-permute-start(bf16[16,512,128]{2,1,0:T(8,128)(2,1)} %refs_0_.1), channel_id=1, source_target_pairs={{0,1},{1,0},{2,3},{3,2},{4,5},{5,4},{6,7},{7,6},{8,9},{9,8},{10,11... | collective-permute-start | bytes 6291464 | tf_op jit(solution)/shard_map/ppermute | solution.py:367
  1.0 0.9 %copy-start.5 = (bf16[128,576]{0,1:T(8,128)(2,1)S(1)}, bf16[128,576]{0,1:T(8,128)(2,1)}, u32[]{:S(2)}) copy-start(bf16[128,576]{0,1:T(8,128)(2,1)} %param.7) | copy-start | bytes 442372
  1.9 0.7 copy-start.6
  2.9 8.6 %collective-permute-start.3 = (bf16[64,640]{1,0:T(8,128)(2,1)S(1)}, bf16[64,640]{1,0:T(8,128)(2,1)S(1)}, u32[]{:S(2)}, u32[]{:S(2)}) collective-permute-start(bf16[64,640]{1,0:T(8,128)(2,1)S(1)} %get-tuple-element.10), channel_id=1, source_target_pairs={{8,0},{10,2},{12,4},{14,6},{0,8},{2,10},{4,12},{6,14},{9,1},{11,3}... | collective-permute-start | bytes 245768 | tf_op jit(solution)/shard_map/ppermute | solution.py:358
  6.5 6.5 %collective-permute-start.2 = (bf16[64,640]{1,0:T(8,128)(2,1)S(1)}, bf16[64,640]{1,0:T(8,128)(2,1)S(1)}, u32[]{:S(2)}, u32[]{:S(2)}) collective-permute-start(bf16[64,640]{1,0:T(8,128)(2,1)S(1)} %get-tuple-element.10), channel_id=1, source_target_pairs={{4,0},{6,2},{0,4},{2,6},{12,8},{14,10},{8,12},{10,14},{5,1},{7,3},... | collective-permute-start | bytes 245768 | tf_op jit(solution)/shard_map/ppermute | solution.py:358
  11.5 6.5 %collective-permute-start.5 = (bf16[64,640]{1,0:T(8,128)(2,1)S(1)}, bf16[64,640]{1,0:T(8,128)(2,1)S(1)}, u32[]{:S(2)}, u32[]{:S(2)}) collective-permute-start(bf16[64,640]{1,0:T(8,128)(2,1)S(1)} %get-tuple-element.10), channel_id=1, source_target_pairs={{2,0},{0,2},{6,4},{4,6},{10,8},{8,10},{14,12},{12,14},{3,1},{1,3},... | collective-permute-start | bytes 245768 | tf_op jit(solution)/shard_map/ppermute | solution.py:358
  13.1 4.4 %collective-permute-start.4 = (bf16[64,640]{1,0:T(8,128)(2,1)S(1)}, bf16[64,640]{1,0:T(8,128)(2,1)S(1)}, u32[]{:S(2)}, u32[]{:S(2)}) collective-permute-start(bf16[64,640]{1,0:T(8,128)(2,1)S(1)} %collective-permute-done.3), channel_id=1, source_target_pairs={{4,0},{6,2},{0,4},{2,6},{12,8},{14,10},{8,12},{10,14},{5,1},{7,3},... | collective-permute-start | bytes 245768 | tf_op jit(solution)/shard_map/ppermute | solution.py:358
  17.5 5.3 %collective-permute-start.8 = (bf16[64,640]{1,0:T(8,128)(2,1)S(1)}, bf16[64,640]{1,0:T(8,128)(2,1)S(1)}, u32[]{:S(2)}, u32[]{:S(2)}) collective-permute-start(bf16[64,640]{1,0:T(8,128)(2,1)S(1)} %collective-permute-done.3), channel_id=1, source_target_pairs={{2,0},{0,2},{6,4},{4,6},{10,8},{8,10},{14,12},{12,14},{3,1},{1,3},... | collective-permute-start | bytes 245768 | tf_op jit(solution)/shard_map/ppermute | solution.py:358
  18.0 4.8 %collective-permute-start.7 = (bf16[64,640]{1,0:T(8,128)(2,1)S(1)}, bf16[64,640]{1,0:T(8,128)(2,1)S(1)}, u32[]{:S(2)}, u32[]{:S(2)}) collective-permute-start(bf16[64,640]{1,0:T(8,128)(2,1)S(1)} %collective-permute-done.2), channel_id=1, source_target_pairs={{2,0},{0,2},{6,4},{4,6},{10,8},{8,10},{14,12},{12,14},{3,1},{1,3},... | collective-permute-start | bytes 245768 | tf_op jit(solution)/shard_map/ppermute | solution.py:358
  22.8 8.7 %collective-permute-start.6 = (bf16[256,640]{1,0:T(8,128)(2,1)S(1)}, bf16[256,640]{1,0:T(8,128)(2,1)S(1)}, u32[]{:S(2)}, u32[]{:S(2)}) collective-permute-start(bf16[256,640]{1,0:T(8,128)(2,1)S(1)} %constant_dynamic-update-slice_fusion.refs_2_.refs_1_), channel_id=1, source_target_pairs={{0,1},{1,0},{2,3},{3,2},{4,5},{5,4},{6,7},{7,6},{8,9},{9,8},{10,11... | collective-permute-start | bytes 983048 | tf_op jit(solution)/shard_map/ppermute | solution.py:363
  22.8 4.9 %collective-permute-start.9 = (bf16[64,640]{1,0:T(8,128)(2,1)S(1)}, bf16[64,640]{1,0:T(8,128)(2,1)S(1)}, u32[]{:S(2)}, u32[]{:S(2)}) collective-permute-start(bf16[64,640]{1,0:T(8,128)(2,1)S(1)} %collective-permute-done.4), channel_id=1, source_target_pairs={{2,0},{0,2},{6,4},{4,6},{10,8},{8,10},{14,12},{12,14},{3,1},{1,3},... | collective-permute-start | bytes 245768 | tf_op jit(solution)/shard_map/ppermute | solution.py:358
  27.8 6.4 %collective-permute-start.10 = (bf16[192,640]{1,0:T(8,128)(2,1)S(1)}, bf16[192,640]{1,0:T(8,128)(2,1)S(1)}, u32[]{:S(2)}, u32[]{:S(2)}) collective-permute-start(bf16[192,640]{1,0:T(8,128)(2,1)S(1)} %constant_dynamic-update-slice_fusion.4.refs_4_), channel_id=1, source_target_pairs={{0,1},{1,0},{2,3},{3,2},{4,5},{5,4},{6,7},{7,6},{8,9},{9,8},{10,11... | collective-permute-start | bytes 737288 | tf_op jit(solution)/shard_map/ppermute | solution.py:364
  27.9 1.1 %copy-start.1 = (bf16[64,6144]{1,0:T(8,128)(2,1)S(1)}, bf16[64,6144]{1,0:T(8,128)(2,1)}, u32[]{:S(2)}) copy-start(bf16[64,6144]{1,0:T(8,128)(2,1)} %queries.3) | copy-start | bytes 2359300
  29.0 1.6 %copy-start.4 = (bf16[16,128,512]{2,1,0:T(8,128)(2,1)S(1)}, bf16[16,128,512]{2,1,0:T(8,128)(2,1)}, u32[]{:S(2)}) copy-start(bf16[16,128,512]{2,1,0:T(8,128)(2,1)} %key_up.1) | copy-start | bytes 6291460
  31.5 2.7 %copy-start.3 = (bf16[16,512,128]{2,1,0:T(8,128)(2,1)S(1)}, bf16[16,512,128]{2,1,0:T(8,128)(2,1)}, u32[]{:S(2)}) copy-start(bf16[16,512,128]{2,1,0:T(8,128)(2,1)} %refs_0_.1) | copy-start | bytes 6291460
  34.2 4.7 %copy-start.2 = (bf16[64,6144]{1,0:T(8,128)(2,1)S(1)}, bf16[64,6144]{1,0:T(8,128)(2,1)}, u32[]{:S(2)}) copy-start(bf16[64,6144]{1,0:T(8,128)(2,1)} %queries.3) | copy-start | bytes 2359300
  36.8 8.9 %collective-permute-start.22 = (bf16[64,2048]{1,0:T(8,128)(2,1)S(1)}, bf16[64,2048]{1,0:T(8,128)(2,1)S(1)}, u32[]{:S(2)}, u32[]{:S(2)}) collective-permute-start(bf16[64,2048]{1,0:T(8,128)(2,1)S(1)} %attend.7.refs_0_), channel_id=1, source_target_pairs={{0,4},{4,8},{8,12},{12,14},{14,10},{10,6},{6,2},{2,0},{1,5},{5,9},... | collective-permute-start | bytes 786440 | tf_op jit(solution)/shard_map/ppermute | solution.py:394
  37.7 9.5 %collective-permute-start.26 = (bf16[64,2048]{1,0:T(8,128)(2,1)S(1)}, bf16[64,2048]{1,0:T(8,128)(2,1)S(1)}, u32[]{:S(2)}, u32[]{:S(2)}) collective-permute-start(bf16[64,2048]{1,0:T(8,128)(2,1)S(1)} %attend.7.refs_0_), channel_id=1, source_target_pairs={{4,0},{8,4},{12,8},{14,12},{10,14},{6,10},{2,6},{0,2},{5,1},{9,5},... | collective-permute-start | bytes 786440 | tf_op jit(solution)/shard_map/ppermute | solution.py:394
  41.8 27.8 %copy-start = (bf16[2048,896]{1,0:T(8,128)(2,1)S(1)}, bf16[2048,896]{1,0:T(8,128)(2,1)}, u32[]{:S(2)}) copy-start(bf16[2048,896]{1,0:T(8,128)(2,1)} %refs_1_.1) | copy-start | bytes 11010052
  41.8 7.8 %collective-permute-start.16 = (bf16[64,1024]{1,0:T(8,128)(2,1)S(1)}, bf16[64,1024]{1,0:T(8,128)(2,1)S(1)}, u32[]{:S(2)}, u32[]{:S(2)}) collective-permute-start(bf16[64,1024]{1,0:T(8,128)(2,1)S(1)} %attend.4.refs_0_), channel_id=1, source_target_pairs={{4,0},{8,4},{12,8},{14,12},{10,14},{6,10},{2,6},{0,2},{5,1},{9,5},... | collective-permute-start | bytes 393224 | tf_op jit(solution)/shard_map/ppermute | solution.py:394
  45.1 7.4 %collective-permute-start.17 = (bf16[64,1024]{1,0:T(8,128)(2,1)S(1)}, bf16[64,1024]{1,0:T(8,128)(2,1)S(1)}, u32[]{:S(2)}, u32[]{:S(2)}) collective-permute-start(bf16[64,1024]{1,0:T(8,128)(2,1)S(1)} %attend.5.refs_1_), channel_id=1, source_target_pairs={{4,0},{8,4},{12,8},{14,12},{10,14},{6,10},{2,6},{0,2},{5,1},{9,5},... | collective-permute-start | bytes 393224 | tf_op jit(solution)/shard_map/ppermute | solution.py:394
  45.7 14.7 %collective-permute-start.23 = (bf16[64,2048]{1,0:T(8,128)(2,1)S(1)}, bf16[64,2048]{1,0:T(8,128)(2,1)S(1)}, u32[]{:S(2)}, u32[]{:S(2)}) collective-permute-start(bf16[64,2048]{1,0:T(8,128)(2,1)S(1)} %collective-permute-done.22.refs_0_), channel_id=1, source_target_pairs={{0,4},{4,8},{8,12},{12,14},{14,10},{10,6},{6,2},{2,0},{1,5},{5,9},... | collective-permute-start | bytes 786440 | tf_op jit(solution)/shard_map/ppermute | solution.py:394
  47.1 14.5 %collective-permute-start.27 = (bf16[64,2048]{1,0:T(8,128)(2,1)S(1)}, bf16[64,2048]{1,0:T(8,128)(2,1)S(1)}, u32[]{:S(2)}, u32[]{:S(2)}) collective-permute-start(bf16[64,2048]{1,0:T(8,128)(2,1)S(1)} %collective-permute-done.26.refs_1_), channel_id=1, source_target_pairs={{4,0},{8,4},{12,8},{14,12},{10,14},{6,10},{2,6},{0,2},{5,1},{9,5},... | collective-permute-start | bytes 786440 | tf_op jit(solution)/shard_map/ppermute | solution.py:394
  49.6 8.1 %collective-permute-start.11 = (bf16[64,1024]{1,0:T(8,128)(2,1)S(1)}, bf16[64,1024]{1,0:T(8,128)(2,1)S(1)}, u32[]{:S(2)}, u32[]{:S(2)}) collective-permute-start(bf16[64,1024]{1,0:T(8,128)(2,1)S(1)} %attend.4.refs_0_), channel_id=1, source_target_pairs={{0,4},{4,8},{8,12},{12,14},{14,10},{10,6},{6,2},{2,0},{1,5},{5,9},... | collective-permute-start | bytes 393224 | tf_op jit(solution)/shard_map/ppermute | solution.py:394
  52.5 7.2 %collective-permute-start.12 = (bf16[64,1024]{1,0:T(8,128)(2,1)S(1)}, bf16[64,1024]{1,0:T(8,128)(2,1)S(1)}, u32[]{:S(2)}, u32[]{:S(2)}) collective-permute-start(bf16[64,1024]{1,0:T(8,128)(2,1)S(1)} %attend.5.refs_1_), channel_id=1, source_target_pairs={{0,4},{4,8},{8,12},{12,14},{14,10},{10,6},{6,2},{2,0},{1,5},{5,9},... | collective-permute-start | bytes 393224 | tf_op jit(solution)/shard_map/ppermute | solution.py:394
  57.7 8.7 %collective-permute-start.18 = (bf16[64,2048]{1,0:T(8,128)(2,1)S(1)}, bf16[64,2048]{1,0:T(8,128)(2,1)S(1)}, u32[]{:S(2)}, u32[]{:S(2)}) collective-permute-start(bf16[64,2048]{1,0:T(8,128)(2,1)S(1)} %constant_dynamic-update-slice_fusion.9.refs_1_), channel_id=1, source_target_pairs={{4,0},{8,4},{12,8},{14,12},{10,14},{6,10},{2,6},{0,2},{5,1},{9,5},... | collective-permute-start | bytes 786440 | tf_op jit(solution)/shard_map/ppermute | solution.py:394
  59.7 9.2 %collective-permute-start.13 = (bf16[64,2048]{1,0:T(8,128)(2,1)S(1)}, bf16[64,2048]{1,0:T(8,128)(2,1)S(1)}, u32[]{:S(2)}, u32[]{:S(2)}) collective-permute-start(bf16[64,2048]{1,0:T(8,128)(2,1)S(1)} %constant_dynamic-update-slice_fusion.7.refs_0_), channel_id=1, source_target_pairs={{0,4},{4,8},{8,12},{12,14},{14,10},{10,6},{6,2},{2,0},{1,5},{5,9},... | collective-permute-start | bytes 786440 | tf_op jit(solution)/shard_map/ppermute | solution.py:394
  60.4 14.1 %collective-permute-start.24 = (bf16[64,2048]{1,0:T(8,128)(2,1)S(1)}, bf16[64,2048]{1,0:T(8,128)(2,1)S(1)}, u32[]{:S(2)}, u32[]{:S(2)}) collective-permute-start(bf16[64,2048]{1,0:T(8,128)(2,1)S(1)} %collective-permute-done.23.refs_0_), channel_id=1, source_target_pairs={{0,4},{4,8},{8,12},{12,14},{14,10},{10,6},{6,2},{2,0},{1,5},{5,9},... | collective-permute-start | bytes 786440 | tf_op jit(solution)/shard_map/ppermute | solution.py:394
  61.6 13.7 %collective-permute-start.28 = (bf16[64,2048]{1,0:T(8,128)(2,1)S(1)}, bf16[64,2048]{1,0:T(8,128)(2,1)S(1)}, u32[]{:S(2)}, u32[]{:S(2)}) collective-permute-start(bf16[64,2048]{1,0:T(8,128)(2,1)S(1)} %collective-permute-done.27.refs_1_), channel_id=1, source_target_pairs={{4,0},{8,4},{12,8},{14,12},{10,14},{6,10},{2,6},{0,2},{5,1},{9,5},... | collective-permute-start | bytes 786440 | tf_op jit(solution)/shard_map/ppermute | solution.py:394
  66.4 15.1 %collective-permute-start.19 = (bf16[64,2048]{1,0:T(8,128)(2,1)S(1)}, bf16[64,2048]{1,0:T(8,128)(2,1)S(1)}, u32[]{:S(2)}, u32[]{:S(2)}) collective-permute-start(bf16[64,2048]{1,0:T(8,128)(2,1)S(1)} %collective-permute-done.18.refs_1_), channel_id=1, source_target_pairs={{4,0},{8,4},{12,8},{14,12},{10,14},{6,10},{2,6},{0,2},{5,1},{9,5},... | collective-permute-start | bytes 786440 | tf_op jit(solution)/shard_map/ppermute | solution.py:394
  68.9 14.2 %collective-permute-start.14 = (bf16[64,2048]{1,0:T(8,128)(2,1)S(1)}, bf16[64,2048]{1,0:T(8,128)(2,1)S(1)}, u32[]{:S(2)}, u32[]{:S(2)}) collective-permute-start(bf16[64,2048]{1,0:T(8,128)(2,1)S(1)} %collective-permute-done.13.refs_0_), channel_id=1, source_target_pairs={{0,4},{4,8},{8,12},{12,14},{14,10},{10,6},{6,2},{2,0},{1,5},{5,9},... | collective-permute-start | bytes 786440 | tf_op jit(solution)/shard_map/ppermute | solution.py:394
  74.6 6.2 %collective-permute-start.25 = (bf16[64,1024]{1,0:T(8,128)(2,1)S(1)}, bf16[64,1024]{1,0:T(8,128)(2,1)S(1)}, u32[]{:S(2)}, u32[]{:S(2)}) collective-permute-start(bf16[64,1024]{1,0:T(8,128)(2,1)S(1)} %slice.18), channel_id=1, source_target_pairs={{0,4},{4,8},{8,12},{12,14},{14,10},{10,6},{6,2},{2,0},{1,5},{5,9},... | collective-permute-start | bytes 393224 | tf_op jit(solution)/shard_map/ppermute | solution.py:394
  75.3 5.5 %collective-permute-start.29 = (bf16[64,1024]{1,0:T(8,128)(2,1)S(1)}, bf16[64,1024]{1,0:T(8,128)(2,1)S(1)}, u32[]{:S(2)}, u32[]{:S(2)}) collective-permute-start(bf16[64,1024]{1,0:T(8,128)(2,1)S(1)} %slice.19), channel_id=1, source_target_pairs={{4,0},{8,4},{12,8},{14,12},{10,14},{6,10},{2,6},{0,2},{5,1},{9,5},... | collective-permute-start | bytes 393224 | tf_op jit(solution)/shard_map/ppermute | solution.py:394
  81.5 7.9 %collective-permute-start.20 = (bf16[64,1024]{1,0:T(8,128)(2,1)S(1)}, bf16[64,1024]{1,0:T(8,128)(2,1)S(1)}, u32[]{:S(2)}, u32[]{:S(2)}) collective-permute-start(bf16[64,1024]{1,0:T(8,128)(2,1)S(1)} %slice.17), channel_id=1, source_target_pairs={{4,0},{8,4},{12,8},{14,12},{10,14},{6,10},{2,6},{0,2},{5,1},{9,5},... | collective-permute-start | bytes 393224 | tf_op jit(solution)/shard_map/ppermute | solution.py:394
  83.1 6.3 %collective-permute-start.15 = (bf16[64,1024]{1,0:T(8,128)(2,1)S(1)}, bf16[64,1024]{1,0:T(8,128)(2,1)S(1)}, u32[]{:S(2)}, u32[]{:S(2)}) collective-permute-start(bf16[64,1024]{1,0:T(8,128)(2,1)S(1)} %slice.16), channel_id=1, source_target_pairs={{0,4},{4,8},{8,12},{12,14},{14,10},{10,6},{6,2},{2,0},{1,5},{5,9},... | collective-permute-start | bytes 393224 | tf_op jit(solution)/shard_map/ppermute | solution.py:394

commit v5 on v4

--- a/solution.py
+++ b/solution.py
@@ -130,14 +130,14 @@
     )(queries, key_up)
 
 
-def attend_kernel(part, groups, own, earlier, finish, query_rows, *refs):
+def attend_kernel(offset_rows, part, groups, own, earlier, finish, query_rows, *refs):
     refs = list(refs)
     value_up = refs.pop(0) if finish else None
     old_sums, old_stats = (refs.pop(0), refs.pop(0)) if earlier else (None, None)
     groups, refs = refs[:groups], refs[groups:]
     keys = refs[-1]
     total = query_rows.shape[0]
-    rows = total // 8
+    rows = offset_rows
 
     @pl.when(pl.program_id(0) == 0)
     def _():
@@ -204,6 +204,8 @@
     step = 8
     first, count = blocks
     heads = count * step
+    if first == 0:
+        step, count = heads, 1
     key_total = sum(key.shape[0] for key in keys)
     finish = value_up is not None
     operands, specs = [query_rows], [pl.BlockSpec((step * rows, WIDE), lambda i: (first + i, 0))]
@@ -225,7 +227,7 @@
         ]
     return pl.pallas_call(
         functools.partial(
-            attend_kernel, 4 * rows, len(keys), own, bool(earlier), finish
+            attend_kernel, rows, 4 * rows, len(keys), own, bool(earlier), finish
         ),
         grid=(count,),
         in_specs=specs,

time: 91.2 us -> 90.6 us (level)
  transfers between devices with their start and end apart: 30 -> 30, of which waited for: 11 -> 11; matrix products, arithmetic and copies ran while one was open for 0% -> 0% of each run, Pallas kernels for 23% -> 22%
where the time goes in v5:
time: 90.6 us; the launch traced here: 90.4 us
  starting transfers between devices  33.9 us (37%)
  waiting for transfers between devices  30.2 us (33%)
  Pallas kernels  21.4 us (24%)
  local copies, waits for them, and re-layouts  4.49 us (5%)
    ppermute x18, starting transfers between devices, layer(): held[name] = lax.ppermute(value, 'seq', right if name[0] == 'r' else left)  22 us
    ppermute x18, waiting for transfers between devices, layer(): held[name] = lax.ppermute(value, 'seq', right if name[0] == 'r' else left)  16.2 us
    ppermute x7, waiting for transfers between devices, layer(): lax.ppermute(slots[slot], 'seq', [(d ^ bit, d) for d in everyone])  14 us
    ppermute x7, starting transfers between devices, layer(): lax.ppermute(slots[slot], 'seq', [(d ^ bit, d) for d in everyone])  10.8 us
    pallas_call x10, Pallas kernels, project(): pl.pallas_call(functools.partial(project_kernel, count, offsets, rows_of,...  10.7 us
    pallas_call x4, Pallas kernels, attend(): pl.pallas_call(functools.partial(attend_kernel, rows, 4 * rows, len(keys)...  8.54 us
    unnamed x21, local copies, waits for them, and re-layouts  4.41 us
    pallas_call x2, Pallas kernels, lift(): pl.pallas_call(lift_kernel, grid=(steps,), in_specs=[pl.BlockSpec((rows,...  1.88 us
  transfers between devices with their start and end apart: 30, of which 11 were waited for; matrix products, arithmetic and copies ran while one was open for 0% of the time, Pallas kernels for 22%

profile of v5, /device:TPU:0, one launch (start us, length us, event | category | flops | bytes accessed | tf_op | source)
XLA Modules:
  0.0 90.4 jit_solution(267396904179998922)
XLA Ops:
  0.0 0.5 collective-permute-start.21
  0.5 0.0 collective-permute-start
  0.5 0.5 collective-permute-start.1
  1.0 0.9 %copy-done.5 = bf16[128,576]{0,1:T(8,128)(2,1)S(1)} copy-done((bf16[128,576]{0,1:T(8,128)(2,1)S(1)}, bf16[128,576]{0,1:T(8,128)(2,1)}, u32[]{:S(2)}) %copy-start.5) | copy-done | bytes 147480
  1.9 0.7 copy-done.6
  2.6 0.3 prepare.1
  2.9 3.6 %collective-permute-start.3 = (bf16[64,640]{1,0:T(8,128)(2,1)S(1)}, bf16[64,640]{1,0:T(8,128)(2,1)S(1)}, u32[]{:S(2)}, u32[]{:S(2)}) collective-permute-start(bf16[64,640]{1,0:T(8,128)(2,1)S(1)} %get-tuple-element.10), channel_id=1, source_target_pairs={{8,0},{10,2},{12,4},{14,6},{0,8},{2,10},{4,12},{6,14},{9,1},{11,3}... | collective-permute-start | bytes 245768 | tf_op jit(solution)/shard_map/ppermute | solution.py:360
  6.5 1.6 %collective-permute-start.2 = (bf16[64,640]{1,0:T(8,128)(2,1)S(1)}, bf16[64,640]{1,0:T(8,128)(2,1)S(1)}, u32[]{:S(2)}, u32[]{:S(2)}) collective-permute-start(bf16[64,640]{1,0:T(8,128)(2,1)S(1)} %get-tuple-element.10), channel_id=1, source_target_pairs={{4,0},{6,2},{0,4},{2,6},{12,8},{14,10},{8,12},{10,14},{5,1},{7,3},... | collective-permute-start | bytes 245768 | tf_op jit(solution)/shard_map/ppermute | solution.py:360
  8.1 3.4 %collective-permute-done.3 = bf16[64,640]{1,0:T(8,128)(2,1)S(1)} collective-permute-done((bf16[64,640]{1,0:T(8,128)(2,1)S(1)}, bf16[64,640]{1,0:T(8,128)(2,1)S(1)}, u32[]{:S(2)}, u32[]{:S(2)}) %collective-permute-start.3) | collective-permute-done | bytes 81952 | tf_op jit(solution)/shard_map/ppermute | solution.py:360
  11.5 1.6 %collective-permute-start.5 = (bf16[64,640]{1,0:T(8,128)(2,1)S(1)}, bf16[64,640]{1,0:T(8,128)(2,1)S(1)}, u32[]{:S(2)}, u32[]{:S(2)}) collective-permute-start(bf16[64,640]{1,0:T(8,128)(2,1)S(1)} %get-tuple-element.10), channel_id=1, source_target_pairs={{2,0},{0,2},{6,4},{4,6},{10,8},{8,10},{14,12},{12,14},{3,1},{1,3},... | collective-permute-start | bytes 245768 | tf_op jit(solution)/shard_map/ppermute | solution.py:360
  13.1 0.6 collective-permute-start.4
  13.7 3.8 %collective-permute-done.4 = bf16[64,640]{1,0:T(8,128)(2,1)S(1)} collective-permute-done((bf16[64,640]{1,0:T(8,128)(2,1)S(1)}, bf16[64,640]{1,0:T(8,128)(2,1)S(1)}, u32[]{:S(2)}, u32[]{:S(2)}) %collective-permute-start.4) | collective-permute-done | bytes 81952 | tf_op jit(solution)/shard_map/ppermute | solution.py:360
  17.5 0.5 collective-permute-start.8
  18.0 1.6 %collective-permute-start.7 = (bf16[64,640]{1,0:T(8,128)(2,1)S(1)}, bf16[64,640]{1,0:T(8,128)(2,1)S(1)}, u32[]{:S(2)}, u32[]{:S(2)}) collective-permute-start(bf16[64,640]{1,0:T(8,128)(2,1)S(1)} %collective-permute-done.2), channel_id=1, source_target_pairs={{2,0},{0,2},{6,4},{4,6},{10,8},{8,10},{14,12},{12,14},{3,1},{1,3},... | collective-permute-start | bytes 245768 | tf_op jit(solution)/shard_map/ppermute | solution.py:360
  19.6 3.2 %collective-permute-done.7.refs_3_ = bf16[64,640]{1,0:T(8,128)(2,1)S(1)} collective-permute-done((bf16[64,640]{1,0:T(8,128)(2,1)S(1)}, bf16[64,640]{1,0:T(8,128)(2,1)S(1)}, u32[]{:S(2)}, u32[]{:S(2)}) %collective-permute-start.7) | collective-permute-done | bytes 81952 | tf_op jit(solution)/shard_map/ppermute | solution.py:360
  22.8 1.3 %collective-permute-start.9 = (bf16[64,640]{1,0:T(8,128)(2,1)S(1)}, bf16[64,640]{1,0:T(8,128)(2,1)S(1)}, u32[]{:S(2)}, u32[]{:S(2)}) collective-permute-start(bf16[64,640]{1,0:T(8,128)(2,1)S(1)} %collective-permute-done.4), channel_id=1, source_target_pairs={{2,0},{0,2},{6,4},{4,6},{10,8},{8,10},{14,12},{12,14},{3,1},{1,3},... | collective-permute-start | bytes 245768 | tf_op jit(solution)/shard_map/ppermute | solution.py:360
  24.2 3.6 %collective-permute-done.9.refs_3_ = bf16[64,640]{1,0:T(8,128)(2,1)S(1)} collective-permute-done((bf16[64,640]{1,0:T(8,128)(2,1)S(1)}, bf16[64,640]{1,0:T(8,128)(2,1)S(1)}, u32[]{:S(2)}, u32[]{:S(2)}) %collective-permute-start.9) | collective-permute-done | bytes 81952 | tf_op jit(solution)/shard_map/ppermute | solution.py:360
  27.8 0.1 collective-permute-start.10
  27.9 0.0 copy-start.1
  27.9 1.1 %copy-done.1 = bf16[64,6144]{1,0:T(8,128)(2,1)S(1)} copy-done((bf16[64,6144]{1,0:T(8,128)(2,1)S(1)}, bf16[64,6144]{1,0:T(8,128)(2,1)}, u32[]{:S(2)}) %copy-start.1) | copy-done | bytes 786456
  29.0 1.6 %copy-done.4 = bf16[16,128,512]{2,1,0:T(8,128)(2,1)S(1)} copy-done((bf16[16,128,512]{2,1,0:T(8,128)(2,1)S(1)}, bf16[16,128,512]{2,1,0:T(8,128)(2,1)}, u32[]{:S(2)}) %copy-start.4) | copy-done | bytes 2097176
  30.6 0.9 %lift.3.query_rows = bf16[1024,640]{1,0:T(8,128)(2,1)S(1)} custom-call(bf16[64,6144]{1,0:T(8,128)(2,1)S(1)} %copy-done.1, bf16[16,128,512]{2,1,0:T(8,128)(2,1)S(1)} %copy-done.4), custom_call_target="tpu_custom_call" | custom-call | flops 134217728 | bytes 3801088 | tf_op jit(solution)/shard_map/lift/pallas_call | solution.py:114
  31.5 0.0 copy-start.3
  31.6 2.4 %attend.6 = (f32[1024,512]{1,0:T(8,128)S(1)}, f32[1024,256]{1,0:T(8,128)S(1)}) custom-call(bf16[1024,640]{1,0:T(8,128)(2,1)S(1)} %lift.3.query_rows, bf16[128,640]{1,0:T(8,128)(2,1)S(1)} %get-tuple-element.9.refs_1_.refs_0_, bf16[256,640]{1,0:T(8,128)(2,1)S(1)} %constant_dynamic-update-slice_fusion.refs_2_.refs_1_, ...), custom_call_target="tpu_custom_call" | custom-call | flops 1946157056 | bytes 4653056 | tf_op jit(solution)/shard_map/attend/pallas_call | solution.py:228
  34.0 2.3 %attend.7.refs_0_ = bf16[64,2048]{1,0:T(8,128)(2,1)S(1)} custom-call(bf16[1024,640]{1,0:T(8,128)(2,1)S(1)} %lift.3.query_rows, bf16[16,512,128]{2,1,0:T(8,128)(2,1)S(1)} %copy-done.3, f32[1024,512]{1,0:T(8,128)S(1)} %get-tuple-element.11.refs_1_, f32[1024,256]{1,0:T(8,128)S(1)} %get-tuple-element.12.refs_2_, ...), custom_call_target="tpu_custom_call" | custom-call | flops 738197504 | bytes 3997696 | tf_op jit(solution)/shard_map/attend/pallas_call | solution.py:228
  36.2 0.9 collective-permute-start.22
  37.1 1.2 %collective-permute-start.26 = (bf16[64,2048]{1,0:T(8,128)(2,1)S(1)}, bf16[64,2048]{1,0:T(8,128)(2,1)S(1)}, u32[]{:S(2)}, u32[]{:S(2)}) collective-permute-start(bf16[64,2048]{1,0:T(8,128)(2,1)S(1)} %attend.7.refs_0_), channel_id=1, source_target_pairs={{4,0},{8,4},{12,8},{14,12},{10,14},{6,10},{2,6},{0,2},{5,1},{9,5},... | collective-permute-start | bytes 786440 | tf_op jit(solution)/shard_map/ppermute | solution.py:396
  38.3 0.9 %lift.2.query_rows = bf16[1024,640]{1,0:T(8,128)(2,1)S(1)} custom-call(bf16[64,6144]{1,0:T(8,128)(2,1)S(1)} %copy-done.2, bf16[16,128,512]{2,1,0:T(8,128)(2,1)S(1)} %collective-permute-done.key_up), custom_call_target="tpu_custom_call" | custom-call | flops 134217728 | bytes 3801088 | tf_op jit(solution)/shard_map/lift/pallas_call | solution.py:114
  39.3 2.0 %attend.4.refs_0_ = bf16[64,1024]{1,0:T(8,128)(2,1)S(1)} custom-call(bf16[1024,640]{1,0:T(8,128)(2,1)S(1)} %lift.2.query_rows, bf16[16,512,128]{2,1,0:T(8,128)(2,1)S(1)} %collective-permute-done.1.refs_0_, bf16[128,640]{1,0:T(8,128)(2,1)S(1)} %get-tuple-element.9.refs_1_.refs_0_, bf16[256,640]{1,0:T(8,128)(2,1)S(1)} %constant_dynamic-update-slice_fusion.refs_2_.refs_1_, ...), custom_call_target="tpu_custom_call" | custom-call | flops 1275068416 | bytes 3145728 | tf_op jit(solution)/shard_map/attend/pallas_call | solution.py:228
  41.2 0.0 copy-start
  41.2 1.3 %collective-permute-start.16 = (bf16[64,1024]{1,0:T(8,128)(2,1)S(1)}, bf16[64,1024]{1,0:T(8,128)(2,1)S(1)}, u32[]{:S(2)}, u32[]{:S(2)}) collective-permute-start(bf16[64,1024]{1,0:T(8,128)(2,1)S(1)} %attend.4.refs_0_), channel_id=1, source_target_pairs={{4,0},{8,4},{12,8},{14,12},{10,14},{6,10},{2,6},{0,2},{5,1},{9,5},... | collective-permute-start | bytes 393224 | tf_op jit(solution)/shard_map/ppermute | solution.py:396
  42.5 2.0 %attend.5.refs_1_ = bf16[64,1024]{1,0:T(8,128)(2,1)S(1)} custom-call(bf16[1024,640]{1,0:T(8,128)(2,1)S(1)} %lift.2.query_rows, bf16[16,512,128]{2,1,0:T(8,128)(2,1)S(1)} %collective-permute-done.1.refs_0_, bf16[128,640]{1,0:T(8,128)(2,1)S(1)} %get-tuple-element.9.refs_1_.refs_0_, bf16[256,640]{1,0:T(8,128)(2,1)S(1)} %constant_dynamic-update-slice_fusion.refs_2_.refs_1_, ...), custom_call_target="tpu_custom_call" | custom-call | flops 1275068416 | bytes 3145728 | tf_op jit(solution)/shard_map/attend/pallas_call | solution.py:228
  44.5 0.7 collective-permute-start.17
  45.1 1.4 %collective-permute-start.23 = (bf16[64,2048]{1,0:T(8,128)(2,1)S(1)}, bf16[64,2048]{1,0:T(8,128)(2,1)S(1)}, u32[]{:S(2)}, u32[]{:S(2)}) collective-permute-start(bf16[64,2048]{1,0:T(8,128)(2,1)S(1)} %collective-permute-done.22.refs_0_), channel_id=1, source_target_pairs={{0,4},{4,8},{8,12},{12,14},{14,10},{10,6},{6,2},{2,0},{1,5},{5,9},... | collective-permute-start | bytes 786440 | tf_op jit(solution)/shard_map/ppermute | solution.py:396
  46.6 0.9 %collective-permute-start.27 = (bf16[64,2048]{1,0:T(8,128)(2,1)S(1)}, bf16[64,2048]{1,0:T(8,128)(2,1)S(1)}, u32[]{:S(2)}, u32[]{:S(2)}) collective-permute-start(bf16[64,2048]{1,0:T(8,128)(2,1)S(1)} %collective-permute-done.26.refs_1_), channel_id=1, source_target_pairs={{4,0},{8,4},{12,8},{14,12},{10,14},{6,10},{2,6},{0,2},{5,1},{9,5},... | collective-permute-start | bytes 786440 | tf_op jit(solution)/shard_map/ppermute | solution.py:396
  47.5 1.6 %collective-permute-done.16 = bf16[64,1024]{1,0:T(8,128)(2,1)S(1)} collective-permute-done((bf16[64,1024]{1,0:T(8,128)(2,1)S(1)}, bf16[64,1024]{1,0:T(8,128)(2,1)S(1)}, u32[]{:S(2)}, u32[]{:S(2)}) %collective-permute-start.16) | collective-permute-done | bytes 131104 | tf_op jit(solution)/shard_map/ppermute | solution.py:396
  49.1 1.7 %collective-permute-start.11 = (bf16[64,1024]{1,0:T(8,128)(2,1)S(1)}, bf16[64,1024]{1,0:T(8,128)(2,1)S(1)}, u32[]{:S(2)}, u32[]{:S(2)}) collective-permute-start(bf16[64,1024]{1,0:T(8,128)(2,1)S(1)} %attend.4.refs_0_), channel_id=1, source_target_pairs={{0,4},{4,8},{8,12},{12,14},{14,10},{10,6},{6,2},{2,0},{1,5},{5,9},... | collective-permute-start | bytes 393224 | tf_op jit(solution)/shard_map/ppermute | solution.py:396
  50.8 1.1 %collective-permute-done.17 = bf16[64,1024]{1,0:T(8,128)(2,1)S(1)} collective-permute-done((bf16[64,1024]{1,0:T(8,128)(2,1)S(1)}, bf16[64,1024]{1,0:T(8,128)(2,1)S(1)}, u32[]{:S(2)}, u32[]{:S(2)}) %collective-permute-start.17) | collective-permute-done | bytes 131104 | tf_op jit(solution)/shard_map/ppermute | solution.py:396
  51.9 1.7 %collective-permute-start.12 = (bf16[64,1024]{1,0:T(8,128)(2,1)S(1)}, bf16[64,1024]{1,0:T(8,128)(2,1)S(1)}, u32[]{:S(2)}, u32[]{:S(2)}) collective-permute-start(bf16[64,1024]{1,0:T(8,128)(2,1)S(1)} %attend.5.refs_1_), channel_id=1, source_target_pairs={{0,4},{4,8},{8,12},{12,14},{14,10},{10,6},{6,2},{2,0},{1,5},{5,9},... | collective-permute-start | bytes 393224 | tf_op jit(solution)/shard_map/ppermute | solution.py:396
  53.6 3.5 %collective-permute-done.11 = bf16[64,1024]{1,0:T(8,128)(2,1)S(1)} collective-permute-done((bf16[64,1024]{1,0:T(8,128)(2,1)S(1)}, bf16[64,1024]{1,0:T(8,128)(2,1)S(1)}, u32[]{:S(2)}, u32[]{:S(2)}) %collective-permute-start.11) | collective-permute-done | bytes 131104 | tf_op jit(solution)/shard_map/ppermute | solution.py:396
  57.1 2.0 %collective-permute-start.18 = (bf16[64,2048]{1,0:T(8,128)(2,1)S(1)}, bf16[64,2048]{1,0:T(8,128)(2,1)S(1)}, u32[]{:S(2)}, u32[]{:S(2)}) collective-permute-start(bf16[64,2048]{1,0:T(8,128)(2,1)S(1)} %constant_dynamic-update-slice_fusion.9.refs_1_), channel_id=1, source_target_pairs={{4,0},{8,4},{12,8},{14,12},{10,14},{6,10},{2,6},{0,2},{5,1},{9,5},... | collective-permute-start | bytes 786440 | tf_op jit(solution)/shard_map/ppermute | solution.py:396
  59.1 0.7 collective-permute-start.13
  59.8 1.2 %collective-permute-start.24 = (bf16[64,2048]{1,0:T(8,128)(2,1)S(1)}, bf16[64,2048]{1,0:T(8,128)(2,1)S(1)}, u32[]{:S(2)}, u32[]{:S(2)}) collective-permute-start(bf16[64,2048]{1,0:T(8,128)(2,1)S(1)} %collective-permute-done.23.refs_0_), channel_id=1, source_target_pairs={{0,4},{4,8},{8,12},{12,14},{14,10},{10,6},{6,2},{2,0},{1,5},{5,9},... | collective-permute-start | bytes 786440 | tf_op jit(solution)/shard_map/ppermute | solution.py:396
  61.0 0.9 collective-permute-start.28
  61.9 3.9 %collective-permute-done.18.refs_1_ = bf16[64,2048]{1,0:T(8,128)(2,1)S(1)} collective-permute-done((bf16[64,2048]{1,0:T(8,128)(2,1)S(1)}, bf16[64,2048]{1,0:T(8,128)(2,1)S(1)}, u32[]{:S(2)}, u32[]{:S(2)}) %collective-permute-start.18) | collective-permute-done | bytes 262176 | tf_op jit(solution)/shard_map/ppermute | solution.py:396
  65.8 2.5 %collective-permute-start.19 = (bf16[64,2048]{1,0:T(8,128)(2,1)S(1)}, bf16[64,2048]{1,0:T(8,128)(2,1)S(1)}, u32[]{:S(2)}, u32[]{:S(2)}) collective-permute-start(bf16[64,2048]{1,0:T(8,128)(2,1)S(1)} %collective-permute-done.18.refs_1_), channel_id=1, source_target_pairs={{4,0},{8,4},{12,8},{14,12},{10,14},{6,10},{2,6},{0,2},{5,1},{9,5},... | collective-permute-start | bytes 786440 | tf_op jit(solution)/shard_map/ppermute | solution.py:396
  68.3 0.1 collective-permute-done.13.refs_0_
  68.4 0.7 collective-permute-start.14
  69.0 0.7 project.14.refs_3_
  69.8 4.2 %collective-permute-done.24.refs_0_ = bf16[64,2048]{1,0:T(8,128)(2,1)S(1)} collective-permute-done((bf16[64,2048]{1,0:T(8,128)(2,1)S(1)}, bf16[64,2048]{1,0:T(8,128)(2,1)S(1)}, u32[]{:S(2)}, u32[]{:S(2)}) %collective-permute-start.24) | collective-permute-done | bytes 262176 | tf_op jit(solution)/shard_map/ppermute | solution.py:396
  74.0 0.7 collective-permute-start.25
  74.7 1.6 %collective-permute-start.29 = (bf16[64,1024]{1,0:T(8,128)(2,1)S(1)}, bf16[64,1024]{1,0:T(8,128)(2,1)S(1)}, u32[]{:S(2)}, u32[]{:S(2)}) collective-permute-start(bf16[64,1024]{1,0:T(8,128)(2,1)S(1)} %slice.19), channel_id=1, source_target_pairs={{4,0},{8,4},{12,8},{14,12},{10,14},{6,10},{2,6},{0,2},{5,1},{9,5},... | collective-permute-start | bytes 393224 | tf_op jit(solution)/shard_map/ppermute | solution.py:396
  76.3 0.7 project.13.refs_3_
  77.0 0.7 project.12.refs_3_
  77.8 0.7 project.11.refs_3_
  78.5 1.7 %collective-permute-done.25.refs_0_ = bf16[64,1024]{1,0:T(8,128)(2,1)S(1)} collective-permute-done((bf16[64,1024]{1,0:T(8,128)(2,1)S(1)}, bf16[64,1024]{1,0:T(8,128)(2,1)S(1)}, u32[]{:S(2)}, u32[]{:S(2)}) %collective-permute-start.25) | collective-permute-done | bytes 131104 | tf_op jit(solution)/shard_map/ppermute | solution.py:396
  80.2 0.7 project.10.refs_3_
  80.9 1.6 %collective-permute-start.20 = (bf16[64,1024]{1,0:T(8,128)(2,1)S(1)}, bf16[64,1024]{1,0:T(8,128)(2,1)S(1)}, u32[]{:S(2)}, u32[]{:S(2)}) collective-permute-start(bf16[64,1024]{1,0:T(8,128)(2,1)S(1)} %slice.17), channel_id=1, source_target_pairs={{4,0},{8,4},{12,8},{14,12},{10,14},{6,10},{2,6},{0,2},{5,1},{9,5},... | collective-permute-start | bytes 393224 | tf_op jit(solution)/shard_map/ppermute | solution.py:396
  82.5 0.6 collective-permute-start.15
  83.1 1.4 %project.15.refs_4_ = bf16[8,1,64,896]{3,2,1,0:T(8,128)(2,1)} custom-call(bf16[64,1024]{1,0:T(8,128)(2,1)S(1)} %attend.4.refs_0_, bf16[64,1024]{1,0:T(8,128)(2,1)S(1)} %attend.5.refs_1_, bf16[2048,896]{1,0:T(8,128)(2,1)S(1)} %collective-permute-done.21.refs_2_, f32[64,896]{1,0:T(8,128)S(1)} %project.14.refs_3_), custom_call_target="tpu_custom_call" | custom-call | flops 234881024 | bytes 3670016 | tf_op jit(solution)/shard_map/project/pallas_call | solution.py:312
  84.5 1.4 %project.16.refs_4_ = bf16[8,1,64,896]{3,2,1,0:T(8,128)(2,1)} custom-call(bf16[64,2048]{1,0:T(8,128)(2,1)S(1)} %constant_dynamic-update-slice_fusion.7.refs_0_, bf16[64,2048]{1,0:T(8,128)(2,1)S(1)} %constant_dynamic-update-slice_fusion.9.refs_1_, bf16[2048,896]{1,0:T(8,128)(2,1)S(1)} %collective-permute-done.21.refs_2_, ...), custom_call_target="tpu_custom_call", output_to_operand_aliasing={{}: (4, {})} | custom-call | flops 469762048 | bytes 3670016 | tf_op jit(solution)/shard_map/project/pallas_call | solution.py:312
  85.9 1.4 %project.17.refs_4_ = bf16[8,1,64,896]{3,2,1,0:T(8,128)(2,1)} custom-call(bf16[64,2048]{1,0:T(8,128)(2,1)S(1)} %collective-permute-done.13.refs_0_, bf16[64,2048]{1,0:T(8,128)(2,1)S(1)} %collective-permute-done.18.refs_1_, bf16[2048,896]{1,0:T(8,128)(2,1)S(1)} %collective-permute-done.21.refs_2_, ...), custom_call_target="tpu_custom_call", output_to_operand_aliasing={{}: (4, {})} | custom-call | flops 469762048 | bytes 3670016 | tf_op jit(solution)/shard_map/project/pallas_call | solution.py:312
  87.4 1.4 %project.18.refs_4_ = bf16[8,1,64,896]{3,2,1,0:T(8,128)(2,1)} custom-call(bf16[64,2048]{1,0:T(8,128)(2,1)S(1)} %collective-permute-done.14.refs_0_, bf16[64,2048]{1,0:T(8,128)(2,1)S(1)} %collective-permute-done.19.refs_1_, bf16[2048,896]{1,0:T(8,128)(2,1)S(1)} %collective-permute-done.21.refs_2_, ...), custom_call_target="tpu_custom_call", output_to_operand_aliasing={{}: (4, {})} | custom-call | flops 469762048 | bytes 3670016 | tf_op jit(solution)/shard_map/project/pallas_call | solution.py:312
  88.8 1.4 %project.19 = bf16[8,1,64,896]{3,2,1,0:T(8,128)(2,1)} custom-call(bf16[64,1024]{1,0:T(8,128)(2,1)S(1)} %collective-permute-done.15.refs_0_, bf16[64,1024]{1,0:T(8,128)(2,1)S(1)} %collective-permute-done.20.refs_1_, bf16[2048,896]{1,0:T(8,128)(2,1)S(1)} %collective-permute-done.21.refs_2_, ...), custom_call_target="tpu_custom_call", output_to_operand_aliasing={{}: (4, {})} | custom-call | flops 234881024 | bytes 3670016 | tf_op jit(solution)/shard_map/project/pallas_call | solution.py:312
  (42 shorter events, 0.2 us)
Async XLA Ops:
  0.0 83.1 %collective-permute-start.21 = (bf16[2048,896]{1,0:T(8,128)(2,1)}, bf16[2048,896]{1,0:T(8,128)(2,1)S(1)}, u32[]{:S(2)}, u32[]{:S(2)}) collective-permute-start(bf16[2048,896]{1,0:T(8,128)(2,1)} %refs_1_.1), channel_id=1, source_target_pairs={{0,1},{1,0},{2,3},{3,2},{4,5},{5,4},{6,7},{7,6},{8,9},{9,8},{10,11... | collective-permute-start | bytes 11010056 | tf_op jit(solution)/shard_map/ppermute | solution.py:370
  0.5 37.8 %collective-permute-start = (bf16[16,128,512]{2,1,0:T(8,128)(2,1)}, bf16[16,128,512]{2,1,0:T(8,128)(2,1)S(1)}, u32[]{:S(2)}, u32[]{:S(2)}) collective-permute-start(bf16[16,128,512]{2,1,0:T(8,128)(2,1)} %key_up.1), channel_id=1, source_target_pairs={{0,1},{1,0},{2,3},{3,2},{4,5},{5,4},{6,7},{7,6},{8,9},{9,8},{10,11... | collective-permute-start | bytes 6291464 | tf_op jit(solution)/shard_map/ppermute | solution.py:368
  0.5 38.8 %collective-permute-start.1 = (bf16[16,512,128]{2,1,0:T(8,128)(2,1)}, bf16[16,512,128]{2,1,0:T(8,128)(2,1)S(1)}, u32[]{:S(2)}, u32[]{:S(2)}) collective-permute-start(bf16[16,512,128]{2,1,0:T(8,128)(2,1)} %refs_0_.1), channel_id=1, source_target_pairs={{0,1},{1,0},{2,3},{3,2},{4,5},{5,4},{6,7},{7,6},{8,9},{9,8},{10,11... | collective-permute-start | bytes 6291464 | tf_op jit(solution)/shard_map/ppermute | solution.py:369
  1.0 0.9 %copy-start.5 = (bf16[128,576]{0,1:T(8,128)(2,1)S(1)}, bf16[128,576]{0,1:T(8,128)(2,1)}, u32[]{:S(2)}) copy-start(bf16[128,576]{0,1:T(8,128)(2,1)} %param.7) | copy-start | bytes 442372
  1.9 0.7 copy-start.6
  2.9 8.6 %collective-permute-start.3 = (bf16[64,640]{1,0:T(8,128)(2,1)S(1)}, bf16[64,640]{1,0:T(8,128)(2,1)S(1)}, u32[]{:S(2)}, u32[]{:S(2)}) collective-permute-start(bf16[64,640]{1,0:T(8,128)(2,1)S(1)} %get-tuple-element.10), channel_id=1, source_target_pairs={{8,0},{10,2},{12,4},{14,6},{0,8},{2,10},{4,12},{6,14},{9,1},{11,3}... | collective-permute-start | bytes 245768 | tf_op jit(solution)/shard_map/ppermute | solution.py:360
  6.5 6.5 %collective-permute-start.2 = (bf16[64,640]{1,0:T(8,128)(2,1)S(1)}, bf16[64,640]{1,0:T(8,128)(2,1)S(1)}, u32[]{:S(2)}, u32[]{:S(2)}) collective-permute-start(bf16[64,640]{1,0:T(8,128)(2,1)S(1)} %get-tuple-element.10), channel_id=1, source_target_pairs={{4,0},{6,2},{0,4},{2,6},{12,8},{14,10},{8,12},{10,14},{5,1},{7,3},... | collective-permute-start | bytes 245768 | tf_op jit(solution)/shard_map/ppermute | solution.py:360
  11.5 6.5 %collective-permute-start.5 = (bf16[64,640]{1,0:T(8,128)(2,1)S(1)}, bf16[64,640]{1,0:T(8,128)(2,1)S(1)}, u32[]{:S(2)}, u32[]{:S(2)}) collective-permute-start(bf16[64,640]{1,0:T(8,128)(2,1)S(1)} %get-tuple-element.10), channel_id=1, source_target_pairs={{2,0},{0,2},{6,4},{4,6},{10,8},{8,10},{14,12},{12,14},{3,1},{1,3},... | collective-permute-start | bytes 245768 | tf_op jit(solution)/shard_map/ppermute | solution.py:360
  13.1 4.4 %collective-permute-start.4 = (bf16[64,640]{1,0:T(8,128)(2,1)S(1)}, bf16[64,640]{1,0:T(8,128)(2,1)S(1)}, u32[]{:S(2)}, u32[]{:S(2)}) collective-permute-start(bf16[64,640]{1,0:T(8,128)(2,1)S(1)} %collective-permute-done.3), channel_id=1, source_target_pairs={{4,0},{6,2},{0,4},{2,6},{12,8},{14,10},{8,12},{10,14},{5,1},{7,3},... | collective-permute-start | bytes 245768 | tf_op jit(solution)/shard_map/ppermute | solution.py:360
  17.5 5.3 %collective-permute-start.8 = (bf16[64,640]{1,0:T(8,128)(2,1)S(1)}, bf16[64,640]{1,0:T(8,128)(2,1)S(1)}, u32[]{:S(2)}, u32[]{:S(2)}) collective-permute-start(bf16[64,640]{1,0:T(8,128)(2,1)S(1)} %collective-permute-done.3), channel_id=1, source_target_pairs={{2,0},{0,2},{6,4},{4,6},{10,8},{8,10},{14,12},{12,14},{3,1},{1,3},... | collective-permute-start | bytes 245768 | tf_op jit(solution)/shard_map/ppermute | solution.py:360
  18.0 4.8 %collective-permute-start.7 = (bf16[64,640]{1,0:T(8,128)(2,1)S(1)}, bf16[64,640]{1,0:T(8,128)(2,1)S(1)}, u32[]{:S(2)}, u32[]{:S(2)}) collective-permute-start(bf16[64,640]{1,0:T(8,128)(2,1)S(1)} %collective-permute-done.2), channel_id=1, source_target_pairs={{2,0},{0,2},{6,4},{4,6},{10,8},{8,10},{14,12},{12,14},{3,1},{1,3},... | collective-permute-start | bytes 245768 | tf_op jit(solution)/shard_map/ppermute | solution.py:360
  22.8 8.7 %collective-permute-start.6 = (bf16[256,640]{1,0:T(8,128)(2,1)S(1)}, bf16[256,640]{1,0:T(8,128)(2,1)S(1)}, u32[]{:S(2)}, u32[]{:S(2)}) collective-permute-start(bf16[256,640]{1,0:T(8,128)(2,1)S(1)} %constant_dynamic-update-slice_fusion.refs_2_.refs_1_), channel_id=1, source_target_pairs={{0,1},{1,0},{2,3},{3,2},{4,5},{5,4},{6,7},{7,6},{8,9},{9,8},{10,11... | collective-permute-start | bytes 983048 | tf_op jit(solution)/shard_map/ppermute | solution.py:365
  22.8 4.9 %collective-permute-start.9 = (bf16[64,640]{1,0:T(8,128)(2,1)S(1)}, bf16[64,640]{1,0:T(8,128)(2,1)S(1)}, u32[]{:S(2)}, u32[]{:S(2)}) collective-permute-start(bf16[64,640]{1,0:T(8,128)(2,1)S(1)} %collective-permute-done.4), channel_id=1, source_target_pairs={{2,0},{0,2},{6,4},{4,6},{10,8},{8,10},{14,12},{12,14},{3,1},{1,3},... | collective-permute-start | bytes 245768 | tf_op jit(solution)/shard_map/ppermute | solution.py:360
  27.8 6.2 %collective-permute-start.10 = (bf16[192,640]{1,0:T(8,128)(2,1)S(1)}, bf16[192,640]{1,0:T(8,128)(2,1)S(1)}, u32[]{:S(2)}, u32[]{:S(2)}) collective-permute-start(bf16[192,640]{1,0:T(8,128)(2,1)S(1)} %constant_dynamic-update-slice_fusion.4.refs_4_), channel_id=1, source_target_pairs={{0,1},{1,0},{2,3},{3,2},{4,5},{5,4},{6,7},{7,6},{8,9},{9,8},{10,11... | collective-permute-start | bytes 737288 | tf_op jit(solution)/shard_map/ppermute | solution.py:366
  27.9 1.1 %copy-start.1 = (bf16[64,6144]{1,0:T(8,128)(2,1)S(1)}, bf16[64,6144]{1,0:T(8,128)(2,1)}, u32[]{:S(2)}) copy-start(bf16[64,6144]{1,0:T(8,128)(2,1)} %queries.3) | copy-start | bytes 2359300
  29.0 1.6 %copy-start.4 = (bf16[16,128,512]{2,1,0:T(8,128)(2,1)S(1)}, bf16[16,128,512]{2,1,0:T(8,128)(2,1)}, u32[]{:S(2)}) copy-start(bf16[16,128,512]{2,1,0:T(8,128)(2,1)} %key_up.1) | copy-start | bytes 6291460
  31.5 2.4 %copy-start.3 = (bf16[16,512,128]{2,1,0:T(8,128)(2,1)S(1)}, bf16[16,512,128]{2,1,0:T(8,128)(2,1)}, u32[]{:S(2)}) copy-start(bf16[16,512,128]{2,1,0:T(8,128)(2,1)} %refs_0_.1) | copy-start | bytes 6291460
  34.0 4.4 %copy-start.2 = (bf16[64,6144]{1,0:T(8,128)(2,1)S(1)}, bf16[64,6144]{1,0:T(8,128)(2,1)}, u32[]{:S(2)}) copy-start(bf16[64,6144]{1,0:T(8,128)(2,1)} %queries.3) | copy-start | bytes 2359300
  36.2 8.9 %collective-permute-start.22 = (bf16[64,2048]{1,0:T(8,128)(2,1)S(1)}, bf16[64,2048]{1,0:T(8,128)(2,1)S(1)}, u32[]{:S(2)}, u32[]{:S(2)}) collective-permute-start(bf16[64,2048]{1,0:T(8,128)(2,1)S(1)} %attend.7.refs_0_), channel_id=1, source_target_pairs={{0,4},{4,8},{8,12},{12,14},{14,10},{10,6},{6,2},{2,0},{1,5},{5,9},... | collective-permute-start | bytes 786440 | tf_op jit(solution)/shard_map/ppermute | solution.py:396
  37.1 9.5 %collective-permute-start.26 = (bf16[64,2048]{1,0:T(8,128)(2,1)S(1)}, bf16[64,2048]{1,0:T(8,128)(2,1)S(1)}, u32[]{:S(2)}, u32[]{:S(2)}) collective-permute-start(bf16[64,2048]{1,0:T(8,128)(2,1)S(1)} %attend.7.refs_0_), channel_id=1, source_target_pairs={{4,0},{8,4},{12,8},{14,12},{10,14},{6,10},{2,6},{0,2},{5,1},{9,5},... | collective-permute-start | bytes 786440 | tf_op jit(solution)/shard_map/ppermute | solution.py:396
  41.2 27.8 %copy-start = (bf16[2048,896]{1,0:T(8,128)(2,1)S(1)}, bf16[2048,896]{1,0:T(8,128)(2,1)}, u32[]{:S(2)}) copy-start(bf16[2048,896]{1,0:T(8,128)(2,1)} %refs_1_.1) | copy-start | bytes 11010052
  41.2 7.8 %collective-permute-start.16 = (bf16[64,1024]{1,0:T(8,128)(2,1)S(1)}, bf16[64,1024]{1,0:T(8,128)(2,1)S(1)}, u32[]{:S(2)}, u32[]{:S(2)}) collective-permute-start(bf16[64,1024]{1,0:T(8,128)(2,1)S(1)} %attend.4.refs_0_), channel_id=1, source_target_pairs={{4,0},{8,4},{12,8},{14,12},{10,14},{6,10},{2,6},{0,2},{5,1},{9,5},... | collective-permute-start | bytes 393224 | tf_op jit(solution)/shard_map/ppermute | solution.py:396
  44.5 7.4 %collective-permute-start.17 = (bf16[64,1024]{1,0:T(8,128)(2,1)S(1)}, bf16[64,1024]{1,0:T(8,128)(2,1)S(1)}, u32[]{:S(2)}, u32[]{:S(2)}) collective-permute-start(bf16[64,1024]{1,0:T(8,128)(2,1)S(1)} %attend.5.refs_1_), channel_id=1, source_target_pairs={{4,0},{8,4},{12,8},{14,12},{10,14},{6,10},{2,6},{0,2},{5,1},{9,5},... | collective-permute-start | bytes 393224 | tf_op jit(solution)/shard_map/ppermute | solution.py:396
  45.1 14.7 %collective-permute-start.23 = (bf16[64,2048]{1,0:T(8,128)(2,1)S(1)}, bf16[64,2048]{1,0:T(8,128)(2,1)S(1)}, u32[]{:S(2)}, u32[]{:S(2)}) collective-permute-start(bf16[64,2048]{1,0:T(8,128)(2,1)S(1)} %collective-permute-done.22.refs_0_), channel_id=1, source_target_pairs={{0,4},{4,8},{8,12},{12,14},{14,10},{10,6},{6,2},{2,0},{1,5},{5,9},... | collective-permute-start | bytes 786440 | tf_op jit(solution)/shard_map/ppermute | solution.py:396
  46.6 14.5 %collective-permute-start.27 = (bf16[64,2048]{1,0:T(8,128)(2,1)S(1)}, bf16[64,2048]{1,0:T(8,128)(2,1)S(1)}, u32[]{:S(2)}, u32[]{:S(2)}) collective-permute-start(bf16[64,2048]{1,0:T(8,128)(2,1)S(1)} %collective-permute-done.26.refs_1_), channel_id=1, source_target_pairs={{4,0},{8,4},{12,8},{14,12},{10,14},{6,10},{2,6},{0,2},{5,1},{9,5},... | collective-permute-start | bytes 786440 | tf_op jit(solution)/shard_map/ppermute | solution.py:396
  49.1 8.1 %collective-permute-start.11 = (bf16[64,1024]{1,0:T(8,128)(2,1)S(1)}, bf16[64,1024]{1,0:T(8,128)(2,1)S(1)}, u32[]{:S(2)}, u32[]{:S(2)}) collective-permute-start(bf16[64,1024]{1,0:T(8,128)(2,1)S(1)} %attend.4.refs_0_), channel_id=1, source_target_pairs={{0,4},{4,8},{8,12},{12,14},{14,10},{10,6},{6,2},{2,0},{1,5},{5,9},... | collective-permute-start | bytes 393224 | tf_op jit(solution)/shard_map/ppermute | solution.py:396
  51.9 7.2 %collective-permute-start.12 = (bf16[64,1024]{1,0:T(8,128)(2,1)S(1)}, bf16[64,1024]{1,0:T(8,128)(2,1)S(1)}, u32[]{:S(2)}, u32[]{:S(2)}) collective-permute-start(bf16[64,1024]{1,0:T(8,128)(2,1)S(1)} %attend.5.refs_1_), channel_id=1, source_target_pairs={{0,4},{4,8},{8,12},{12,14},{14,10},{10,6},{6,2},{2,0},{1,5},{5,9},... | collective-permute-start | bytes 393224 | tf_op jit(solution)/shard_map/ppermute | solution.py:396
  57.1 8.7 %collective-permute-start.18 = (bf16[64,2048]{1,0:T(8,128)(2,1)S(1)}, bf16[64,2048]{1,0:T(8,128)(2,1)S(1)}, u32[]{:S(2)}, u32[]{:S(2)}) collective-permute-start(bf16[64,2048]{1,0:T(8,128)(2,1)S(1)} %constant_dynamic-update-slice_fusion.9.refs_1_), channel_id=1, source_target_pairs={{4,0},{8,4},{12,8},{14,12},{10,14},{6,10},{2,6},{0,2},{5,1},{9,5},... | collective-permute-start | bytes 786440 | tf_op jit(solution)/shard_map/ppermute | solution.py:396
  59.1 9.2 %collective-permute-start.13 = (bf16[64,2048]{1,0:T(8,128)(2,1)S(1)}, bf16[64,2048]{1,0:T(8,128)(2,1)S(1)}, u32[]{:S(2)}, u32[]{:S(2)}) collective-permute-start(bf16[64,2048]{1,0:T(8,128)(2,1)S(1)} %constant_dynamic-update-slice_fusion.7.refs_0_), channel_id=1, source_target_pairs={{0,4},{4,8},{8,12},{12,14},{14,10},{10,6},{6,2},{2,0},{1,5},{5,9},... | collective-permute-start | bytes 786440 | tf_op jit(solution)/shard_map/ppermute | solution.py:396
  59.8 14.1 %collective-permute-start.24 = (bf16[64,2048]{1,0:T(8,128)(2,1)S(1)}, bf16[64,2048]{1,0:T(8,128)(2,1)S(1)}, u32[]{:S(2)}, u32[]{:S(2)}) collective-permute-start(bf16[64,2048]{1,0:T(8,128)(2,1)S(1)} %collective-permute-done.23.refs_0_), channel_id=1, source_target_pairs={{0,4},{4,8},{8,12},{12,14},{14,10},{10,6},{6,2},{2,0},{1,5},{5,9},... | collective-permute-start | bytes 786440 | tf_op jit(solution)/shard_map/ppermute | solution.py:396
  61.0 13.7 %collective-permute-start.28 = (bf16[64,2048]{1,0:T(8,128)(2,1)S(1)}, bf16[64,2048]{1,0:T(8,128)(2,1)S(1)}, u32[]{:S(2)}, u32[]{:S(2)}) collective-permute-start(bf16[64,2048]{1,0:T(8,128)(2,1)S(1)} %collective-permute-done.27.refs_1_), channel_id=1, source_target_pairs={{4,0},{8,4},{12,8},{14,12},{10,14},{6,10},{2,6},{0,2},{5,1},{9,5},... | collective-permute-start | bytes 786440 | tf_op jit(solution)/shard_map/ppermute | solution.py:396
  65.8 15.1 %collective-permute-start.19 = (bf16[64,2048]{1,0:T(8,128)(2,1)S(1)}, bf16[64,2048]{1,0:T(8,128)(2,1)S(1)}, u32[]{:S(2)}, u32[]{:S(2)}) collective-permute-start(bf16[64,2048]{1,0:T(8,128)(2,1)S(1)} %collective-permute-done.18.refs_1_), channel_id=1, source_target_pairs={{4,0},{8,4},{12,8},{14,12},{10,14},{6,10},{2,6},{0,2},{5,1},{9,5},... | collective-permute-start | bytes 786440 | tf_op jit(solution)/shard_map/ppermute | solution.py:396
  68.4 14.2 %collective-permute-start.14 = (bf16[64,2048]{1,0:T(8,128)(2,1)S(1)}, bf16[64,2048]{1,0:T(8,128)(2,1)S(1)}, u32[]{:S(2)}, u32[]{:S(2)}) collective-permute-start(bf16[64,2048]{1,0:T(8,128)(2,1)S(1)} %collective-permute-done.13.refs_0_), channel_id=1, source_target_pairs={{0,4},{4,8},{8,12},{12,14},{14,10},{10,6},{6,2},{2,0},{1,5},{5,9},... | collective-permute-start | bytes 786440 | tf_op jit(solution)/shard_map/ppermute | solution.py:396
  74.0 6.2 %collective-permute-start.25 = (bf16[64,1024]{1,0:T(8,128)(2,1)S(1)}, bf16[64,1024]{1,0:T(8,128)(2,1)S(1)}, u32[]{:S(2)}, u32[]{:S(2)}) collective-permute-start(bf16[64,1024]{1,0:T(8,128)(2,1)S(1)} %slice.18), channel_id=1, source_target_pairs={{0,4},{4,8},{8,12},{12,14},{14,10},{10,6},{6,2},{2,0},{1,5},{5,9},... | collective-permute-start | bytes 393224 | tf_op jit(solution)/shard_map/ppermute | solution.py:396
  74.7 5.5 %collective-permute-start.29 = (bf16[64,1024]{1,0:T(8,128)(2,1)S(1)}, bf16[64,1024]{1,0:T(8,128)(2,1)S(1)}, u32[]{:S(2)}, u32[]{:S(2)}) collective-permute-start(bf16[64,1024]{1,0:T(8,128)(2,1)S(1)} %slice.19), channel_id=1, source_target_pairs={{4,0},{8,4},{12,8},{14,12},{10,14},{6,10},{2,6},{0,2},{5,1},{9,5},... | collective-permute-start | bytes 393224 | tf_op jit(solution)/shard_map/ppermute | solution.py:396
  80.9 7.9 %collective-permute-start.20 = (bf16[64,1024]{1,0:T(8,128)(2,1)S(1)}, bf16[64,1024]{1,0:T(8,128)(2,1)S(1)}, u32[]{:S(2)}, u32[]{:S(2)}) collective-permute-start(bf16[64,1024]{1,0:T(8,128)(2,1)S(1)} %slice.17), channel_id=1, source_target_pairs={{4,0},{8,4},{12,8},{14,12},{10,14},{6,10},{2,6},{0,2},{5,1},{9,5},... | collective-permute-start | bytes 393224 | tf_op jit(solution)/shard_map/ppermute | solution.py:396
  82.5 6.3 %collective-permute-start.15 = (bf16[64,1024]{1,0:T(8,128)(2,1)S(1)}, bf16[64,1024]{1,0:T(8,128)(2,1)S(1)}, u32[]{:S(2)}, u32[]{:S(2)}) collective-permute-start(bf16[64,1024]{1,0:T(8,128)(2,1)S(1)} %slice.16), channel_id=1, source_target_pairs={{0,4},{4,8},{8,12},{12,14},{14,10},{10,6},{6,2},{2,0},{1,5},{5,9},... | collective-permute-start | bytes 393224 | tf_op jit(solution)/shard_map/ppermute | solution.py:396

commit v6 on v5

--- a/solution.py
+++ b/solution.py
@@ -361,9 +361,11 @@
     near = [m for m in range(1, seq_count) if m % 2 == 0] + [1]
     far = [m for m in range(2, seq_count) if m % 2 == 1]
     near_keys = jnp.concatenate([slots[m] for m in near], 0)
-    far_keys = jnp.concatenate([slots[m] for m in far], 0)
+    middle_keys = jnp.concatenate([slots[m] for m in far[:-1]], 0)
+    last_keys = slots[far[-1]]
     near_swap = lax.ppermute(near_keys, "head", swap_pairs)
-    far_swap = lax.ppermute(far_keys, "head", swap_pairs)
+    middle_swap = lax.ppermute(middle_keys, "head", swap_pairs)
+    last_swap = lax.ppermute(last_keys, "head", swap_pairs)
 
     key_other = lax.ppermute(key_up, "head", swap_pairs)
     value_other = lax.ppermute(value_up, "head", swap_pairs)
@@ -371,9 +373,9 @@
     rows_a = lift(queries, key_up, False)
     rows_b = lift(queries, key_other, True)
     count = key_up.shape[0] // 8
-    early = [own_keys, near_keys, near_swap] + [slots[m] for m in far[:-1]]
-    late = [slots[far[-1]], far_swap]
-    keys = [own_keys, near_keys, near_swap, far_keys, far_swap]
+    early = [own_keys, near_keys, near_swap, middle_keys]
+    late = [middle_swap, last_keys, last_swap]
+    keys = early + late
     own = own_keys.shape[0]
     running = attend(rows_a, early, rows, (0, count), own)
     heads_a = attend(rows_a, late, rows, (0, count), 0, value_up, running)

time: 90.6 us -> 90 us (level)
    unnamed x21 -> x20, local copies, waits for them, and re-layouts: 4.41 us -> 4.39 us
  transfers between devices with their start and end apart: 30 -> 31, of which waited for: 11 -> 13; matrix products, arithmetic and copies ran while one was open for 0% -> 0% of each run, Pallas kernels for 22% -> 22%
where the time goes in v6:
time: 90 us; the launch traced here: 89.8 us
  starting transfers between devices  33.1 us (37%)
  waiting for transfers between devices  30.4 us (34%)
  Pallas kernels  21.3 us (24%)
  local copies, waits for them, and re-layouts  4.48 us (5%)
    ppermute x18, starting transfers between devices, layer(): held[name] = lax.ppermute(value, 'seq', right if name[0] == 'r' else left)  21.6 us
    ppermute x18, waiting for transfers between devices, layer(): held[name] = lax.ppermute(value, 'seq', right if name[0] == 'r' else left)  15.7 us
    ppermute x7, waiting for transfers between devices, layer(): lax.ppermute(slots[slot], 'seq', [(d ^ bit, d) for d in everyone])  14.7 us
    pallas_call x10, Pallas kernels, project(): pl.pallas_call(functools.partial(project_kernel, count, offsets, rows_of,...  10.7 us
    ppermute x7, starting transfers between devices, layer(): lax.ppermute(slots[slot], 'seq', [(d ^ bit, d) for d in everyone])  9.95 us
    pallas_call x4, Pallas kernels, attend(): pl.pallas_call(functools.partial(attend_kernel, rows, 4 * rows, len(keys)...  8.52 us
    unnamed x20, local copies, waits for them, and re-layouts  4.39 us
    pallas_call x2, Pallas kernels, lift(): pl.pallas_call(lift_kernel, grid=(steps,), in_specs=[pl.BlockSpec((rows,...  1.88 us
  transfers between devices with their start and end apart: 31, of which 13 were waited for; matrix products, arithmetic and copies ran while one was open for 0% of the time, Pallas kernels for 22%

profile of v6, /device:TPU:0, one launch (start us, length us, event | category | flops | bytes accessed | tf_op | source)
XLA Modules:
  0.0 89.8 jit_solution(12550267162255637965)
XLA Ops:
  0.0 0.5 collective-permute-start.22
  0.5 0.0 collective-permute-start
  0.5 0.5 collective-permute-start.1
  1.0 0.9 %copy-done.5 = bf16[128,576]{0,1:T(8,128)(2,1)S(1)} copy-done((bf16[128,576]{0,1:T(8,128)(2,1)S(1)}, bf16[128,576]{0,1:T(8,128)(2,1)}, u32[]{:S(2)}) %copy-start.5) | copy-done | bytes 147480
  1.9 0.7 copy-done.6
  2.6 0.3 prepare.1
  2.9 3.6 %collective-permute-start.3 = (bf16[64,640]{1,0:T(8,128)(2,1)S(1)}, bf16[64,640]{1,0:T(8,128)(2,1)S(1)}, u32[]{:S(2)}, u32[]{:S(2)}) collective-permute-start(bf16[64,640]{1,0:T(8,128)(2,1)S(1)} %get-tuple-element.10), channel_id=1, source_target_pairs={{8,0},{10,2},{12,4},{14,6},{0,8},{2,10},{4,12},{6,14},{9,1},{11,3}... | collective-permute-start | bytes 245768 | tf_op jit(solution)/shard_map/ppermute | solution.py:360
  6.5 1.6 %collective-permute-start.2 = (bf16[64,640]{1,0:T(8,128)(2,1)S(1)}, bf16[64,640]{1,0:T(8,128)(2,1)S(1)}, u32[]{:S(2)}, u32[]{:S(2)}) collective-permute-start(bf16[64,640]{1,0:T(8,128)(2,1)S(1)} %get-tuple-element.10), channel_id=1, source_target_pairs={{4,0},{6,2},{0,4},{2,6},{12,8},{14,10},{8,12},{10,14},{5,1},{7,3},... | collective-permute-start | bytes 245768 | tf_op jit(solution)/shard_map/ppermute | solution.py:360
  8.1 3.4 %collective-permute-done.3 = bf16[64,640]{1,0:T(8,128)(2,1)S(1)} collective-permute-done((bf16[64,640]{1,0:T(8,128)(2,1)S(1)}, bf16[64,640]{1,0:T(8,128)(2,1)S(1)}, u32[]{:S(2)}, u32[]{:S(2)}) %collective-permute-start.3) | collective-permute-done | bytes 81952 | tf_op jit(solution)/shard_map/ppermute | solution.py:360
  11.5 1.6 %collective-permute-start.5 = (bf16[64,640]{1,0:T(8,128)(2,1)S(1)}, bf16[64,640]{1,0:T(8,128)(2,1)S(1)}, u32[]{:S(2)}, u32[]{:S(2)}) collective-permute-start(bf16[64,640]{1,0:T(8,128)(2,1)S(1)} %get-tuple-element.10), channel_id=1, source_target_pairs={{2,0},{0,2},{6,4},{4,6},{10,8},{8,10},{14,12},{12,14},{3,1},{1,3},... | collective-permute-start | bytes 245768 | tf_op jit(solution)/shard_map/ppermute | solution.py:360
  13.1 0.6 collective-permute-start.4
  13.7 3.8 %collective-permute-done.4 = bf16[64,640]{1,0:T(8,128)(2,1)S(1)} collective-permute-done((bf16[64,640]{1,0:T(8,128)(2,1)S(1)}, bf16[64,640]{1,0:T(8,128)(2,1)S(1)}, u32[]{:S(2)}, u32[]{:S(2)}) %collective-permute-start.4) | collective-permute-done | bytes 81952 | tf_op jit(solution)/shard_map/ppermute | solution.py:360
  17.5 0.1 collective-permute-start.6
  17.6 0.5 collective-permute-start.7
  18.1 1.1 %copy-done.1 = bf16[64,6144]{1,0:T(8,128)(2,1)S(1)} copy-done((bf16[64,6144]{1,0:T(8,128)(2,1)S(1)}, bf16[64,6144]{1,0:T(8,128)(2,1)}, u32[]{:S(2)}) %copy-start.1) | copy-done | bytes 786456
  19.3 1.6 %copy-done.4 = bf16[16,128,512]{2,1,0:T(8,128)(2,1)S(1)} copy-done((bf16[16,128,512]{2,1,0:T(8,128)(2,1)S(1)}, bf16[16,128,512]{2,1,0:T(8,128)(2,1)}, u32[]{:S(2)}) %copy-start.4) | copy-done | bytes 2097176
  20.9 0.9 %lift.3.query_rows = bf16[1024,640]{1,0:T(8,128)(2,1)S(1)} custom-call(bf16[64,6144]{1,0:T(8,128)(2,1)S(1)} %copy-done.1, bf16[16,128,512]{2,1,0:T(8,128)(2,1)S(1)} %copy-done.4), custom_call_target="tpu_custom_call" | custom-call | flops 134217728 | bytes 3801088 | tf_op jit(solution)/shard_map/lift/pallas_call | solution.py:114
  21.8 0.7 collective-permute-done.7
  22.5 1.0 %collective-permute-start.8 = (bf16[64,640]{1,0:T(8,128)(2,1)S(1)}, bf16[64,640]{1,0:T(8,128)(2,1)S(1)}, u32[]{:S(2)}, u32[]{:S(2)}) collective-permute-start(bf16[64,640]{1,0:T(8,128)(2,1)S(1)} %collective-permute-done.3), channel_id=1, source_target_pairs={{2,0},{0,2},{6,4},{4,6},{10,8},{8,10},{14,12},{12,14},{3,1},{1,3},... | collective-permute-start | bytes 245768 | tf_op jit(solution)/shard_map/ppermute | solution.py:360
  23.5 3.4 %collective-permute-done.8 = bf16[64,640]{1,0:T(8,128)(2,1)S(1)} collective-permute-done((bf16[64,640]{1,0:T(8,128)(2,1)S(1)}, bf16[64,640]{1,0:T(8,128)(2,1)S(1)}, u32[]{:S(2)}, u32[]{:S(2)}) %collective-permute-start.8) | collective-permute-done | bytes 81952 | tf_op jit(solution)/shard_map/ppermute | solution.py:360
  26.9 1.1 %collective-permute-start.10 = (bf16[64,640]{1,0:T(8,128)(2,1)S(1)}, bf16[64,640]{1,0:T(8,128)(2,1)S(1)}, u32[]{:S(2)}, u32[]{:S(2)}) collective-permute-start(bf16[64,640]{1,0:T(8,128)(2,1)S(1)} %collective-permute-done.4), channel_id=1, source_target_pairs={{2,0},{0,2},{6,4},{4,6},{10,8},{8,10},{14,12},{12,14},{3,1},{1,3},... | collective-permute-start | bytes 245768 | tf_op jit(solution)/shard_map/ppermute | solution.py:360
  28.0 3.4 %collective-permute-done.10.refs_6_.refs_4_ = bf16[64,640]{1,0:T(8,128)(2,1)S(1)} collective-permute-done((bf16[64,640]{1,0:T(8,128)(2,1)S(1)}, bf16[64,640]{1,0:T(8,128)(2,1)S(1)}, u32[]{:S(2)}, u32[]{:S(2)}) %collective-permute-start.10) | collective-permute-done | bytes 81952 | tf_op jit(solution)/shard_map/ppermute | solution.py:360
  31.4 0.5 collective-permute-start.11
  31.9 2.4 %attend.6 = (f32[1024,512]{1,0:T(8,128)S(1)}, f32[1024,256]{1,0:T(8,128)S(1)}) custom-call(bf16[1024,640]{1,0:T(8,128)(2,1)S(1)} %lift.3.query_rows, bf16[128,640]{1,0:T(8,128)(2,1)S(1)} %get-tuple-element.9.refs_1_.refs_0_, bf16[256,640]{1,0:T(8,128)(2,1)S(1)} %constant_dynamic-update-slice_fusion.refs_2_.refs_1_, ...), custom_call_target="tpu_custom_call" | custom-call | flops 1946157056 | bytes 4653056 | tf_op jit(solution)/shard_map/attend/pallas_call | solution.py:228
  34.3 2.2 %attend.7.refs_0_ = bf16[64,2048]{1,0:T(8,128)(2,1)S(1)} custom-call(bf16[1024,640]{1,0:T(8,128)(2,1)S(1)} %lift.3.query_rows, bf16[16,512,128]{2,1,0:T(8,128)(2,1)S(1)} %copy-done.3, f32[1024,512]{1,0:T(8,128)S(1)} %get-tuple-element.11.refs_1_, f32[1024,256]{1,0:T(8,128)S(1)} %get-tuple-element.12.refs_2_, ...), custom_call_target="tpu_custom_call" | custom-call | flops 738197504 | bytes 3997696 | tf_op jit(solution)/shard_map/attend/pallas_call | solution.py:228
  36.5 0.7 collective-permute-start.23
  37.2 1.4 %collective-permute-start.27 = (bf16[64,2048]{1,0:T(8,128)(2,1)S(1)}, bf16[64,2048]{1,0:T(8,128)(2,1)S(1)}, u32[]{:S(2)}, u32[]{:S(2)}) collective-permute-start(bf16[64,2048]{1,0:T(8,128)(2,1)S(1)} %attend.7.refs_0_), channel_id=1, source_target_pairs={{4,0},{8,4},{12,8},{14,12},{10,14},{6,10},{2,6},{0,2},{5,1},{9,5},... | collective-permute-start | bytes 786440 | tf_op jit(solution)/shard_map/ppermute | solution.py:398
  38.6 0.9 %lift.2.query_rows = bf16[1024,640]{1,0:T(8,128)(2,1)S(1)} custom-call(bf16[64,6144]{1,0:T(8,128)(2,1)S(1)} %copy-done.2, bf16[16,128,512]{2,1,0:T(8,128)(2,1)S(1)} %collective-permute-done.key_up), custom_call_target="tpu_custom_call" | custom-call | flops 134217728 | bytes 3801088 | tf_op jit(solution)/shard_map/lift/pallas_call | solution.py:114
  39.6 1.9 %attend.4.refs_0_ = bf16[64,1024]{1,0:T(8,128)(2,1)S(1)} custom-call(bf16[1024,640]{1,0:T(8,128)(2,1)S(1)} %lift.2.query_rows, bf16[16,512,128]{2,1,0:T(8,128)(2,1)S(1)} %collective-permute-done.1.refs_0_, bf16[128,640]{1,0:T(8,128)(2,1)S(1)} %get-tuple-element.9.refs_1_.refs_0_, bf16[256,640]{1,0:T(8,128)(2,1)S(1)} %constant_dynamic-update-slice_fusion.refs_2_.refs_1_, ...), custom_call_target="tpu_custom_call" | custom-call | flops 1275068416 | bytes 3145728 | tf_op jit(solution)/shard_map/attend/pallas_call | solution.py:228
  41.5 1.1 %collective-permute-start.17 = (bf16[64,1024]{1,0:T(8,128)(2,1)S(1)}, bf16[64,1024]{1,0:T(8,128)(2,1)S(1)}, u32[]{:S(2)}, u32[]{:S(2)}) collective-permute-start(bf16[64,1024]{1,0:T(8,128)(2,1)S(1)} %attend.4.refs_0_), channel_id=1, source_target_pairs={{4,0},{8,4},{12,8},{14,12},{10,14},{6,10},{2,6},{0,2},{5,1},{9,5},... | collective-permute-start | bytes 393224 | tf_op jit(solution)/shard_map/ppermute | solution.py:398
  42.7 2.0 %attend.5.refs_1_ = bf16[64,1024]{1,0:T(8,128)(2,1)S(1)} custom-call(bf16[1024,640]{1,0:T(8,128)(2,1)S(1)} %lift.2.query_rows, bf16[16,512,128]{2,1,0:T(8,128)(2,1)S(1)} %collective-permute-done.1.refs_0_, bf16[128,640]{1,0:T(8,128)(2,1)S(1)} %get-tuple-element.9.refs_1_.refs_0_, bf16[256,640]{1,0:T(8,128)(2,1)S(1)} %constant_dynamic-update-slice_fusion.refs_2_.refs_1_, ...), custom_call_target="tpu_custom_call" | custom-call | flops 1275068416 | bytes 3145728 | tf_op jit(solution)/shard_map/attend/pallas_call | solution.py:228
  44.6 0.6 collective-permute-start.18
  45.3 1.5 %collective-permute-start.24 = (bf16[64,2048]{1,0:T(8,128)(2,1)S(1)}, bf16[64,2048]{1,0:T(8,128)(2,1)S(1)}, u32[]{:S(2)}, u32[]{:S(2)}) collective-permute-start(bf16[64,2048]{1,0:T(8,128)(2,1)S(1)} %collective-permute-done.23.refs_0_), channel_id=1, source_target_pairs={{0,4},{4,8},{8,12},{12,14},{14,10},{10,6},{6,2},{2,0},{1,5},{5,9},... | collective-permute-start | bytes 786440 | tf_op jit(solution)/shard_map/ppermute | solution.py:398
  46.7 1.1 %collective-permute-start.28 = (bf16[64,2048]{1,0:T(8,128)(2,1)S(1)}, bf16[64,2048]{1,0:T(8,128)(2,1)S(1)}, u32[]{:S(2)}, u32[]{:S(2)}) collective-permute-start(bf16[64,2048]{1,0:T(8,128)(2,1)S(1)} %collective-permute-done.27.refs_1_), channel_id=1, source_target_pairs={{4,0},{8,4},{12,8},{14,12},{10,14},{6,10},{2,6},{0,2},{5,1},{9,5},... | collective-permute-start | bytes 786440 | tf_op jit(solution)/shard_map/ppermute | solution.py:398
  47.8 1.4 %collective-permute-done.17 = bf16[64,1024]{1,0:T(8,128)(2,1)S(1)} collective-permute-done((bf16[64,1024]{1,0:T(8,128)(2,1)S(1)}, bf16[64,1024]{1,0:T(8,128)(2,1)S(1)}, u32[]{:S(2)}, u32[]{:S(2)}) %collective-permute-start.17) | collective-permute-done | bytes 131104 | tf_op jit(solution)/shard_map/ppermute | solution.py:398
  49.2 1.9 %collective-permute-start.12 = (bf16[64,1024]{1,0:T(8,128)(2,1)S(1)}, bf16[64,1024]{1,0:T(8,128)(2,1)S(1)}, u32[]{:S(2)}, u32[]{:S(2)}) collective-permute-start(bf16[64,1024]{1,0:T(8,128)(2,1)S(1)} %attend.4.refs_0_), channel_id=1, source_target_pairs={{0,4},{4,8},{8,12},{12,14},{14,10},{10,6},{6,2},{2,0},{1,5},{5,9},... | collective-permute-start | bytes 393224 | tf_op jit(solution)/shard_map/ppermute | solution.py:398
  51.1 0.9 %collective-permute-done.18 = bf16[64,1024]{1,0:T(8,128)(2,1)S(1)} collective-permute-done((bf16[64,1024]{1,0:T(8,128)(2,1)S(1)}, bf16[64,1024]{1,0:T(8,128)(2,1)S(1)}, u32[]{:S(2)}, u32[]{:S(2)}) %collective-permute-start.18) | collective-permute-done | bytes 131104 | tf_op jit(solution)/shard_map/ppermute | solution.py:398
  52.0 1.9 %collective-permute-start.13 = (bf16[64,1024]{1,0:T(8,128)(2,1)S(1)}, bf16[64,1024]{1,0:T(8,128)(2,1)S(1)}, u32[]{:S(2)}, u32[]{:S(2)}) collective-permute-start(bf16[64,1024]{1,0:T(8,128)(2,1)S(1)} %attend.5.refs_1_), channel_id=1, source_target_pairs={{0,4},{4,8},{8,12},{12,14},{14,10},{10,6},{6,2},{2,0},{1,5},{5,9},... | collective-permute-start | bytes 393224 | tf_op jit(solution)/shard_map/ppermute | solution.py:398
  53.9 3.2 %collective-permute-done.12 = bf16[64,1024]{1,0:T(8,128)(2,1)S(1)} collective-permute-done((bf16[64,1024]{1,0:T(8,128)(2,1)S(1)}, bf16[64,1024]{1,0:T(8,128)(2,1)S(1)}, u32[]{:S(2)}, u32[]{:S(2)}) %collective-permute-start.12) | collective-permute-done | bytes 131104 | tf_op jit(solution)/shard_map/ppermute | solution.py:398
  57.1 1.7 %collective-permute-start.19 = (bf16[64,2048]{1,0:T(8,128)(2,1)S(1)}, bf16[64,2048]{1,0:T(8,128)(2,1)S(1)}, u32[]{:S(2)}, u32[]{:S(2)}) collective-permute-start(bf16[64,2048]{1,0:T(8,128)(2,1)S(1)} %constant_dynamic-update-slice_fusion.8.refs_1_), channel_id=1, source_target_pairs={{4,0},{8,4},{12,8},{14,12},{10,14},{6,10},{2,6},{0,2},{5,1},{9,5},... | collective-permute-start | bytes 786440 | tf_op jit(solution)/shard_map/ppermute | solution.py:398
  58.9 0.6 collective-permute-start.14
  59.5 1.5 %collective-permute-start.25 = (bf16[64,2048]{1,0:T(8,128)(2,1)S(1)}, bf16[64,2048]{1,0:T(8,128)(2,1)S(1)}, u32[]{:S(2)}, u32[]{:S(2)}) collective-permute-start(bf16[64,2048]{1,0:T(8,128)(2,1)S(1)} %collective-permute-done.24.refs_0_), channel_id=1, source_target_pairs={{0,4},{4,8},{8,12},{12,14},{14,10},{10,6},{6,2},{2,0},{1,5},{5,9},... | collective-permute-start | bytes 786440 | tf_op jit(solution)/shard_map/ppermute | solution.py:398
  61.0 0.6 collective-permute-start.29
  61.5 4.4 %collective-permute-done.19.refs_1_ = bf16[64,2048]{1,0:T(8,128)(2,1)S(1)} collective-permute-done((bf16[64,2048]{1,0:T(8,128)(2,1)S(1)}, bf16[64,2048]{1,0:T(8,128)(2,1)S(1)}, u32[]{:S(2)}, u32[]{:S(2)}) %collective-permute-start.19) | collective-permute-done | bytes 262176 | tf_op jit(solution)/shard_map/ppermute | solution.py:398
  65.9 2.1 %collective-permute-start.20 = (bf16[64,2048]{1,0:T(8,128)(2,1)S(1)}, bf16[64,2048]{1,0:T(8,128)(2,1)S(1)}, u32[]{:S(2)}, u32[]{:S(2)}) collective-permute-start(bf16[64,2048]{1,0:T(8,128)(2,1)S(1)} %collective-permute-done.19.refs_1_), channel_id=1, source_target_pairs={{4,0},{8,4},{12,8},{14,12},{10,14},{6,10},{2,6},{0,2},{5,1},{9,5},... | collective-permute-start | bytes 786440 | tf_op jit(solution)/shard_map/ppermute | solution.py:398
  68.0 0.1 collective-permute-done.14.refs_0_
  68.1 0.6 collective-permute-start.15
  68.7 0.7 project.14.refs_3_
  69.4 4.3 %collective-permute-done.25.refs_0_ = bf16[64,2048]{1,0:T(8,128)(2,1)S(1)} collective-permute-done((bf16[64,2048]{1,0:T(8,128)(2,1)S(1)}, bf16[64,2048]{1,0:T(8,128)(2,1)S(1)}, u32[]{:S(2)}, u32[]{:S(2)}) %collective-permute-start.25) | collective-permute-done | bytes 262176 | tf_op jit(solution)/shard_map/ppermute | solution.py:398
  73.7 0.6 collective-permute-start.26
  74.4 1.7 %collective-permute-start.30 = (bf16[64,1024]{1,0:T(8,128)(2,1)S(1)}, bf16[64,1024]{1,0:T(8,128)(2,1)S(1)}, u32[]{:S(2)}, u32[]{:S(2)}) collective-permute-start(bf16[64,1024]{1,0:T(8,128)(2,1)S(1)} %slice.19), channel_id=1, source_target_pairs={{4,0},{8,4},{12,8},{14,12},{10,14},{6,10},{2,6},{0,2},{5,1},{9,5},... | collective-permute-start | bytes 393224 | tf_op jit(solution)/shard_map/ppermute | solution.py:398
  76.1 0.7 project.13.refs_3_
  76.8 0.7 project.12.refs_3_
  77.5 0.7 project.11.refs_3_
  78.2 1.1 %collective-permute-done.26.refs_0_ = bf16[64,1024]{1,0:T(8,128)(2,1)S(1)} collective-permute-done((bf16[64,1024]{1,0:T(8,128)(2,1)S(1)}, bf16[64,1024]{1,0:T(8,128)(2,1)S(1)}, u32[]{:S(2)}, u32[]{:S(2)}) %collective-permute-start.26) | collective-permute-done | bytes 131104 | tf_op jit(solution)/shard_map/ppermute | solution.py:398
  79.3 0.2 collective-permute-done.30.refs_1_
  79.6 0.7 project.10.refs_3_
  80.3 1.5 %collective-permute-start.21 = (bf16[64,1024]{1,0:T(8,128)(2,1)S(1)}, bf16[64,1024]{1,0:T(8,128)(2,1)S(1)}, u32[]{:S(2)}, u32[]{:S(2)}) collective-permute-start(bf16[64,1024]{1,0:T(8,128)(2,1)S(1)} %slice.17), channel_id=1, source_target_pairs={{4,0},{8,4},{12,8},{14,12},{10,14},{6,10},{2,6},{0,2},{5,1},{9,5},... | collective-permute-start | bytes 393224 | tf_op jit(solution)/shard_map/ppermute | solution.py:398
  81.9 0.6 collective-permute-start.16
  82.5 1.4 %project.15.refs_4_ = bf16[8,1,64,896]{3,2,1,0:T(8,128)(2,1)} custom-call(bf16[64,1024]{1,0:T(8,128)(2,1)S(1)} %attend.4.refs_0_, bf16[64,1024]{1,0:T(8,128)(2,1)S(1)} %attend.5.refs_1_, bf16[2048,896]{1,0:T(8,128)(2,1)S(1)} %collective-permute-done.22.refs_2_, f32[64,896]{1,0:T(8,128)S(1)} %project.14.refs_3_), custom_call_target="tpu_custom_call" | custom-call | flops 234881024 | bytes 3670016 | tf_op jit(solution)/shard_map/project/pallas_call | solution.py:312
  83.9 1.4 %project.16.refs_4_ = bf16[8,1,64,896]{3,2,1,0:T(8,128)(2,1)} custom-call(bf16[64,2048]{1,0:T(8,128)(2,1)S(1)} %constant_dynamic-update-slice_fusion.6.refs_0_, bf16[64,2048]{1,0:T(8,128)(2,1)S(1)} %constant_dynamic-update-slice_fusion.8.refs_1_, bf16[2048,896]{1,0:T(8,128)(2,1)S(1)} %collective-permute-done.22.refs_2_, ...), custom_call_target="tpu_custom_call", output_to_operand_aliasing={{}: (4, {})} | custom-call | flops 469762048 | bytes 3670016 | tf_op jit(solution)/shard_map/project/pallas_call | solution.py:312
  85.3 1.4 %project.17.refs_4_ = bf16[8,1,64,896]{3,2,1,0:T(8,128)(2,1)} custom-call(bf16[64,2048]{1,0:T(8,128)(2,1)S(1)} %collective-permute-done.14.refs_0_, bf16[64,2048]{1,0:T(8,128)(2,1)S(1)} %collective-permute-done.19.refs_1_, bf16[2048,896]{1,0:T(8,128)(2,1)S(1)} %collective-permute-done.22.refs_2_, ...), custom_call_target="tpu_custom_call", output_to_operand_aliasing={{}: (4, {})} | custom-call | flops 469762048 | bytes 3670016 | tf_op jit(solution)/shard_map/project/pallas_call | solution.py:312
  86.8 1.4 %project.18.refs_4_ = bf16[8,1,64,896]{3,2,1,0:T(8,128)(2,1)} custom-call(bf16[64,2048]{1,0:T(8,128)(2,1)S(1)} %collective-permute-done.15.refs_0_, bf16[64,2048]{1,0:T(8,128)(2,1)S(1)} %collective-permute-done.20.refs_1_, bf16[2048,896]{1,0:T(8,128)(2,1)S(1)} %collective-permute-done.22.refs_2_, ...), custom_call_target="tpu_custom_call", output_to_operand_aliasing={{}: (4, {})} | custom-call | flops 469762048 | bytes 3670016 | tf_op jit(solution)/shard_map/project/pallas_call | solution.py:312
  88.2 1.4 %project.19 = bf16[8,1,64,896]{3,2,1,0:T(8,128)(2,1)} custom-call(bf16[64,1024]{1,0:T(8,128)(2,1)S(1)} %collective-permute-done.16.refs_0_, bf16[64,1024]{1,0:T(8,128)(2,1)S(1)} %collective-permute-done.21.refs_1_, bf16[2048,896]{1,0:T(8,128)(2,1)S(1)} %collective-permute-done.22.refs_2_, ...), custom_call_target="tpu_custom_call", output_to_operand_aliasing={{}: (4, {})} | custom-call | flops 234881024 | bytes 3670016 | tf_op jit(solution)/shard_map/project/pallas_call | solution.py:312
  (43 shorter events, 0.2 us)
Async XLA Ops:
  0.0 82.5 %collective-permute-start.22 = (bf16[2048,896]{1,0:T(8,128)(2,1)}, bf16[2048,896]{1,0:T(8,128)(2,1)S(1)}, u32[]{:S(2)}, u32[]{:S(2)}) collective-permute-start(bf16[2048,896]{1,0:T(8,128)(2,1)} %refs_1_.1), channel_id=1, source_target_pairs={{0,1},{1,0},{2,3},{3,2},{4,5},{5,4},{6,7},{7,6},{8,9},{9,8},{10,11... | collective-permute-start | bytes 11010056 | tf_op jit(solution)/shard_map/ppermute | solution.py:372
  0.5 38.1 %collective-permute-start = (bf16[16,128,512]{2,1,0:T(8,128)(2,1)}, bf16[16,128,512]{2,1,0:T(8,128)(2,1)S(1)}, u32[]{:S(2)}, u32[]{:S(2)}) collective-permute-start(bf16[16,128,512]{2,1,0:T(8,128)(2,1)} %key_up.1), channel_id=1, source_target_pairs={{0,1},{1,0},{2,3},{3,2},{4,5},{5,4},{6,7},{7,6},{8,9},{9,8},{10,11... | collective-permute-start | bytes 6291464 | tf_op jit(solution)/shard_map/ppermute | solution.py:370
  0.5 39.1 %collective-permute-start.1 = (bf16[16,512,128]{2,1,0:T(8,128)(2,1)}, bf16[16,512,128]{2,1,0:T(8,128)(2,1)S(1)}, u32[]{:S(2)}, u32[]{:S(2)}) collective-permute-start(bf16[16,512,128]{2,1,0:T(8,128)(2,1)} %refs_0_.1), channel_id=1, source_target_pairs={{0,1},{1,0},{2,3},{3,2},{4,5},{5,4},{6,7},{7,6},{8,9},{9,8},{10,11... | collective-permute-start | bytes 6291464 | tf_op jit(solution)/shard_map/ppermute | solution.py:371
  1.0 0.9 %copy-start.5 = (bf16[128,576]{0,1:T(8,128)(2,1)S(1)}, bf16[128,576]{0,1:T(8,128)(2,1)}, u32[]{:S(2)}) copy-start(bf16[128,576]{0,1:T(8,128)(2,1)} %param.7) | copy-start | bytes 442372
  1.9 0.7 copy-start.6
  2.9 8.6 %collective-permute-start.3 = (bf16[64,640]{1,0:T(8,128)(2,1)S(1)}, bf16[64,640]{1,0:T(8,128)(2,1)S(1)}, u32[]{:S(2)}, u32[]{:S(2)}) collective-permute-start(bf16[64,640]{1,0:T(8,128)(2,1)S(1)} %get-tuple-element.10), channel_id=1, source_target_pairs={{8,0},{10,2},{12,4},{14,6},{0,8},{2,10},{4,12},{6,14},{9,1},{11,3}... | collective-permute-start | bytes 245768 | tf_op jit(solution)/shard_map/ppermute | solution.py:360
  6.5 6.5 %collective-permute-start.2 = (bf16[64,640]{1,0:T(8,128)(2,1)S(1)}, bf16[64,640]{1,0:T(8,128)(2,1)S(1)}, u32[]{:S(2)}, u32[]{:S(2)}) collective-permute-start(bf16[64,640]{1,0:T(8,128)(2,1)S(1)} %get-tuple-element.10), channel_id=1, source_target_pairs={{4,0},{6,2},{0,4},{2,6},{12,8},{14,10},{8,12},{10,14},{5,1},{7,3},... | collective-permute-start | bytes 245768 | tf_op jit(solution)/shard_map/ppermute | solution.py:360
  11.5 6.0 %collective-permute-start.5 = (bf16[64,640]{1,0:T(8,128)(2,1)S(1)}, bf16[64,640]{1,0:T(8,128)(2,1)S(1)}, u32[]{:S(2)}, u32[]{:S(2)}) collective-permute-start(bf16[64,640]{1,0:T(8,128)(2,1)S(1)} %get-tuple-element.10), channel_id=1, source_target_pairs={{2,0},{0,2},{6,4},{4,6},{10,8},{8,10},{14,12},{12,14},{3,1},{1,3},... | collective-permute-start | bytes 245768 | tf_op jit(solution)/shard_map/ppermute | solution.py:360
  13.1 4.4 %collective-permute-start.4 = (bf16[64,640]{1,0:T(8,128)(2,1)S(1)}, bf16[64,640]{1,0:T(8,128)(2,1)S(1)}, u32[]{:S(2)}, u32[]{:S(2)}) collective-permute-start(bf16[64,640]{1,0:T(8,128)(2,1)S(1)} %collective-permute-done.3), channel_id=1, source_target_pairs={{4,0},{6,2},{0,4},{2,6},{12,8},{14,10},{8,12},{10,14},{5,1},{7,3},... | collective-permute-start | bytes 245768 | tf_op jit(solution)/shard_map/ppermute | solution.py:360
  17.5 13.8 %collective-permute-start.6 = (bf16[256,640]{1,0:T(8,128)(2,1)S(1)}, bf16[256,640]{1,0:T(8,128)(2,1)S(1)}, u32[]{:S(2)}, u32[]{:S(2)}) collective-permute-start(bf16[256,640]{1,0:T(8,128)(2,1)S(1)} %constant_dynamic-update-slice_fusion.refs_2_.refs_1_), channel_id=1, source_target_pairs={{0,1},{1,0},{2,3},{3,2},{4,5},{5,4},{6,7},{7,6},{8,9},{9,8},{10,11... | collective-permute-start | bytes 983048 | tf_op jit(solution)/shard_map/ppermute | solution.py:366
  17.6 4.8 %collective-permute-start.7 = (bf16[64,640]{1,0:T(8,128)(2,1)S(1)}, bf16[64,640]{1,0:T(8,128)(2,1)S(1)}, u32[]{:S(2)}, u32[]{:S(2)}) collective-permute-start(bf16[64,640]{1,0:T(8,128)(2,1)S(1)} %collective-permute-done.2), channel_id=1, source_target_pairs={{2,0},{0,2},{6,4},{4,6},{10,8},{8,10},{14,12},{12,14},{3,1},{1,3},... | collective-permute-start | bytes 245768 | tf_op jit(solution)/shard_map/ppermute | solution.py:360
  18.1 1.1 %copy-start.1 = (bf16[64,6144]{1,0:T(8,128)(2,1)S(1)}, bf16[64,6144]{1,0:T(8,128)(2,1)}, u32[]{:S(2)}) copy-start(bf16[64,6144]{1,0:T(8,128)(2,1)} %queries.3) | copy-start | bytes 2359300
  19.3 1.6 %copy-start.4 = (bf16[16,128,512]{2,1,0:T(8,128)(2,1)S(1)}, bf16[16,128,512]{2,1,0:T(8,128)(2,1)}, u32[]{:S(2)}) copy-start(bf16[16,128,512]{2,1,0:T(8,128)(2,1)} %key_up.1) | copy-start | bytes 6291460
  22.5 4.4 %collective-permute-start.8 = (bf16[64,640]{1,0:T(8,128)(2,1)S(1)}, bf16[64,640]{1,0:T(8,128)(2,1)S(1)}, u32[]{:S(2)}, u32[]{:S(2)}) collective-permute-start(bf16[64,640]{1,0:T(8,128)(2,1)S(1)} %collective-permute-done.3), channel_id=1, source_target_pairs={{2,0},{0,2},{6,4},{4,6},{10,8},{8,10},{14,12},{12,14},{3,1},{1,3},... | collective-permute-start | bytes 245768 | tf_op jit(solution)/shard_map/ppermute | solution.py:360
  26.9 4.4 %collective-permute-start.10 = (bf16[64,640]{1,0:T(8,128)(2,1)S(1)}, bf16[64,640]{1,0:T(8,128)(2,1)S(1)}, u32[]{:S(2)}, u32[]{:S(2)}) collective-permute-start(bf16[64,640]{1,0:T(8,128)(2,1)S(1)} %collective-permute-done.4), channel_id=1, source_target_pairs={{2,0},{0,2},{6,4},{4,6},{10,8},{8,10},{14,12},{12,14},{3,1},{1,3},... | collective-permute-start | bytes 245768 | tf_op jit(solution)/shard_map/ppermute | solution.py:360
  31.4 2.9 %collective-permute-start.9 = (bf16[128,640]{1,0:T(8,128)(2,1)S(1)}, bf16[128,640]{1,0:T(8,128)(2,1)S(1)}, u32[]{:S(2)}, u32[]{:S(2)}) collective-permute-start(bf16[128,640]{1,0:T(8,128)(2,1)S(1)} %constant_dynamic-update-slice_fusion.4.refs_4_.refs_3_), channel_id=1, source_target_pairs={{0,1},{1,0},{2,3},{3,2},{4,5},{5,4},{6,7},{7,6},{8,9},{9,8},{10,11... | collective-permute-start | bytes 491528 | tf_op jit(solution)/shard_map/ppermute | solution.py:367
  31.4 2.9 %collective-permute-start.11 = (bf16[64,640]{1,0:T(8,128)(2,1)S(1)}, bf16[64,640]{1,0:T(8,128)(2,1)S(1)}, u32[]{:S(2)}, u32[]{:S(2)}) collective-permute-start(bf16[64,640]{1,0:T(8,128)(2,1)S(1)} %collective-permute-done.10.refs_6_.refs_4_), channel_id=1, source_target_pairs={{0,1},{1,0},{2,3},{3,2},{4,5},{5,4},{6,7},{7,6},{8,9},{9,8},{10,11... | collective-permute-start | bytes 245768 | tf_op jit(solution)/shard_map/ppermute | solution.py:368
  31.9 2.4 %copy-start.3 = (bf16[16,512,128]{2,1,0:T(8,128)(2,1)S(1)}, bf16[16,512,128]{2,1,0:T(8,128)(2,1)}, u32[]{:S(2)}) copy-start(bf16[16,512,128]{2,1,0:T(8,128)(2,1)} %refs_0_.1) | copy-start | bytes 6291460
  34.3 4.3 %copy-start.2 = (bf16[64,6144]{1,0:T(8,128)(2,1)S(1)}, bf16[64,6144]{1,0:T(8,128)(2,1)}, u32[]{:S(2)}) copy-start(bf16[64,6144]{1,0:T(8,128)(2,1)} %queries.3) | copy-start | bytes 2359300
  36.5 8.7 %collective-permute-start.23 = (bf16[64,2048]{1,0:T(8,128)(2,1)S(1)}, bf16[64,2048]{1,0:T(8,128)(2,1)S(1)}, u32[]{:S(2)}, u32[]{:S(2)}) collective-permute-start(bf16[64,2048]{1,0:T(8,128)(2,1)S(1)} %attend.7.refs_0_), channel_id=1, source_target_pairs={{0,4},{4,8},{8,12},{12,14},{14,10},{10,6},{6,2},{2,0},{1,5},{5,9},... | collective-permute-start | bytes 786440 | tf_op jit(solution)/shard_map/ppermute | solution.py:398
  37.2 9.5 %collective-permute-start.27 = (bf16[64,2048]{1,0:T(8,128)(2,1)S(1)}, bf16[64,2048]{1,0:T(8,128)(2,1)S(1)}, u32[]{:S(2)}, u32[]{:S(2)}) collective-permute-start(bf16[64,2048]{1,0:T(8,128)(2,1)S(1)} %attend.7.refs_0_), channel_id=1, source_target_pairs={{4,0},{8,4},{12,8},{14,12},{10,14},{6,10},{2,6},{0,2},{5,1},{9,5},... | collective-permute-start | bytes 786440 | tf_op jit(solution)/shard_map/ppermute | solution.py:398
  41.5 27.1 %copy-start = (bf16[2048,896]{1,0:T(8,128)(2,1)S(1)}, bf16[2048,896]{1,0:T(8,128)(2,1)}, u32[]{:S(2)}) copy-start(bf16[2048,896]{1,0:T(8,128)(2,1)} %refs_1_.1) | copy-start | bytes 11010052
  41.5 7.7 %collective-permute-start.17 = (bf16[64,1024]{1,0:T(8,128)(2,1)S(1)}, bf16[64,1024]{1,0:T(8,128)(2,1)S(1)}, u32[]{:S(2)}, u32[]{:S(2)}) collective-permute-start(bf16[64,1024]{1,0:T(8,128)(2,1)S(1)} %attend.4.refs_0_), channel_id=1, source_target_pairs={{4,0},{8,4},{12,8},{14,12},{10,14},{6,10},{2,6},{0,2},{5,1},{9,5},... | collective-permute-start | bytes 393224 | tf_op jit(solution)/shard_map/ppermute | solution.py:398
  44.6 7.4 %collective-permute-start.18 = (bf16[64,1024]{1,0:T(8,128)(2,1)S(1)}, bf16[64,1024]{1,0:T(8,128)(2,1)S(1)}, u32[]{:S(2)}, u32[]{:S(2)}) collective-permute-start(bf16[64,1024]{1,0:T(8,128)(2,1)S(1)} %attend.5.refs_1_), channel_id=1, source_target_pairs={{4,0},{8,4},{12,8},{14,12},{10,14},{6,10},{2,6},{0,2},{5,1},{9,5},... | collective-permute-start | bytes 393224 | tf_op jit(solution)/shard_map/ppermute | solution.py:398
  45.3 14.2 %collective-permute-start.24 = (bf16[64,2048]{1,0:T(8,128)(2,1)S(1)}, bf16[64,2048]{1,0:T(8,128)(2,1)S(1)}, u32[]{:S(2)}, u32[]{:S(2)}) collective-permute-start(bf16[64,2048]{1,0:T(8,128)(2,1)S(1)} %collective-permute-done.23.refs_0_), channel_id=1, source_target_pairs={{0,4},{4,8},{8,12},{12,14},{14,10},{10,6},{6,2},{2,0},{1,5},{5,9},... | collective-permute-start | bytes 786440 | tf_op jit(solution)/shard_map/ppermute | solution.py:398
  46.7 14.2 %collective-permute-start.28 = (bf16[64,2048]{1,0:T(8,128)(2,1)S(1)}, bf16[64,2048]{1,0:T(8,128)(2,1)S(1)}, u32[]{:S(2)}, u32[]{:S(2)}) collective-permute-start(bf16[64,2048]{1,0:T(8,128)(2,1)S(1)} %collective-permute-done.27.refs_1_), channel_id=1, source_target_pairs={{4,0},{8,4},{12,8},{14,12},{10,14},{6,10},{2,6},{0,2},{5,1},{9,5},... | collective-permute-start | bytes 786440 | tf_op jit(solution)/shard_map/ppermute | solution.py:398
  49.2 7.9 %collective-permute-start.12 = (bf16[64,1024]{1,0:T(8,128)(2,1)S(1)}, bf16[64,1024]{1,0:T(8,128)(2,1)S(1)}, u32[]{:S(2)}, u32[]{:S(2)}) collective-permute-start(bf16[64,1024]{1,0:T(8,128)(2,1)S(1)} %attend.4.refs_0_), channel_id=1, source_target_pairs={{0,4},{4,8},{8,12},{12,14},{14,10},{10,6},{6,2},{2,0},{1,5},{5,9},... | collective-permute-start | bytes 393224 | tf_op jit(solution)/shard_map/ppermute | solution.py:398
  52.0 6.8 %collective-permute-start.13 = (bf16[64,1024]{1,0:T(8,128)(2,1)S(1)}, bf16[64,1024]{1,0:T(8,128)(2,1)S(1)}, u32[]{:S(2)}, u32[]{:S(2)}) collective-permute-start(bf16[64,1024]{1,0:T(8,128)(2,1)S(1)} %attend.5.refs_1_), channel_id=1, source_target_pairs={{0,4},{4,8},{8,12},{12,14},{14,10},{10,6},{6,2},{2,0},{1,5},{5,9},... | collective-permute-start | bytes 393224 | tf_op jit(solution)/shard_map/ppermute | solution.py:398
  57.1 8.9 %collective-permute-start.19 = (bf16[64,2048]{1,0:T(8,128)(2,1)S(1)}, bf16[64,2048]{1,0:T(8,128)(2,1)S(1)}, u32[]{:S(2)}, u32[]{:S(2)}) collective-permute-start(bf16[64,2048]{1,0:T(8,128)(2,1)S(1)} %constant_dynamic-update-slice_fusion.8.refs_1_), channel_id=1, source_target_pairs={{4,0},{8,4},{12,8},{14,12},{10,14},{6,10},{2,6},{0,2},{5,1},{9,5},... | collective-permute-start | bytes 786440 | tf_op jit(solution)/shard_map/ppermute | solution.py:398
  58.9 9.2 %collective-permute-start.14 = (bf16[64,2048]{1,0:T(8,128)(2,1)S(1)}, bf16[64,2048]{1,0:T(8,128)(2,1)S(1)}, u32[]{:S(2)}, u32[]{:S(2)}) collective-permute-start(bf16[64,2048]{1,0:T(8,128)(2,1)S(1)} %constant_dynamic-update-slice_fusion.6.refs_0_), channel_id=1, source_target_pairs={{0,4},{4,8},{8,12},{12,14},{14,10},{10,6},{6,2},{2,0},{1,5},{5,9},... | collective-permute-start | bytes 786440 | tf_op jit(solution)/shard_map/ppermute | solution.py:398
  59.5 14.2 %collective-permute-start.25 = (bf16[64,2048]{1,0:T(8,128)(2,1)S(1)}, bf16[64,2048]{1,0:T(8,128)(2,1)S(1)}, u32[]{:S(2)}, u32[]{:S(2)}) collective-permute-start(bf16[64,2048]{1,0:T(8,128)(2,1)S(1)} %collective-permute-done.24.refs_0_), channel_id=1, source_target_pairs={{0,4},{4,8},{8,12},{12,14},{14,10},{10,6},{6,2},{2,0},{1,5},{5,9},... | collective-permute-start | bytes 786440 | tf_op jit(solution)/shard_map/ppermute | solution.py:398
  61.0 13.4 %collective-permute-start.29 = (bf16[64,2048]{1,0:T(8,128)(2,1)S(1)}, bf16[64,2048]{1,0:T(8,128)(2,1)S(1)}, u32[]{:S(2)}, u32[]{:S(2)}) collective-permute-start(bf16[64,2048]{1,0:T(8,128)(2,1)S(1)} %collective-permute-done.28.refs_1_), channel_id=1, source_target_pairs={{4,0},{8,4},{12,8},{14,12},{10,14},{6,10},{2,6},{0,2},{5,1},{9,5},... | collective-permute-start | bytes 786440 | tf_op jit(solution)/shard_map/ppermute | solution.py:398
  65.9 14.4 %collective-permute-start.20 = (bf16[64,2048]{1,0:T(8,128)(2,1)S(1)}, bf16[64,2048]{1,0:T(8,128)(2,1)S(1)}, u32[]{:S(2)}, u32[]{:S(2)}) collective-permute-start(bf16[64,2048]{1,0:T(8,128)(2,1)S(1)} %collective-permute-done.19.refs_1_), channel_id=1, source_target_pairs={{4,0},{8,4},{12,8},{14,12},{10,14},{6,10},{2,6},{0,2},{5,1},{9,5},... | collective-permute-start | bytes 786440 | tf_op jit(solution)/shard_map/ppermute | solution.py:398
  68.1 13.7 %collective-permute-start.15 = (bf16[64,2048]{1,0:T(8,128)(2,1)S(1)}, bf16[64,2048]{1,0:T(8,128)(2,1)S(1)}, u32[]{:S(2)}, u32[]{:S(2)}) collective-permute-start(bf16[64,2048]{1,0:T(8,128)(2,1)S(1)} %collective-permute-done.14.refs_0_), channel_id=1, source_target_pairs={{0,4},{4,8},{8,12},{12,14},{14,10},{10,6},{6,2},{2,0},{1,5},{5,9},... | collective-permute-start | bytes 786440 | tf_op jit(solution)/shard_map/ppermute | solution.py:398
  73.7 5.6 %collective-permute-start.26 = (bf16[64,1024]{1,0:T(8,128)(2,1)S(1)}, bf16[64,1024]{1,0:T(8,128)(2,1)S(1)}, u32[]{:S(2)}, u32[]{:S(2)}) collective-permute-start(bf16[64,1024]{1,0:T(8,128)(2,1)S(1)} %slice.18), channel_id=1, source_target_pairs={{0,4},{4,8},{8,12},{12,14},{14,10},{10,6},{6,2},{2,0},{1,5},{5,9},... | collective-permute-start | bytes 393224 | tf_op jit(solution)/shard_map/ppermute | solution.py:398
  74.4 5.2 %collective-permute-start.30 = (bf16[64,1024]{1,0:T(8,128)(2,1)S(1)}, bf16[64,1024]{1,0:T(8,128)(2,1)S(1)}, u32[]{:S(2)}, u32[]{:S(2)}) collective-permute-start(bf16[64,1024]{1,0:T(8,128)(2,1)S(1)} %slice.19), channel_id=1, source_target_pairs={{4,0},{8,4},{12,8},{14,12},{10,14},{6,10},{2,6},{0,2},{5,1},{9,5},... | collective-permute-start | bytes 393224 | tf_op jit(solution)/shard_map/ppermute | solution.py:398
  80.3 7.9 %collective-permute-start.21 = (bf16[64,1024]{1,0:T(8,128)(2,1)S(1)}, bf16[64,1024]{1,0:T(8,128)(2,1)S(1)}, u32[]{:S(2)}, u32[]{:S(2)}) collective-permute-start(bf16[64,1024]{1,0:T(8,128)(2,1)S(1)} %slice.17), channel_id=1, source_target_pairs={{4,0},{8,4},{12,8},{14,12},{10,14},{6,10},{2,6},{0,2},{5,1},{9,5},... | collective-permute-start | bytes 393224 | tf_op jit(solution)/shard_map/ppermute | solution.py:398
  81.9 6.4 %collective-permute-start.16 = (bf16[64,1024]{1,0:T(8,128)(2,1)S(1)}, bf16[64,1024]{1,0:T(8,128)(2,1)S(1)}, u32[]{:S(2)}, u32[]{:S(2)}) collective-permute-start(bf16[64,1024]{1,0:T(8,128)(2,1)S(1)} %slice.16), channel_id=1, source_target_pairs={{0,4},{4,8},{8,12},{12,14},{14,10},{10,6},{6,2},{2,0},{1,5},{5,9},... | collective-permute-start | bytes 393224 | tf_op jit(solution)/shard_map/ppermute | solution.py:398
